TPU v7x, 32 devices: a whole 2x2x4 slice. The times are simulated.
32 devices in a mesh: dp: 8 (over z, core), tensor: 4 (over y, x).
Axes of the slice: x: 2, y: 2, z: 4, core: 2. Of those that a mesh axis runs over, the one named last changes fastest.
Arguments:
- block_input_rows: bfloat16 [2, 8, 2048, 1024], P(None, 'dp', 'tensor'), may hold values from -6 to 6
- output_gradient: bfloat16 [2, 8, 2048, 1024], P(None, 'dp', 'tensor'), may hold values from -6 to 6
- segment_numbers: int32 [2, 8, 2048], P(None, 'dp'), may hold values from 0 to 4, never falling along the last dimension, each value on 1 to 1024 neighbouring positions
- token_keep_mask: int32 [2, 8, 2048], P(None, 'dp'), may hold values 0 or 1
- layer_norm_gain: float32 [2, 1024], replicated, may hold values from 0.1 to 1.9
- layer_norm_bias: float32 [2, 1024], replicated, may hold values from -3 to 3
- projection_weight: bfloat16 [3, 1024, 1024], P(None, None, 'tensor'), may hold values from -0.1875 to 0.1875
- output_weight: bfloat16 [1024, 1024], P('tensor'), may hold values from -0.75 to 0.75
- up_weight: bfloat16 [1024, 4096], P(None, 'tensor'), may hold values from -0.1875 to 0.1875
- down_weight: bfloat16 [4096, 1024], P('tensor'), may hold values from -0.09375 to 0.09375
- adapter_first_input: bfloat16 [4, 1024, 128], P(None, None, 'tensor'), may hold values from -0.1875 to 0.1875
- adapter_second_projections: bfloat16 [3, 128, 1024], P(None, None, 'tensor'), may hold values from -0.5 to 0.5
- adapter_second_upward: bfloat16 [128, 4096], P(None, 'tensor'), may hold values from -0.5 to 0.5
- adapter_first_output: bfloat16 [1024, 128], P('tensor'), may hold values from -0.75 to 0.75
- adapter_first_down: bfloat16 [4096, 128], P('tensor'), may hold values from -0.09375 to 0.09375
- adapter_second_output: bfloat16 [2, 128, 1024], P(None, 'tensor'), may hold values from -0.5 to 0.5
Outputs:
- block_output: bfloat16 [2, 8, 2048, 1024], P(None, 'dp', 'tensor')
- grad_in: bfloat16 [2, 8, 2048, 1024], P(None, 'dp', 'tensor')
- grad_norm_gain: float32 [2, 1024], replicated
- grad_norm_bias: float32 [2, 1024], replicated
- grad_lora_a_in: float32 [4, 1024, 128], P(None, None, 'tensor')
- grad_lora_b_qkv: float32 [3, 128, 1024], P(None, None, 'tensor')
- grad_lora_b_up: float32 [128, 4096], P(None, 'tensor')
- grad_lora_a_o: float32 [1024, 128], P('tensor')
- grad_lora_a_down: float32 [4096, 128], P('tensor')
- grad_lora_b_out: float32 [2, 128, 1024], P(None, 'tensor')
Inputs may be any that keep to these rules, and one draw needn't show every extreme that they name: `segment_numbers`: in each group the 2048 tokens hold 5 whole documents one after another, numbered from 0 upward; each has 1 to 1024 tokens and one has exactly 1024.
All inputs are finite; a program needn't handle non-finite values. No bound on the sum of `token_keep_mask` on one device may be relied on, other than what follows from the above.
Results may differ from a plain program's by a relative error of at most 0.012.
The roundings to bfloat16 on the way count: a program that leaves them out, or rounds other values in their place, can miss the bound.
Values may be sent and summed in bfloat16 or wider, within the bound.
A program may use at most 192 MiB of HBM per device.

v0:
```python
import math

import jax
import jax.numpy as jnp
from jax import lax
from jax.sharding import PartitionSpec as P

HEAD_SIZE = 64
ROT = 16
BLOCK = 512


EPSILON = 1e-05
ADAPTER_SCALE = 0.25
NEG_LARGE = -1e30


def normalized(values):
    average = jnp.mean(values, axis=-1, keepdims=True)
    centered = values - average
    variance = jnp.mean(centered * centered, axis=-1, keepdims=True)
    return centered * lax.rsqrt(variance + EPSILON)


def norm_pair(inputs, layer_norm_gain, layer_norm_bias):
    standard = normalized(inputs)
    return (
        standard * layer_norm_gain[0] + layer_norm_bias[0],
        standard * layer_norm_gain[1] + layer_norm_bias[1],
    )


def exact_gelu(value):
    return jax.nn.gelu(value, approximate=False)


def positions(segment):
    sequence_length = segment.shape[0]
    indices = jnp.arange(sequence_length, dtype=jnp.int32)
    previous = jnp.concatenate([segment[:1] - 1, segment[:-1]])
    starting = jnp.where(segment != previous, indices, jnp.zeros_like(indices))
    return indices - lax.cummax(starting, axis=0)


def rotary_tables(segment):
    half_rot = ROT // 2
    exponent = 2.0 * jnp.arange(half_rot, dtype=jnp.float32) / ROT
    frequency = jnp.exp(-math.log(10000.0) * exponent)
    angles = positions(segment).astype(jnp.float32)[:, None] * frequency[None, :]
    return (jnp.cos(angles), jnp.sin(angles))


def rotate(values, cos_table, sin_table):
    half_rot = cos_table.shape[1]
    first_half = values[..., :half_rot]
    second_half = values[..., half_rot : 2 * half_rot]
    cosine = cos_table[:, None, :]
    sine_wide = sin_table[:, None, :]
    return jnp.concatenate(
        [
            first_half * cosine - second_half * sine_wide,
            second_half * cosine + first_half * sine_wide,
            values[..., 2 * half_rot :],
        ],
        axis=-1,
    )


def allowed_pairs(segment, seg_pad, keep_pad, start):
    query_pos = start + jnp.arange(BLOCK, dtype=jnp.int32)
    key_pos = start - 2 * BLOCK + jnp.arange(3 * BLOCK, dtype=jnp.int32)
    query_seg = lax.dynamic_slice_in_dim(segment, start, BLOCK)
    key_seg = lax.dynamic_slice_in_dim(seg_pad, start, 3 * BLOCK)
    key_keep = lax.dynamic_slice_in_dim(keep_pad, start, 3 * BLOCK)
    same_doc = query_seg[:, None] == key_seg[None, :]
    causal = key_pos[None, :] <= query_pos[:, None]
    usable = (key_keep[None, :] == 1) | (key_pos[None, :] == query_pos[:, None])
    return same_doc & causal & usable


def padded_keys(keys_all, values_all, segment, token_keep_mask):
    pad_rows = 2 * BLOCK
    blank = jnp.zeros((pad_rows,) + keys_all.shape[1:], keys_all.dtype)
    key_pad = jnp.concatenate([blank, keys_all], axis=0)
    value_pad = jnp.concatenate([blank, values_all], axis=0)
    seg_pad = jnp.concatenate([jnp.full((pad_rows,), -1, jnp.int32), segment])
    keep_pad = jnp.concatenate([jnp.zeros((pad_rows,), jnp.int32), token_keep_mask])
    return (key_pad, value_pad, seg_pad, keep_pad)


def attend_forward(queries, keys_all, values_all, segment, token_keep_mask):
    sequence_length, head_count, head_width = queries.shape
    scale = 1.0 / math.sqrt(head_width)
    key_pad, value_pad, seg_pad, keep_pad = padded_keys(
        keys_all, values_all, segment, token_keep_mask
    )

    def one_block(block_id):
        start = block_id * BLOCK
        query_block = lax.dynamic_slice_in_dim(queries, start, BLOCK, 0)
        key_block = lax.dynamic_slice_in_dim(key_pad, start, 3 * BLOCK, 0)
        value_block = lax.dynamic_slice_in_dim(value_pad, start, 3 * BLOCK, 0)
        allowed = allowed_pairs(segment, seg_pad, keep_pad, start)
        scores = (
            jnp.einsum("qhd,khd->hqk", query_block, key_block, preferred_element_type=jnp.float32)
            * scale
        )
        scores = jnp.where(allowed[None], scores, NEG_LARGE)
        highest = jnp.max(scores, axis=-1, keepdims=True)
        raised = jnp.exp(scores - highest)
        totals = jnp.sum(raised, axis=-1, keepdims=True)
        weights = (raised / totals).astype(jnp.bfloat16)
        attended_context = jnp.einsum(
            "hqk,khd->qhd", weights, value_block, preferred_element_type=jnp.float32
        )
        return (attended_context, (highest + jnp.log(totals))[..., 0])

    attended_context, log_totals = lax.map(
        one_block, jnp.arange(sequence_length // BLOCK, dtype=jnp.int32)
    )
    return (attended_context.reshape(sequence_length, head_count, head_width), log_totals)


def attend_backward(
    queries, keys_all, values_all, segment, token_keep_mask, log_totals, grad_context
):
    sequence_length, head_count, head_width = queries.shape
    scale = 1.0 / math.sqrt(head_width)
    key_pad, value_pad, seg_pad, keep_pad = padded_keys(
        keys_all, values_all, segment, token_keep_mask
    )

    def one_block(loop_carry, block_id):
        key_acc, value_acc = loop_carry
        start = block_id * BLOCK
        query_block = lax.dynamic_slice_in_dim(queries, start, BLOCK, 0)
        key_block = lax.dynamic_slice_in_dim(key_pad, start, 3 * BLOCK, 0)
        value_block = lax.dynamic_slice_in_dim(value_pad, start, 3 * BLOCK, 0)
        grad_block = lax.dynamic_slice_in_dim(grad_context, start, BLOCK, 0)
        allowed = allowed_pairs(segment, seg_pad, keep_pad, start)
        scores = (
            jnp.einsum("qhd,khd->hqk", query_block, key_block, preferred_element_type=jnp.float32)
            * scale
        )
        scores = jnp.where(allowed[None], scores, NEG_LARGE)
        probs = jnp.exp(scores - log_totals[block_id][..., None])
        probs_low = probs.astype(jnp.bfloat16)
        grad_probs = jnp.einsum(
            "qhd,khd->hqk", grad_block, value_block, preferred_element_type=jnp.float32
        )
        row_terms = jnp.sum(grad_probs * probs, axis=-1, keepdims=True)
        grad_scores = (probs * (grad_probs - row_terms)).astype(jnp.bfloat16)
        grad_query = (
            jnp.einsum("hqk,khd->qhd", grad_scores, key_block, preferred_element_type=jnp.float32)
            * scale
        )
        grad_key = (
            jnp.einsum("hqk,qhd->khd", grad_scores, query_block, preferred_element_type=jnp.float32)
            * scale
        )
        grad_value = jnp.einsum(
            "hqk,qhd->khd", probs_low, grad_block, preferred_element_type=jnp.float32
        )
        key_acc = lax.dynamic_update_slice_in_dim(
            key_acc, lax.dynamic_slice_in_dim(key_acc, start, 3 * BLOCK, 0) + grad_key, start, 0
        )
        value_acc = lax.dynamic_update_slice_in_dim(
            value_acc,
            lax.dynamic_slice_in_dim(value_acc, start, 3 * BLOCK, 0) + grad_value,
            start,
            0,
        )
        return ((key_acc, value_acc), grad_query)

    empty = jnp.zeros((sequence_length + 2 * BLOCK, head_count, head_width), jnp.float32)
    (key_acc, value_acc), grad_query = lax.scan(
        one_block, (empty, empty), jnp.arange(sequence_length // BLOCK, dtype=jnp.int32)
    )
    return (
        grad_query.reshape(sequence_length, head_count, head_width),
        key_acc[2 * BLOCK :],
        value_acc[2 * BLOCK :],
    )


def on_device(
    block_input_rows,
    output_gradient,
    segment_numbers,
    token_keep_mask,
    layer_norm_gain,
    layer_norm_bias,
    projection_weight,
    output_weight,
    up_weight,
    down_weight,
    adapter_first_input,
    adapter_second_projections,
    adapter_second_upward,
    adapter_first_output,
    adapter_first_down,
    adapter_second_output,
):
    local_width = projection_weight.shape[2]
    local_heads = local_width // HEAD_SIZE

    def microbatch_step(loop_carry, batch):
        adapter_gradients, norm_gradients = loop_carry
        rows_input, rows_grad, segment, keep_row = batch
        rows_input = rows_input[0]
        rows_grad = rows_grad[0]
        segment = segment[0]
        keep_row = keep_row[0]
        inputs = rows_input.astype(jnp.float32)
        part_one, part_two = norm_pair(inputs, layer_norm_gain, layer_norm_bias)
        first_normed_rows, second_normed_rows = (
            lax.all_gather(part_one.astype(jnp.bfloat16), "tensor", axis=0, tiled=True),
            lax.all_gather(part_two.astype(jnp.bfloat16), "tensor", axis=0, tiled=True),
        )
        sequence_length = first_normed_rows.shape[0]
        low_local = jnp.concatenate(
            [
                jnp.einsum(
                    "sg,zgc->zsc",
                    first_normed_rows,
                    adapter_first_input[:3],
                    preferred_element_type=jnp.float32,
                ),
                jnp.dot(
                    second_normed_rows, adapter_first_input[3], preferred_element_type=jnp.float32
                )[None],
            ],
            axis=0,
        ).astype(jnp.bfloat16)
        reduced_input = lax.all_gather(low_local, "tensor", axis=2, tiled=True)
        linear_output = jnp.einsum(
            "td,nde->nte", first_normed_rows, projection_weight, preferred_element_type=jnp.float32
        )
        linear_output = linear_output + ADAPTER_SCALE * jnp.einsum(
            "fgb,fbv->fgv",
            reduced_input[:3],
            adapter_second_projections,
            preferred_element_type=jnp.float32,
        )
        lin_heads = linear_output.reshape(3, sequence_length, local_heads, HEAD_SIZE)
        cos_table, sin_table = rotary_tables(segment)
        queries = rotate(lin_heads[0], cos_table, sin_table).astype(jnp.bfloat16)
        keys_all = rotate(lin_heads[1], cos_table, sin_table).astype(jnp.bfloat16)
        values_all = lin_heads[2].astype(jnp.bfloat16)
        context_heads, log_totals = attend_forward(queries, keys_all, values_all, segment, keep_row)
        attended_context = context_heads.reshape(sequence_length, local_width).astype(jnp.bfloat16)
        preactivation = jnp.dot(second_normed_rows, up_weight, preferred_element_type=jnp.float32)
        preactivation = preactivation + ADAPTER_SCALE * jnp.dot(
            reduced_input[3], adapter_second_upward, preferred_element_type=jnp.float32
        )
        hidden_rows = exact_gelu(preactivation).astype(jnp.bfloat16)
        low_partial = jnp.stack(
            [
                jnp.dot(attended_context, adapter_first_output, preferred_element_type=jnp.float32),
                jnp.dot(hidden_rows, adapter_first_down, preferred_element_type=jnp.float32),
            ]
        )
        reduced_output = lax.psum_scatter(
            low_partial, "tensor", scatter_dimension=2, tiled=True
        ).astype(jnp.bfloat16)
        partial_sum = jnp.dot(attended_context, output_weight, preferred_element_type=jnp.float32)
        partial_sum = partial_sum + jnp.dot(
            hidden_rows, down_weight, preferred_element_type=jnp.float32
        )
        side_branch = lax.psum_scatter(
            partial_sum
            + ADAPTER_SCALE
            * jnp.einsum(
                "mgo,mou->gu",
                reduced_output,
                adapter_second_output,
                preferred_element_type=jnp.float32,
            ),
            "tensor",
            scatter_dimension=0,
            tiled=True,
        )
        output_rows = (rows_input.astype(jnp.float32) + side_branch).astype(jnp.bfloat16)
        gradient_total = lax.all_gather(rows_grad, "tensor", axis=0, tiled=True)
        low_grad_local = (
            ADAPTER_SCALE
            * jnp.einsum(
                "ro,hno->hrn",
                gradient_total,
                adapter_second_output,
                preferred_element_type=jnp.float32,
            )
        ).astype(jnp.bfloat16)
        gradient_second_output = ADAPTER_SCALE * jnp.einsum(
            "ntr,td->nrd", reduced_output, gradient_total, preferred_element_type=jnp.float32
        )
        reduced_gradient = lax.all_gather(low_grad_local, "tensor", axis=2, tiled=True)
        gradient_first_output = jnp.einsum(
            "te,tr->er", attended_context, reduced_gradient[0], preferred_element_type=jnp.float32
        )
        gradient_first_down = jnp.einsum(
            "tf,tr->fr", hidden_rows, reduced_gradient[1], preferred_element_type=jnp.float32
        )
        grad_context = jnp.einsum(
            "td,ed->te", gradient_total, output_weight, preferred_element_type=jnp.float32
        )
        grad_context = grad_context + jnp.einsum(
            "dx,zx->dz",
            reduced_gradient[0],
            adapter_first_output,
            preferred_element_type=jnp.float32,
        )
        grad_context = grad_context.astype(jnp.bfloat16)
        grad_hidden = jnp.einsum(
            "td,fd->tf", gradient_total, down_weight, preferred_element_type=jnp.float32
        )
        grad_hidden = grad_hidden + jnp.einsum(
            "vj,bj->vb", reduced_gradient[1], adapter_first_down, preferred_element_type=jnp.float32
        )
        gelu_back = jax.vjp(exact_gelu, preactivation)[1]
        preactivation_gradient = gelu_back(grad_hidden)[0].astype(jnp.bfloat16)
        grad_query, grad_key, grad_value = attend_backward(
            queries,
            keys_all,
            values_all,
            segment,
            keep_row,
            log_totals,
            grad_context.reshape(sequence_length, local_heads, HEAD_SIZE),
        )

        def rotate_pair(query_lin, key_lin):
            return (rotate(query_lin, cos_table, sin_table), rotate(key_lin, cos_table, sin_table))

        rotate_back = jax.vjp(rotate_pair, lin_heads[0], lin_heads[1])[1]
        grad_lq, grad_lk = rotate_back((grad_query, grad_key))
        linear_gradient = (
            jnp.stack([grad_lq, grad_lk, grad_value])
            .reshape(3, sequence_length, local_width)
            .astype(jnp.bfloat16)
        )
        gradient_second_projections = ADAPTER_SCALE * jnp.einsum(
            "ntr,nte->nre", reduced_input[:3], linear_gradient, preferred_element_type=jnp.float32
        )
        gradient_second_upward = ADAPTER_SCALE * jnp.einsum(
            "tr,tf->rf",
            reduced_input[3],
            preactivation_gradient,
            preferred_element_type=jnp.float32,
        )
        low_in_partial = jnp.concatenate(
            [
                ADAPTER_SCALE
                * jnp.einsum(
                    "oqv,okv->oqk",
                    linear_gradient,
                    adapter_second_projections,
                    preferred_element_type=jnp.float32,
                ),
                (
                    ADAPTER_SCALE
                    * jnp.einsum(
                        "vp,up->vu",
                        preactivation_gradient,
                        adapter_second_upward,
                        preferred_element_type=jnp.float32,
                    )
                )[None],
            ],
            axis=0,
        )
        reduced_input_gradient = lax.psum_scatter(
            low_in_partial, "tensor", scatter_dimension=2, tiled=True
        ).astype(jnp.bfloat16)
        gradient_first_input = jnp.concatenate(
            [
                jnp.einsum(
                    "td,ntr->ndr",
                    first_normed_rows,
                    reduced_input_gradient[:3],
                    preferred_element_type=jnp.float32,
                ),
                jnp.einsum(
                    "td,tr->dr",
                    second_normed_rows,
                    reduced_input_gradient[3],
                    preferred_element_type=jnp.float32,
                )[None],
            ],
            axis=0,
        )
        grad_one = jnp.einsum(
            "nte,nde->td", linear_gradient, projection_weight, preferred_element_type=jnp.float32
        )
        grad_one = grad_one + jnp.einsum(
            "iqw,isw->qs",
            reduced_input_gradient[:3],
            adapter_first_input[:3],
            preferred_element_type=jnp.float32,
        )
        grad_two = jnp.einsum(
            "tf,df->td", preactivation_gradient, up_weight, preferred_element_type=jnp.float32
        )
        grad_two = grad_two + jnp.einsum(
            "bo,eo->be",
            reduced_input_gradient[3],
            adapter_first_input[3],
            preferred_element_type=jnp.float32,
        )
        norm_back = jax.vjp(norm_pair, inputs, layer_norm_gain, layer_norm_bias)[1]
        own_one, own_two = (
            lax.psum_scatter(grad_one, "tensor", scatter_dimension=0, tiled=True),
            lax.psum_scatter(grad_two, "tensor", scatter_dimension=0, tiled=True),
        )
        grad_rows_in, grad_gain, grad_bias = norm_back((own_one, own_two))
        input_gradient_rows = (rows_grad.astype(jnp.float32) + grad_rows_in).astype(jnp.bfloat16)
        adapter_terms = (
            gradient_first_input,
            gradient_second_projections,
            gradient_second_upward,
            gradient_first_output,
            gradient_first_down,
            gradient_second_output,
        )
        adapter_gradients = jax.tree.map(
            lambda left_operand, right_operand: left_operand + right_operand,
            adapter_gradients,
            adapter_terms,
        )
        norm_gradients = (norm_gradients[0] + grad_gain, norm_gradients[1] + grad_bias)
        return ((adapter_gradients, norm_gradients), (output_rows[None], input_gradient_rows[None]))

    adapter_offset = (
        jnp.zeros(adapter_first_input.shape, jnp.float32),
        jnp.zeros(adapter_second_projections.shape, jnp.float32),
        jnp.zeros(adapter_second_upward.shape, jnp.float32),
        jnp.zeros(adapter_first_output.shape, jnp.float32),
        jnp.zeros(adapter_first_down.shape, jnp.float32),
        jnp.zeros(adapter_second_output.shape, jnp.float32),
    )
    norm_offset = (
        jnp.zeros(layer_norm_gain.shape, jnp.float32),
        jnp.zeros(layer_norm_bias.shape, jnp.float32),
    )
    (adapter_gradients, norm_gradients), (output_total, input_gradient_total) = lax.scan(
        microbatch_step,
        (adapter_offset, norm_offset),
        (block_input_rows, output_gradient, segment_numbers, token_keep_mask),
    )
    adapter_gradients = lax.psum(
        (
            adapter_gradients[0],
            adapter_gradients[1],
            adapter_gradients[2],
            adapter_gradients[3],
            adapter_gradients[4],
            adapter_gradients[5],
        ),
        "dp",
    )
    norm_gradients = lax.psum((norm_gradients[0], norm_gradients[1]), ("dp", "tensor"))
    return (
        output_total,
        input_gradient_total,
        norm_gradients[0],
        norm_gradients[1],
        adapter_gradients[0],
        adapter_gradients[1],
        adapter_gradients[2],
        adapter_gradients[3],
        adapter_gradients[4],
        adapter_gradients[5],
    )


def solution(mesh):
    in_specs = (
        P(None, "dp", "tensor", None),
        P(None, "dp", "tensor", None),
        P(None, "dp", None),
        P(None, "dp", None),
        P(),
        P(),
        P(None, None, "tensor"),
        P("tensor", None),
        P(None, "tensor"),
        P("tensor", None),
        P(None, None, "tensor"),
        P(None, None, "tensor"),
        P(None, "tensor"),
        P("tensor", None),
        P("tensor", None),
        P(None, "tensor", None),
    )
    out_specs = (
        P(None, "dp", "tensor", None),
        P(None, "dp", "tensor", None),
        P(),
        P(),
        P(None, None, "tensor"),
        P(None, None, "tensor"),
        P(None, "tensor"),
        P("tensor", None),
        P("tensor", None),
        P(None, "tensor", None),
    )
    return jax.shard_map(
        on_device, mesh=mesh, in_specs=in_specs, out_specs=out_specs, check_vma=False
    )
```

profile of v0, /device:TPU:0, one launch (start us, length us, event | category | flops | bytes accessed | tf_op | source)
XLA Modules:
  0.0 2193.3 jit_solution(8398129028556277716)
XLA Ops:
  8.1 2095.4 %while.93 = (s32[]{:T(128)}, f32[4,1024,32]{1,2,0:T(8,128)}, f32[3,128,256]{2,1,0:T(8,128)}, f32[128,1024]{1,0:T(8,128)}, f32[256,128]{1,0:T(8,128)}, /*index=5*...) while((s32[]{:T(128)}, f32[4,1024,32]{1,2,0:T(8,128)}, ...), condition=%wide.region_23.24_spmd.clone, body=%wide.region_0.23_spmd.clone.sunk | while | flops 36162449408 | bytes 1144980864 | solution.py:445
  19.9 46.4 %all-gather.16.cloned.1.call-done = bf16[1,1,2048,1024]{3,2,1,0:T(8,128)(2,1)} async-done(((bf16[1,1,512,1024]{3,2,1,0:T(8,128)(2,1)}), bf16[1,1,2048,1024]{3,2,1,0:T(8,128)(2,1)}) %all-gather.16.cloned.1.call-update) | async-done | bytes 4194320 | tf_op jit(solution)/shard_map/while/body/eval_jaxpr/all_gather | solution.py:284
  70.8 50.0 %all-gather.10.cloned.1.call-done = bf16[2048,1024]{1,0:T(8,128)(2,1)} async-done(((bf16[512,1024]{1,0:T(8,128)(2,1)}), bf16[2048,1024]{1,0:T(8,128)(2,1)}) %all-gather.10.cloned.1.call-update) | async-done | bytes 4194320 | tf_op jit(solution)/shard_map/while/body/eval_jaxpr/all_gather | solution.py:218
  124.3 50.9 %all-gather.12.cloned.1.call-done = bf16[2048,1024]{1,0:T(8,128)(2,1)} async-done(((bf16[512,1024]{1,0:T(8,128)(2,1)}), bf16[2048,1024]{1,0:T(8,128)(2,1)}) %all-gather.12.cloned.1.call-update) | async-done | bytes 4194320 | tf_op jit(solution)/shard_map/while/body/eval_jaxpr/all_gather | solution.py:217
  206.4 34.0 %all-gather.14.cloned.1.call-done = bf16[4,2048,128]{1,2,0:T(8,128)(2,1)} async-done(((bf16[4,2048,32]{1,2,0:T(8,128)(2,1)}), bf16[4,2048,128]{1,2,0:T(8,128)(2,1)}) %all-gather.14.cloned.1.call-update) | async-done | bytes 2097168 | tf_op jit(solution)/shard_map/while/body/eval_jaxpr/all_gather | solution.py:235
  248.4 63.5 %while.94 = (s32[]{:T(128)}, bf16[4,512,4,64]{1,3,2,0:T(8,128)(2,1)}, f32[4,4,512]{2,1,0:T(4,128)S(1)}, s32[4]{0:T(128)S(1)}, bf16[3072,4,64]{0,2,1:T(8,128)(2,1...) while((s32[]{:T(128)}, ...), condition=%wide.region_8.8_spmd, body=%wide.region_5.7_spmd.sunk | while | flops 847775232 | bytes 51758428 | solution.py:118
  315.9 175.3 %while.95 = (s32[]{:T(128)}, f32[3072,4,64]{0,2,1:T(8,128)}, f32[3072,4,64]{0,2,1:T(8,128)}, f32[4,512,4,64]{1,0,3,2:T(4,128)}, s32[4]{0:T(128)S(1)}, /*index=5*...) while((s32[]{:T(128)}, f32[3072,4,64]{0,2,1:T(8,128)}, ...), condition=%wide.region_11.11_spmd, body=%wide.region_9.10_spmd.sunk | while | flops 2047608320 | bytes 133522856 | solution.py:176
  565.0 213.1 %all-reduce.25 = (bf16[4,2048,128]{1,0,2:T(4,128)(2,1)}, bf16[2,2048,128]{1,0,2:T(2,128)(2,1)}) all-reduce(f32[4,2048,128]{1,0,2:T(4,128)} %copy.115, f32[2,2048,128]{1,0,2:T(2,128)} %copy.118), channel_id=3, replica_groups=mesh['dp'=8,'tensor'=4] {'tensor'}, use_global_device_ids=true, to_apply=%region_12.12.clone | all-reduce | flops 1572864 | bytes 9437184 | tf_op jit(solution)/shard_map/while
  830.5 44.5 %reduce-scatter.4.cloned.1.call-done = f32[512,1024]{1,0:T(8,128)} async-done(((f32[2048,1024]{1,0:T(8,128)}), f32[512,1024]{1,0:T(8,128)}) %reduce-scatter.4.cloned.1.call-update) | async-done | bytes 2097168 | tf_op jit(solution)/shard_map/while/body/eval_jaxpr/reduce_scatter | solution.py:412
  874.9 89.4 %reduce-scatter.6.cloned.1.call-done = f32[512,1024]{1,0:T(8,128)} async-done(((f32[2048,1024]{1,0:T(8,128)}), f32[512,1024]{1,0:T(8,128)}) %reduce-scatter.6.cloned.1.call-update) | async-done | bytes 2097168 | tf_op jit(solution)/shard_map/while/body/eval_jaxpr/reduce_scatter | solution.py:413
  972.4 81.3 %reduce-scatter.8.cloned.1.call-done = f32[512,1024]{1,0:T(8,128)} async-done(((f32[2048,1024]{1,0:T(8,128)}), f32[512,1024]{1,0:T(8,128)}) %reduce-scatter.8.cloned.1.call-update) | async-done | bytes 2097168 | tf_op jit(solution)/shard_map/while/body/eval_jaxpr/reduce_scatter | solution.py:270
  1068.4 43.7 %all-gather.16.cloned.1.call-done = bf16[1,1,2048,1024]{3,2,1,0:T(8,128)(2,1)} async-done(((bf16[1,1,512,1024]{3,2,1,0:T(8,128)(2,1)}), bf16[1,1,2048,1024]{3,2,1,0:T(8,128)(2,1)}) %all-gather.16.cloned.1.call-update) | async-done | bytes 4194320 | tf_op jit(solution)/shard_map/while/body/eval_jaxpr/all_gather | solution.py:284
  1116.6 49.9 %all-gather.10.cloned.1.call-done = bf16[2048,1024]{1,0:T(8,128)(2,1)} async-done(((bf16[512,1024]{1,0:T(8,128)(2,1)}), bf16[2048,1024]{1,0:T(8,128)(2,1)}) %all-gather.10.cloned.1.call-update) | async-done | bytes 4194320 | tf_op jit(solution)/shard_map/while/body/eval_jaxpr/all_gather | solution.py:218
  1169.9 50.9 %all-gather.12.cloned.1.call-done = bf16[2048,1024]{1,0:T(8,128)(2,1)} async-done(((bf16[512,1024]{1,0:T(8,128)(2,1)}), bf16[2048,1024]{1,0:T(8,128)(2,1)}) %all-gather.12.cloned.1.call-update) | async-done | bytes 4194320 | tf_op jit(solution)/shard_map/while/body/eval_jaxpr/all_gather | solution.py:217
  1251.8 34.3 %all-gather.14.cloned.1.call-done = bf16[4,2048,128]{1,2,0:T(8,128)(2,1)} async-done(((bf16[4,2048,32]{1,2,0:T(8,128)(2,1)}), bf16[4,2048,128]{1,2,0:T(8,128)(2,1)}) %all-gather.14.cloned.1.call-update) | async-done | bytes 2097168 | tf_op jit(solution)/shard_map/while/body/eval_jaxpr/all_gather | solution.py:235
  1294.2 63.3 %while.94 = (s32[]{:T(128)}, bf16[4,512,4,64]{1,3,2,0:T(8,128)(2,1)}, f32[4,4,512]{2,1,0:T(4,128)S(1)}, s32[4]{0:T(128)S(1)}, bf16[3072,4,64]{0,2,1:T(8,128)(2,1...) while((s32[]{:T(128)}, ...), condition=%wide.region_8.8_spmd, body=%wide.region_5.7_spmd.sunk | while | flops 847775232 | bytes 51758428 | solution.py:118
  1361.5 175.2 %while.95 = (s32[]{:T(128)}, f32[3072,4,64]{0,2,1:T(8,128)}, f32[3072,4,64]{0,2,1:T(8,128)}, f32[4,512,4,64]{1,0,3,2:T(4,128)}, s32[4]{0:T(128)S(1)}, /*index=5*...) while((s32[]{:T(128)}, f32[3072,4,64]{0,2,1:T(8,128)}, ...), condition=%wide.region_11.11_spmd, body=%wide.region_9.10_spmd.sunk | while | flops 2047608320 | bytes 133522856 | solution.py:176
  1560.3 21.4 multiply_convert_fusion.4
  1610.4 213.1 %all-reduce.25 = (bf16[4,2048,128]{1,0,2:T(4,128)(2,1)}, bf16[2,2048,128]{1,0,2:T(2,128)(2,1)}) all-reduce(f32[4,2048,128]{1,0,2:T(4,128)} %copy.115, f32[2,2048,128]{1,0,2:T(2,128)} %copy.118), channel_id=3, replica_groups=mesh['dp'=8,'tensor'=4] {'tensor'}, use_global_device_ids=true, to_apply=%region_12.12.clone | all-reduce | flops 1572864 | bytes 9437184 | tf_op jit(solution)/shard_map/while
  1876.8 43.6 %reduce-scatter.4.cloned.1.call-done = f32[512,1024]{1,0:T(8,128)} async-done(((f32[2048,1024]{1,0:T(8,128)}), f32[512,1024]{1,0:T(8,128)}) %reduce-scatter.4.cloned.1.call-update) | async-done | bytes 2097168 | tf_op jit(solution)/shard_map/while/body/eval_jaxpr/reduce_scatter | solution.py:412
  1920.4 89.2 %reduce-scatter.6.cloned.1.call-done = f32[512,1024]{1,0:T(8,128)} async-done(((f32[2048,1024]{1,0:T(8,128)}), f32[512,1024]{1,0:T(8,128)}) %reduce-scatter.6.cloned.1.call-update) | async-done | bytes 2097168 | tf_op jit(solution)/shard_map/while/body/eval_jaxpr/reduce_scatter | solution.py:413
  2017.7 81.2 %reduce-scatter.8.cloned.1.call-done = f32[512,1024]{1,0:T(8,128)} async-done(((f32[2048,1024]{1,0:T(8,128)}), f32[512,1024]{1,0:T(8,128)}) %reduce-scatter.8.cloned.1.call-update) | async-done | bytes 2097168 | tf_op jit(solution)/shard_map/while/body/eval_jaxpr/reduce_scatter | solution.py:270
  2104.1 40.3 %all-reduce.17 = (f32[2,1024]{1,0:T(2,128)}, f32[2,1024]{1,0:T(2,128)}) all-reduce(f32[2,1024]{1,0:T(2,128)} %get-tuple-element.757, f32[2,1024]{1,0:T(2,128)} %get-tuple-element.758), channel_id=1, replica_groups=mesh['dp'=8,'tensor'=4] {'dp','tensor'}, use_global_device_ids=true, to_apply=%region_24.25 | all-reduce | flops 4096 | bytes 32768 | tf_op jit(solution)/shard_map/psum | solution.py:461
  2144.4 31.8 %all-reduce.24.cloned.1.call-done = (f32[4,1024,32]{1,2,0:T(8,128)}, f32[3,128,256]{2,1,0:T(8,128)}, f32[128,1024]{1,0:T(8,128)}, f32[256,128]{1,0:T(8,128)}, f3...) async-done(((f32[4,1024,32]{1,2,0:T(8,128)}, f32[3,128,256]{2,1,0:T(8,128)}, f32[128,1024]{1,0:T(8,128)}, f32[256,128]{1,0:T(8,128)}, f32[1024,128]{1,0:T(8,128)}, ...) | async-done | bytes 2359312 | tf_op jit(solution)/shard_map/psum | solution.py:450
  (857 shorter events, 832.2 us)
Async XLA Ops:
  8.4 58.0 %all-gather.16.cloned.1.call-start = ((), (), s32[]{:S(2)}) async-start(), calls=%async_computation.7 | async-start | bytes 5242880 | tf_op jit(solution)/shard_map/while/body/eval_jaxpr/all_gather | solution.py:284
  10.9 109.9 %all-gather.10.cloned.1.call-start = ((), (), s32[]{:S(2)}) async-start(), calls=%async_computation.4 | async-start | bytes 5242880 | tf_op jit(solution)/shard_map/while/body/eval_jaxpr/all_gather | solution.py:218
  15.5 159.8 %all-gather.12.cloned.1.call-start = ((), (), s32[]{:S(2)}) async-start(), calls=%async_computation.5 | async-start | bytes 5242880 | tf_op jit(solution)/shard_map/while/body/eval_jaxpr/all_gather | solution.py:217
  16.2 188.7 %all-gather.18.cloned.1.call-start = ((), (), s32[]{:S(2)}) async-start(), calls=%async_computation.8 | async-start | bytes 1310720 | tf_op jit(solution)/shard_map/while/body/eval_jaxpr/all_gather | solution.py:297
  19.9 227.1 %copy-start.39 = (f32[2048,8]{0,1:T(8,128)}, f32[2048,8]{0,1:T(8,128)S(1)}, u32[]{:S(2)}) copy-start(f32[2048,8]{0,1:T(8,128)S(1)} %get-tuple-element.1380) | copy-start | bytes 196612 | tf_op jit(solution)/shard_map/while
  19.9 227.1 %copy-start.41 = (f32[2048,8]{0,1:T(8,128)}, f32[2048,8]{0,1:T(8,128)S(1)}, u32[]{:S(2)}) copy-start(f32[2048,8]{0,1:T(8,128)S(1)} %get-tuple-element.1379) | copy-start | bytes 196612 | tf_op jit(solution)/shard_map/while
  70.7 169.7 %all-gather.14.cloned.1.call-start = ((), (), s32[]{:S(2)}) async-start(), calls=%async_computation.6 | async-start | bytes 2621440 | tf_op jit(solution)/shard_map/while/body/eval_jaxpr/all_gather | solution.py:235
  179.9 695.1 %reduce-scatter.4.cloned.1.call-start = ((), (), s32[]{:S(2)}) async-start(), calls=%async_computation.9 | async-start | bytes 10485760 | tf_op jit(solution)/shard_map/while/body/eval_jaxpr/reduce_scatter | solution.py:412
  565.0 215.2 %copy-start.24 = (bf16[4,1024,32]{1,2,0:T(8,128)(2,1)S(1)}, bf16[4,1024,32]{1,2,0:T(8,128)(2,1)}, u32[]{:S(2)}) copy-start(bf16[4,1024,32]{1,2,0:T(8,128)(2,1)} %get-tuple-element.1653) | copy-start | bytes 786436 | tf_op jit(solution)/shard_map/while
  788.4 176.0 %reduce-scatter.6.cloned.1.call-start = ((), (), s32[]{:S(2)}) async-start(), calls=%async_computation.10 | async-start | bytes 10485760 | tf_op jit(solution)/shard_map/while/body/eval_jaxpr/reduce_scatter | solution.py:413
  801.6 252.1 %reduce-scatter.8.cloned.1.call-start = ((), (), s32[]{:S(2)}) async-start(), calls=%async_computation.11 | async-start | bytes 10485760 | tf_op jit(solution)/shard_map/while/body/eval_jaxpr/reduce_scatter | solution.py:270
  830.4 140.6 %copy-start.68 = (f32[3,128,256]{2,1,0:T(8,128)}, f32[3,128,256]{2,1,0:T(8,128)S(1)}, u32[]{:S(2)}) copy-start(f32[3,128,256]{2,1,0:T(8,128)S(1)} %fusion.331) | copy-start | bytes 1179652 | tf_op jit(solution)/shard_map/while
  1056.9 55.3 %all-gather.16.cloned.1.call-start = ((), (), s32[]{:S(2)}) async-start(), calls=%async_computation.7 | async-start | bytes 5242880 | tf_op jit(solution)/shard_map/while/body/eval_jaxpr/all_gather | solution.py:284
  1059.4 107.0 %all-gather.10.cloned.1.call-start = ((), (), s32[]{:S(2)}) async-start(), calls=%async_computation.4 | async-start | bytes 5242880 | tf_op jit(solution)/shard_map/while/body/eval_jaxpr/all_gather | solution.py:218
  1064.0 156.9 %all-gather.12.cloned.1.call-start = ((), (), s32[]{:S(2)}) async-start(), calls=%async_computation.5 | async-start | bytes 5242880 | tf_op jit(solution)/shard_map/while/body/eval_jaxpr/all_gather | solution.py:217
  1064.7 185.6 %all-gather.18.cloned.1.call-start = ((), (), s32[]{:S(2)}) async-start(), calls=%async_computation.8 | async-start | bytes 1310720 | tf_op jit(solution)/shard_map/while/body/eval_jaxpr/all_gather | solution.py:297
  1068.4 224.4 %copy-start.39 = (f32[2048,8]{0,1:T(8,128)}, f32[2048,8]{0,1:T(8,128)S(1)}, u32[]{:S(2)}) copy-start(f32[2048,8]{0,1:T(8,128)S(1)} %get-tuple-element.1380) | copy-start | bytes 196612 | tf_op jit(solution)/shard_map/while
  1068.4 224.4 %copy-start.41 = (f32[2048,8]{0,1:T(8,128)}, f32[2048,8]{0,1:T(8,128)S(1)}, u32[]{:S(2)}) copy-start(f32[2048,8]{0,1:T(8,128)S(1)} %get-tuple-element.1379) | copy-start | bytes 196612 | tf_op jit(solution)/shard_map/while
  1116.4 169.7 %all-gather.14.cloned.1.call-start = ((), (), s32[]{:S(2)}) async-start(), calls=%async_computation.6 | async-start | bytes 2621440 | tf_op jit(solution)/shard_map/while/body/eval_jaxpr/all_gather | solution.py:235
  1225.5 694.9 %reduce-scatter.4.cloned.1.call-start = ((), (), s32[]{:S(2)}) async-start(), calls=%async_computation.9 | async-start | bytes 10485760 | tf_op jit(solution)/shard_map/while/body/eval_jaxpr/reduce_scatter | solution.py:412
  1610.4 215.2 %copy-start.24 = (bf16[4,1024,32]{1,2,0:T(8,128)(2,1)S(1)}, bf16[4,1024,32]{1,2,0:T(8,128)(2,1)}, u32[]{:S(2)}) copy-start(bf16[4,1024,32]{1,2,0:T(8,128)(2,1)} %get-tuple-element.1653) | copy-start | bytes 786436 | tf_op jit(solution)/shard_map/while
  1833.8 175.8 %reduce-scatter.6.cloned.1.call-start = ((), (), s32[]{:S(2)}) async-start(), calls=%async_computation.10 | async-start | bytes 10485760 | tf_op jit(solution)/shard_map/while/body/eval_jaxpr/reduce_scatter | solution.py:413
  1847.1 251.9 %reduce-scatter.8.cloned.1.call-start = ((), (), s32[]{:S(2)}) async-start(), calls=%async_computation.11 | async-start | bytes 10485760 | tf_op jit(solution)/shard_map/while/body/eval_jaxpr/reduce_scatter | solution.py:270
  2103.5 72.7 %all-reduce.24.cloned.1.call-start = ((), (), s32[]{:S(2)}) async-start(), calls=%async_computation.3 | async-start | bytes 4718592 | tf_op jit(solution)/shard_map/psum | solution.py:450
  (190 other events, 3162.0 us)
Sparse Core Ops, SparseCore 0:
  11.0 55.2 all-gather.15
  68.2 52.5 all-gather.9
  122.7 52.5 all-gather.11
  177.0 26.4 all-gather.17
  205.2 35.1 all-gather.13
  788.5 86.4 reduce-scatter.3
  878.0 86.3 reduce-scatter.5
  967.4 86.2 reduce-scatter.7
  1059.5 52.5 all-gather.15
  1113.8 52.5 all-gather.9
  1168.3 52.5 all-gather.11
  1222.6 26.4 all-gather.17
  1251.0 35.1 all-gather.13
  1833.9 86.4 reduce-scatter.3
  1923.3 86.2 reduce-scatter.5
  2012.6 86.3 reduce-scatter.7
Sparse Core Ops, SparseCore 1:
  2108.0 68.1 all-reduce.23
where the time goes:
time: 2200 us; the launch traced here: 2190 us
  waiting for transfers between devices  823 us (37%)
  matrix products  485 us (22%)
  blocking collectives  467 us (21%)
  local copies, waits for them, and re-layouts  221 us (10%)
  other arithmetic  144 us (7%)
  loops' own time  36.3 us (2%)
    while x2, blocking collectives  426 us
    reduce_scatter x2, waiting for transfers between devices, microbatch_step(): lax.psum_scatter(grad_two, 'tensor', scatter_dimension=0, tiled=True)  179 us
    reduce_scatter x2, waiting for transfers between devices, microbatch_step(): lax.psum_scatter(partial_sum + ADAPTER_SCALE * jnp.einsum('mgo,mou->gu',...  163 us
    all_gather x2, waiting for transfers between devices, microbatch_step(): lax.all_gather(part_one.astype(jnp.bfloat16), 'tensor', axis=0, tiled=True)  102 us
    all_gather x2, waiting for transfers between devices, microbatch_step(): lax.all_gather(part_two.astype(jnp.bfloat16), 'tensor', axis=0, tiled=True)  99.9 us
    dynamic_update_slice x16, local copies, waits for them, and re-layouts, attend_forward(): lax.map(one_block, jnp.arange(sequence_length // BLOCK, dtype=jnp.int32))  93.1 us
    all_gather x2, waiting for transfers between devices, microbatch_step(): gradient_total = lax.all_gather(rows_grad, 'tensor', axis=0, tiled=True)  90.2 us
    reduce_scatter x2, waiting for transfers between devices, microbatch_step(): lax.psum_scatter(grad_one, 'tensor', scatter_dimension=0, tiled=True)  88 us
  transfers between devices with their start and end apart: 17, of which 15 were waited for; matrix products, arithmetic and copies ran while one was open for 8% of the time, Pallas kernels for 0%

commit v1 on v0

v1 whole, which is shorter than its diff:
```python
import functools
import math

import jax
import jax.numpy as jnp
from jax import lax
from jax.experimental import pallas as pl
from jax.experimental.pallas import tpu as pltpu
from jax.sharding import PartitionSpec as P

HEAD = 64
HALF = 8
N_DOCS = 5
TILE = 256
SLOTS = 5
EPSILON = 1e-05
SCALE = 0.25
F32 = jnp.float32
BF = jnp.bfloat16


def dot(a, b, ca, cb):
    return lax.dot_general(a, b, (((ca,), (cb,)), ((), ())), preferred_element_type=F32)


def attention_kernel(heads, lo_ref, lin_ref, g_ref, cos_ref, sin_ref, segq_ref, segk_ref,
                     ctx_ref, dlin_ref, qt, kt, vt, kn, vn, qz, acc, s_scr, e_scr):
    width = heads * HEAD
    length = lin_ref.shape[1]
    blocks = length // TILE

    def rotate(z, cos, sin):
        a, b = z[:HALF], z[HALF:2 * HALF]
        return jnp.concatenate([a * cos - b * sin, b * cos + a * sin, z[2 * HALF:]], axis=0)

    def prepare(c, carry):
        cols = pl.ds(pl.multiple_of(c * TILE, TILE), TILE)
        cos, sin = cos_ref[:, cols], sin_ref[:, cols]
        for h in range(heads):
            rows = pl.ds(h * HEAD, HEAD)
            q = rotate(lin_ref[pl.ds(h * HEAD, HEAD), cols], cos, sin).astype(BF).astype(F32) * 0.125
            k = rotate(lin_ref[pl.ds(width + h * HEAD, HEAD), cols], cos, sin)
            v = lin_ref[pl.ds(2 * width + h * HEAD, HEAD), cols]
            qt[rows, cols] = q.astype(BF)
            kt[rows, cols] = k.astype(BF)
            vt[rows, cols] = v.astype(BF)
            kn[h, cols, :] = jnp.transpose(k).astype(BF)
            vn[h, cols, :] = jnp.transpose(v).astype(BF)
            qn = jnp.transpose(q)
            qz[h, cols, :] = jnp.concatenate([jnp.zeros_like(qn), qn], axis=1).astype(BF)
            acc[h, cols, :] = jnp.zeros((TILE, 2 * HEAD), F32)
        return carry

    lax.fori_loop(0, blocks, prepare, 0)

    def query_block(qb, carry):
        lo = lo_ref[qb]
        qcols = pl.ds(pl.multiple_of(qb * TILE, TILE), TILE)
        segq = segq_ref[:, qcols]

        def scores(kb, tops):
            krows = pl.ds(pl.multiple_of(kb * TILE, TILE), TILE)
            kpos = kb * TILE + lax.broadcasted_iota(jnp.int32, (TILE, TILE), 0)
            qpos = qb * TILE + lax.broadcasted_iota(jnp.int32, (TILE, TILE), 1)
            allowed = ((segk_ref[krows, :] == segq) & (kpos <= qpos)) | (kpos == qpos)
            out = []
            for h in range(heads):
                s = dot(kn[h, krows, :], qt[pl.ds(h * HEAD, HEAD), qcols], 1, 0)
                s = jnp.where(allowed, s, -1e30)
                s_scr[h, kb - lo] = s
                out.append(jnp.maximum(tops[h], jnp.max(s, axis=0, keepdims=True)))
            return tuple(out)

        tops = lax.fori_loop(lo, qb + 1, scores,
                             tuple(jnp.full((1, TILE), -1e30, F32) for _ in range(heads)))

        def weights(kb, sums):
            kcols = pl.ds(pl.multiple_of(kb * TILE, TILE), TILE)
            out = []
            for h in range(heads):
                e = jnp.exp(s_scr[h, kb - lo] - tops[h])
                low = e.astype(BF)
                e_scr[h, kb - lo] = low
                total, ctx = sums[h]
                out.append((total + jnp.sum(e, axis=0, keepdims=True),
                            ctx + dot(vt[pl.ds(h * HEAD, HEAD), kcols], low, 1, 0)))
            return tuple(out)

        sums = lax.fori_loop(lo, qb + 1, weights,
                             tuple((jnp.zeros((1, TILE), F32), jnp.zeros((HEAD, TILE), F32))
                                   for _ in range(heads)))
        gts, gzs, terms = [], [], []
        for h in range(heads):
            rows = pl.ds(h * HEAD, HEAD)
            inverse = 1.0 / sums[h][0]
            ctx = sums[h][1] * inverse
            ctx_ref[rows, qcols] = ctx.astype(BF)
            g = g_ref[rows, qcols].astype(F32)
            terms.append(jnp.sum(g * ctx, axis=0, keepdims=True) * inverse)
            g = g * inverse
            gts.append(g.astype(BF))
            gn = jnp.transpose(g)
            gzs.append(jnp.concatenate([gn, jnp.zeros_like(gn)], axis=1).astype(BF))

        def backward(kb, dqs):
            krows = pl.ds(pl.multiple_of(kb * TILE, TILE), TILE)
            out = []
            for h in range(heads):
                low = e_scr[h, kb - lo]
                dp = dot(vn[h, krows, :], gts[h], 1, 0)
                ds = (low.astype(F32) * (dp - terms[h])).astype(BF)
                acc[h, krows, :] += dot(low, gzs[h], 1, 0) + dot(ds, qz[h, qcols, :], 1, 0)
                out.append(dqs[h] + dot(kt[pl.ds(h * HEAD, HEAD), krows], ds, 1, 0))
            return tuple(out)

        dqs = lax.fori_loop(lo, qb + 1, backward,
                            tuple(jnp.zeros((HEAD, TILE), F32) for _ in range(heads)))
        cos, sin = cos_ref[:, qcols], sin_ref[:, qcols]
        for h in range(heads):
            dlin_ref[pl.ds(h * HEAD, HEAD), qcols] = rotate(dqs[h] * 0.125, cos, -sin).astype(BF)
        return carry

    lax.fori_loop(0, blocks, query_block, 0)

    def finish(c, carry):
        cols = pl.ds(pl.multiple_of(c * TILE, TILE), TILE)
        cos, sin = cos_ref[:, cols], sin_ref[:, cols]
        for h in range(heads):
            both = jnp.transpose(acc[h, cols, :])
            dlin_ref[pl.ds(width + h * HEAD, HEAD), cols] = rotate(both[HEAD:], cos, -sin).astype(BF)
            dlin_ref[pl.ds(2 * width + h * HEAD, HEAD), cols] = both[:HEAD].astype(BF)
        return carry

    lax.fori_loop(0, blocks, finish, 0)


def attention(lin, g, cos, sin, segment, keep):
    width, length = g.shape
    heads = width // HEAD
    starts = jnp.sum(segment[None, :] < jnp.arange(N_DOCS, dtype=jnp.int32)[:, None], axis=1)
    firsts = segment[::TILE]
    lo = jnp.sum(jnp.where(firsts[:, None] == jnp.arange(N_DOCS)[None, :], starts[None, :], 0), axis=1)
    lo = (lo // TILE).astype(jnp.int32)
    segk = jnp.where(keep == 1, segment, -1)[:, None]
    vmem = pl.BlockSpec(memory_space=pltpu.VMEM)
    return pl.pallas_call(
        functools.partial(attention_kernel, heads),
        grid_spec=pltpu.PrefetchScalarGridSpec(
            num_scalar_prefetch=1,
            in_specs=[vmem] * 6,
            out_specs=[vmem] * 2,
            scratch_shapes=[
                pltpu.VMEM((width, length), BF),
                pltpu.VMEM((width, length), BF),
                pltpu.VMEM((width, length), BF),
                pltpu.VMEM((heads, length, HEAD), BF),
                pltpu.VMEM((heads, length, HEAD), BF),
                pltpu.VMEM((heads, length, 2 * HEAD), BF),
                pltpu.VMEM((heads, length, 2 * HEAD), F32),
                pltpu.VMEM((heads, SLOTS, TILE, TILE), F32),
                pltpu.VMEM((heads, SLOTS, TILE, TILE), BF),
            ]),
        out_shape=[jax.ShapeDtypeStruct((width, length), BF), jax.ShapeDtypeStruct((3 * width, length), BF)],
        compiler_params=pltpu.CompilerParams(vmem_limit_bytes=60 << 20),
        name="attention",
        cost_estimate=pl.CostEstimate(flops=20 * heads * length * 768 * 64, transcendentals=heads * length * 768,
                                      bytes_accessed=13 * width * length * 2),
    )(lo, lin, g, cos, sin, segment[None, :], segk)


def rotary_tables(segment):
    length = segment.shape[0]
    starts = jnp.sum(segment[None, :] < jnp.arange(N_DOCS, dtype=jnp.int32)[:, None], axis=1)
    begin = jnp.sum(jnp.where(segment[None, :] == jnp.arange(N_DOCS)[:, None], starts[:, None], 0), axis=0)
    position = (jnp.arange(length, dtype=jnp.int32) - begin).astype(F32)
    exponent = jnp.arange(HALF, dtype=F32) / HALF
    frequency = jnp.exp(-math.log(10000.0) * exponent)
    angles = frequency[:, None] * position[None, :]
    return jnp.cos(angles), jnp.sin(angles)


def normalized(values):
    average = jnp.mean(values, axis=-1, keepdims=True)
    centered = values - average
    variance = jnp.mean(centered * centered, axis=-1, keepdims=True)
    inverse = lax.rsqrt(variance + EPSILON)
    return centered * inverse, inverse


def on_device(x, gy, segment, keep, gain, bias, w_qkv, w_out, w_up, w_down,
              a_in, b_qkv, b_up, a_out, a_down, b_out):
    width = w_qkv.shape[2]
    micro = x.shape[0]
    a_full = lax.all_gather(a_in, "tensor", axis=2, tiled=True)
    b_full = lax.all_gather(b_out, "tensor", axis=1, tiled=True)

    m_qkv = jnp.concatenate([
        (w_qkv[i].astype(F32) + SCALE * dot(a_full[i], b_qkv[i], 1, 0)).astype(BF) for i in range(3)
    ], axis=1)
    m_up = (w_up.astype(F32) + SCALE * dot(a_full[3], b_up, 1, 0)).astype(BF)
    m_out = (w_out.astype(F32) + SCALE * dot(a_out, b_full[0], 1, 0)).astype(BF)
    m_down = (w_down.astype(F32) + SCALE * dot(a_down, b_full[1], 1, 0)).astype(BF)
    a_three = jnp.concatenate([a_full[0], a_full[1], a_full[2]], axis=1)
    b_both = jnp.concatenate([b_full[0], b_full[1]], axis=0)

    outs, grads, sums = [], [], None
    for m in range(micro):
        rows, seg = x[m, 0], segment[m, 0]
        xg = lax.all_gather(rows, "tensor", axis=0, tiled=True)
        gg = lax.all_gather(gy[m, 0], "tensor", axis=0, tiled=True)
        standard, _ = normalized(xg.astype(F32))
        n1 = (standard * gain[0] + bias[0]).astype(BF)
        n2 = (standard * gain[1] + bias[1]).astype(BF)
        lin = dot(m_qkv, n1, 0, 1)
        low3 = dot(n1, a_three, 1, 0).astype(BF)
        low1 = dot(n2, a_full[3], 1, 0).astype(BF)
        g_ctx = dot(m_out, gg, 1, 1).astype(BF)
        low_grad = (SCALE * dot(gg, b_both, 1, 1)).astype(BF)
        cos, sin = rotary_tables(seg)
        ctx, d_lin = attention(lin, g_ctx, cos, sin, seg, keep[m, 0])

        pre = dot(n2, m_up, 1, 0)
        cdf = 0.5 * (1.0 + lax.erf(pre * math.sqrt(0.5)))
        hidden = (pre * cdf).astype(BF)
        slope = cdf + pre * (math.sqrt(0.5 / math.pi) * jnp.exp(-0.5 * pre * pre))
        d_pre = (dot(gg, m_down, 1, 1) * slope).astype(BF)

        part = dot(ctx, m_out, 0, 0) + dot(hidden, m_down, 1, 0)
        branch = lax.psum_scatter(part.astype(BF), "tensor", scatter_dimension=0, tiled=True)
        outs.append((rows.astype(F32) + branch.astype(F32)).astype(BF))

        one = dot(d_lin, m_qkv, 0, 1)
        two = dot(d_pre, m_up, 1, 1)
        total = (gain[0] * one + gain[1] * two).astype(BF)
        total = lax.psum_scatter(total, "tensor", scatter_dimension=0, tiled=True).astype(F32)
        own, inverse = normalized(rows.astype(F32))
        grad = total - jnp.mean(total, axis=-1, keepdims=True)
        grad = grad - own * jnp.mean(total * own, axis=-1, keepdims=True)
        grads.append((gy[m, 0].astype(F32) + grad * inverse).astype(BF))

        norms = jnp.stack([jnp.sum(one * standard, axis=0), jnp.sum(two * standard, axis=0),
                           jnp.sum(one, axis=0), jnp.sum(two, axis=0)])
        lo_ctx = dot(ctx, a_out, 0, 0).astype(BF)
        lo_hid = dot(hidden, a_down, 1, 0).astype(BF)
        d_b_out = SCALE * jnp.stack([dot(lo_ctx, gg, 0, 0), dot(lo_hid, gg, 0, 0)], axis=1)
        d_a_out = dot(ctx, low_grad[:, :128], 1, 0)
        d_a_down = dot(hidden, low_grad[:, 128:], 0, 0)
        d_b_qkv = SCALE * jnp.stack([
            dot(low3[:, 128 * i:128 * (i + 1)], d_lin[width * i:width * (i + 1)], 0, 1) for i in range(3)])
        d_b_up = SCALE * dot(low1, d_pre, 0, 0)
        back = [(SCALE * dot(d_lin[width * i:width * (i + 1)], b_qkv[i], 0, 1)).astype(BF) for i in range(3)]
        back.append((SCALE * dot(d_pre, b_up, 1, 1)).astype(BF))
        d_a_in = jnp.stack([dot(back[i], n1 if i < 3 else n2, 0, 0) for i in range(4)], axis=1)
        terms = (d_a_in, d_b_qkv, d_b_up, d_a_out, d_a_down, d_b_out, norms)
        sums = terms if sums is None else tuple(p + q for p, q in zip(sums, terms))

    d_a_in, d_b_qkv, d_b_up, d_a_out, d_a_down, d_b_out, norms = sums
    d_a_in = lax.psum_scatter(d_a_in, "tensor", scatter_dimension=0, tiled=True)
    d_b_out = lax.psum_scatter(d_b_out, "tensor", scatter_dimension=0, tiled=True)
    d_a_in, d_b_qkv, d_b_up, d_a_out, d_a_down, d_b_out = lax.psum(
        (d_a_in, d_b_qkv, d_b_up, d_a_out, d_a_down, d_b_out), "dp")
    norms = lax.psum(norms, ("dp", "tensor"))
    return (jnp.stack(outs)[:, None], jnp.stack(grads)[:, None], norms[:2], norms[2:],
            jnp.transpose(d_a_in, (1, 2, 0)), d_b_qkv, d_b_up, d_a_out, d_a_down,
            jnp.transpose(d_b_out, (1, 0, 2)))


def solution(mesh):
    in_specs = (
        P(None, "dp", "tensor", None),
        P(None, "dp", "tensor", None),
        P(None, "dp", None),
        P(None, "dp", None),
        P(),
        P(),
        P(None, None, "tensor"),
        P("tensor", None),
        P(None, "tensor"),
        P("tensor", None),
        P(None, None, "tensor"),
        P(None, None, "tensor"),
        P(None, "tensor"),
        P("tensor", None),
        P("tensor", None),
        P(None, "tensor", None),
    )
    out_specs = (
        P(None, "dp", "tensor", None),
        P(None, "dp", "tensor", None),
        P(),
        P(),
        P(None, None, "tensor"),
        P(None, None, "tensor"),
        P(None, "tensor"),
        P("tensor", None),
        P("tensor", None),
        P(None, "tensor", None),
    )
    return jax.shard_map(
        on_device, mesh=mesh, in_specs=in_specs, out_specs=out_specs, check_vma=False
    )
```

time: 2200 us -> 805 us (0.37)
  waiting for transfers between devices: 823 us -> 340 us
  blocking collectives: 467 us -> 54.9 us
  matrix products: 485 us -> 223 us
  local copies, waits for them, and re-layouts: 221 us -> 26.7 us
  other arithmetic: 144 us -> 41.5 us
  Pallas kernels: 0 us -> 96.1 us
  loops' own time: 36.3 us -> 0 us
    while x2 -> x0, blocking collectives: 426 us -> none
    reduce_scatter x6, waiting for transfers between devices: 429 us -> 129 us  [the longest x2 109 us: on_device(): lax.psum_scatter(part.astype(BF), 'tensor', scatter_dimension=0, tiled=True)]
    dot_general x112 -> x50, matrix products: 478 us -> 223 us  [dot(): lax.dot_general(a, b, (((ca,), (cb,)), ((), ())), preferred_element_type=...]
    all_gather x10 -> x5, waiting for transfers between devices: 360 us -> 144 us  [the longest x2 94.9 us: on_device(): xg = lax.all_gather(rows, 'tensor', axis=0, tiled=True)]
    pallas_call x0 -> x2, Pallas kernels: none -> 96.1 us  [attention(): pl.pallas_call(functools.partial(attention_kernel, heads), grid_spec=pltp...]
    dynamic_update_slice x16 -> x0, local copies, waits for them, and re-layouts: 93.1 us -> none  [attend_forward(): lax.map(one_block, jnp.arange(sequence_length // BLOCK, dtype=jnp.int32))]
    while x394 -> x0, local copies, waits for them, and re-layouts: 40 us -> none
    convert_element_type x12 -> x2, other arithmetic: 48 us -> 9.05 us  [the longest x1 9.04 us: on_device(): n1 = (standard * gain[0] + bias[0]).astype(BF)]
  transfers between devices with their start and end apart: 17 -> 12, of which waited for: 15 -> 7; matrix products, arithmetic and copies ran while one was open for 8% -> 25% of each run, Pallas kernels for 0% -> 6%
where the time goes in v1:
time: 805 us; the launch traced here: 798 us
  waiting for transfers between devices  340 us (42%)
  matrix products  223 us (28%)
  Pallas kernels  96.1 us (12%)
  blocking collectives  54.9 us (7%)
  other arithmetic  41.5 us (5%)
  local copies, waits for them, and re-layouts  26.7 us (3%)
  between operations  15.4 us (2%)
    dot_general x50, matrix products, dot(): lax.dot_general(a, b, (((ca,), (cb,)), ((), ())), preferred_element_type=...  223 us
    reduce_scatter x2, waiting for transfers between devices, on_device(): lax.psum_scatter(part.astype(BF), 'tensor', scatter_dimension=0, tiled=True)  109 us
    pallas_call x2, Pallas kernels, attention(): pl.pallas_call(functools.partial(attention_kernel, heads), grid_spec=pltp...  96.1 us
    all_gather x2, waiting for transfers between devices, on_device(): xg = lax.all_gather(rows, 'tensor', axis=0, tiled=True)  94.9 us
    psum x1, waiting for transfers between devices, on_device(): lax.psum((d_a_in, d_b_qkv, d_b_up, d_a_out, d_a_down, d_b_out), 'dp')  64.4 us
    all_gather x2, waiting for transfers between devices, on_device(): gg = lax.all_gather(gy[m, 0], 'tensor', axis=0, tiled=True)  49.5 us
    psum x1, blocking collectives, on_device(): norms = lax.psum(norms, ('dp', 'tensor'))  41.8 us
    reduce_scatter x2, waiting for transfers between devices, on_device(): lax.psum_scatter(total, 'tensor', scatter_dimension=0, tiled=True)  20.5 us
  transfers between devices with their start and end apart: 12, of which 7 were waited for; matrix products, arithmetic and copies ran while one was open for 25% of the time, Pallas kernels for 6%

profile of v1, /device:TPU:0, one launch (start us, length us, event | category | flops | bytes accessed | tf_op | source)
XLA Modules:
  0.0 798.0 jit_solution(4148486924408884444)
XLA Ops:
  16.9 13.2 %all_gather.20 = bf16[2,128,1024]{2,1,0:T(8,128)(2,1)S(1)} all-gather(bf16[2,32,1024]{2,1,0:T(8,128)(2,1)S(1)} %copy-done.44), channel_id=1, replica_groups=mesh['dp'=8,'tensor'=4] {'tensor'}, dimensions={1}, use_global_device_ids=true | all-gather | bytes 655360 | tf_op jit(solution)/shard_map/all_gather | solution.py:195
  49.4 45.6 %all-gather.16.cloned.1.call-done = bf16[1,1,2048,1024]{3,2,1,0:T(8,128)(2,1)} async-done(((bf16[1,1,512,1024]{3,2,1,0:T(8,128)(2,1)}), bf16[1,1,2048,1024]{3,2,1,0:T(8,128)(2,1)}) %all-gather.16.cloned.1.call-update) | async-done | bytes 4194320 | tf_op jit(solution)/shard_map/all_gather | solution.py:209
  100.1 49.3 %all-gather.12.cloned.1.call-done = bf16[1,1,2048,1024]{3,2,1,0:T(8,128)(2,1)} async-done(((bf16[1,1,512,1024]{3,2,1,0:T(8,128)(2,1)}), bf16[1,1,2048,1024]{3,2,1,0:T(8,128)(2,1)}) %all-gather.12.cloned.1.call-update) | async-done | bytes 4194320 | tf_op jit(solution)/shard_map/all_gather | solution.py:209
  154.3 49.5 %all-gather.18.cloned.1.call-done = bf16[1,1,2048,1024]{3,2,1,0:T(8,128)(2,1)} async-done(((bf16[1,1,512,1024]{3,2,1,0:T(8,128)(2,1)}), bf16[1,1,2048,1024]{3,2,1,0:T(8,128)(2,1)}) %all-gather.18.cloned.1.call-update) | async-done | bytes 4194320 | tf_op jit(solution)/shard_map/all_gather | solution.py:210
  208.3 9.0 %fusion.22 = (bf16[2048,1024]{1,0:T(8,128)(2,1)S(1)}, bf16[2048,1024]{1,0:T(8,128)(2,1)}, bf16[2048,1024]{1,0:T(8,128)(2,1)}, bf16[2048,1024]{1,0:T(8,128)(2,1)}) fusion(bf16[1,1,2048,1024]{3,2,1,0:T(8,128)(2,1)S(1)} %copy-done.6, f32[2048]{0:T(1024)S(1)} %add_rsqrt_fusion, f32[2048]{0:T(1024)S(1)} %broadcast_multiply_fusion, f32[1024]{0:T(1024)S(1)} %bitcast.389, ...), kind=kLoop, calls=%fused_computation.28 | loop fusion | flops 37748736 | bytes 25214976 | tf_op jit(solution)/shard_map/convert_element_type | solution.py:212
  222.9 48.2 %attention.3 = (bf16[256,2048]{1,0:T(8,128)(2,1)}, bf16[768,2048]{1,0:T(8,128)(2,1)}) custom-call(s32[8]{0:T(128)} %and_select_fusion.lo_ref, f32[768,2048]{1,0:T(8,128)} %fusion.238.lin_ref, bf16[256,2048]{1,0:T(8,128)(2,1)} %fusion.77.g_ref, f32[8,2048]{1,0:T(8,128)} %get-tuple-element.113.cos_ref, f32[8,2048]{1,0:T(8,128)} %get-tuple-element.114.sin_ref, ...), custom_call_target="tpu_custom_call" | custom-call | flops 8053063680 | bytes 13631488 | tf_op jit(solution)/shard_map/attention/pallas_call | solution.py:146
  285.1 8.7 %fusion.239.lin_ref = f32[768,2048]{1,0:T(8,128)} fusion(bf16[2048,1024]{1,0:T(8,128)(2,1)} %get-tuple-element.98, bf16[1024,256]{0,1:T(8,128)(2,1)S(1)} %fusion.120, bf16[1024,256]{0,1:T(8,128)(2,1)S(1)} %fusion.119, bf16[1024,256]{0,1:T(8,128)(2,1)S(1)} %fusion.118), kind=kOutput, calls=%fused_computation.312 | convolution fusion | flops 3225944064 | bytes 12058624 | tf_op jit(solution)/shard_map/dot_general | solution.py:23
  298.2 47.9 %attention.2 = (bf16[256,2048]{1,0:T(8,128)(2,1)}, bf16[768,2048]{1,0:T(8,128)(2,1)}) custom-call(s32[8]{0:T(128)} %and_select_fusion.1.lo_ref, f32[768,2048]{1,0:T(8,128)} %fusion.239.lin_ref, bf16[256,2048]{1,0:T(8,128)(2,1)} %fusion.74.g_ref, f32[8,2048]{1,0:T(8,128)} %get-tuple-element.106.cos_ref, f32[8,2048]{1,0:T(8,128)} %get-tuple-element.105.sin_ref, ...), custom_call_target="tpu_custom_call" | custom-call | flops 8053063680 | bytes 13631488 | tf_op jit(solution)/shard_map/attention/pallas_call | solution.py:146
  360.2 8.9 %multiply_convert_fusion = (bf16[2048,1024]{1,0:T(8,128)(2,1)}, f32[2048,1024]{1,0:T(8,128)S(1)}) fusion(bf16[2048,1024]{1,0:T(8,128)(2,1)} %get-tuple-element.78, bf16[1024,1024]{1,0:T(8,128)(2,1)} %add_convert_fusion.5), kind=kOutput, calls=%fused_computation.49 | convolution fusion | flops 4305453056 | bytes 18874368 | tf_op jit(solution)/shard_map/dot_general | solution.py:23
  369.1 8.5 %fusion.39 = bf16[2048,1024]{1,0:T(8,128)(2,1)} fusion(f32[2048,1024]{1,0:T(8,128)S(1)} %get-tuple-element.116, bf16[1024,1024]{1,0:T(8,128)(2,1)S(1)} %copy-done.28, bf16[1,1,2048,1024]{3,2,1,0:T(8,128)(2,1)S(1)} %copy-done.11), kind=kOutput, calls=%fused_computation.45 | convolution fusion | flops 4315938816 | bytes 18874368 | tf_op jit(solution)/shard_map/dot_general | solution.py:23
  384.4 10.3 %multiply_convert_fusion.1 = (bf16[2048,1024]{1,0:T(8,128)(2,1)}, f32[2048,1024]{1,0:T(8,128)}) fusion(bf16[2048,1024]{1,0:T(8,128)(2,1)} %get-tuple-element.97, bf16[1024,1024]{1,0:T(8,128)(2,1)} %add_convert_fusion.5), kind=kOutput, calls=%fused_computation.52 | convolution fusion | flops 4305453056 | bytes 18874368 | tf_op jit(solution)/shard_map/dot_general | solution.py:23
  420.0 11.9 %fusion.33 = bf16[2048,1024]{1,0:T(8,128)(2,1)} fusion(f32[2048,1024]{1,0:T(8,128)} %get-tuple-element.118, bf16[1024,1024]{1,0:T(8,128)(2,1)} %add_convert_fusion.4, bf16[1,1,2048,1024]{3,2,1,0:T(8,128)(2,1)} %all-gather.14.cloned.1.call-done), kind=kOutput, calls=%fused_computation.39 | convolution fusion | flops 4315938816 | bytes 18874368 | tf_op jit(solution)/shard_map/dot_general | solution.py:23
  443.0 7.1 fusion.248
  450.2 7.7 fusion.11
  458.0 7.3 fusion.249
  465.3 7.7 fusion.25
  483.4 7.0 fusion.246
  498.8 41.8 %psum.49 = f32[4,1024]{1,0:T(4,128)S(1)} all-reduce(f32[4,1024]{1,0:T(4,128)S(1)} %maximum_add_fusion.3), channel_id=1, replica_groups=mesh['dp'=8,'tensor'=4] {'dp','tensor'}, use_global_device_ids=true, to_apply=%region_30.31 | all-reduce | flops 4096 | bytes 32768 | tf_op jit(solution)/shard_map/psum | solution.py:262
  561.5 7.3 fusion.152
  568.8 7.0 fusion.140
  578.3 20.5 %reduce-scatter.13.cloned.1.call-done = bf16[512,1024]{1,0:T(8,128)(2,1)} async-done(((bf16[2048,1024]{1,0:T(8,128)(2,1)}), bf16[512,1024]{1,0:T(8,128)(2,1)}) %reduce-scatter.13.cloned.1.call-update) | async-done | bytes 1048592 | tf_op jit(solution)/shard_map/reduce_scatter | solution.py:235
  600.9 53.3 %reduce-scatter.9.cloned.1.call-done = bf16[512,1024]{1,0:T(8,128)(2,1)} async-done(((bf16[2048,1024]{1,0:T(8,128)(2,1)}), bf16[512,1024]{1,0:T(8,128)(2,1)}) %reduce-scatter.9.cloned.1.call-update) | async-done | bytes 1048592 | tf_op jit(solution)/shard_map/reduce_scatter | solution.py:229
  654.2 55.6 %reduce-scatter.7.cloned.1.call-done = bf16[512,1024]{1,0:T(8,128)(2,1)} async-done(((bf16[2048,1024]{1,0:T(8,128)(2,1)}), bf16[512,1024]{1,0:T(8,128)(2,1)}) %reduce-scatter.7.cloned.1.call-update) | async-done | bytes 1048592 | tf_op jit(solution)/shard_map/reduce_scatter | solution.py:229
  716.6 64.4 %all-reduce.3.cloned.1.call-done = (f32[4,1024,32]{1,2,0:T(8,128)}, f32[3,128,256]{2,1,0:T(8,128)}, f32[128,1024]{1,0:T(8,128)}, f32[256,128]{1,0:T(8,128)}, f32[1024,128]{1,0:T(8,128)}, /*index=5*/f32[2,32,1024]{2,1,0:T(8,128)}) async-done(((f32[4,1024,32]{1,2,0:T(8,128)}, f32[3,128,256]{2,1,0:T(8,128)}, f32[128,1024]{1,0:T(8,128)}, f32[256,128]{1,0:T(8,128)}, f32[1024,128]{1,0:T(8,128)}, ...) | async-done | bytes 2359312 | tf_op jit(solution)/shard_map/psum | solution.py:260
  (224 shorter events, 185.0 us)
Async XLA Ops:
  7.2 29.1 %copy-start = (bf16[1024,128]{1,0:T(8,128)(2,1)S(1)}, bf16[1024,128]{1,0:T(8,128)(2,1)}, u32[]{:S(2)}) copy-start(bf16[1024,128]{1,0:T(8,128)(2,1)} %param.30) | copy-start | bytes 786436
  7.2 33.9 %all-gather.10.cloned.1.call-start = ((), (), s32[]{:S(2)}) async-start(), calls=%async_computation.6 | async-start | bytes 1310720 | tf_op jit(solution)/shard_map/all_gather | solution.py:194
  7.9 87.0 %all-gather.16.cloned.1.call-start = ((), (), s32[]{:S(2)}) async-start(), calls=%async_computation.15 | async-start | bytes 5242880 | tf_op jit(solution)/shard_map/all_gather | solution.py:209
  11.1 138.3 %all-gather.12.cloned.1.call-start = ((), (), s32[]{:S(2)}) async-start(), calls=%async_computation.13 | async-start | bytes 5242880 | tf_op jit(solution)/shard_map/all_gather | solution.py:209
  11.8 191.9 %all-gather.18.cloned.1.call-start = ((), (), s32[]{:S(2)}) async-start(), calls=%async_computation.16 | async-start | bytes 5242880 | tf_op jit(solution)/shard_map/all_gather | solution.py:210
  13.4 280.4 %all-gather.14.cloned.1.call-start = ((), (), s32[]{:S(2)}) async-start(), calls=%async_computation.14 | async-start | bytes 5242880 | tf_op jit(solution)/shard_map/all_gather | solution.py:210
  14.0 561.8 %reduce-scatter.17.cloned.1.call-start = ((), (), s32[]{:S(2)}) async-start(), calls=%async_computation.12 | async-start | bytes 1310720 | tf_op jit(solution)/shard_map/reduce_scatter | solution.py:259
  36.3 9.2 %copy-start.27 = (bf16[128,1024]{1,0:T(8,128)(2,1)S(1)}, bf16[128,1024]{1,0:T(8,128)(2,1)}, u32[]{:S(2)}) copy-start(bf16[128,1024]{1,0:T(8,128)(2,1)} %param.28) | copy-start | bytes 786436
  42.4 242.6 %copy-start.31 = (bf16[1024,256]{0,1:T(8,128)(2,1)}, bf16[1024,256]{0,1:T(8,128)(2,1)S(1)}, u32[]{:S(2)}) copy-start(bf16[1024,256]{0,1:T(8,128)(2,1)S(1)} %fusion.118) | copy-start | bytes 1572868
  43.9 241.1 %copy-start.33 = (bf16[1024,256]{0,1:T(8,128)(2,1)}, bf16[1024,256]{0,1:T(8,128)(2,1)S(1)}, u32[]{:S(2)}) copy-start(bf16[1024,256]{0,1:T(8,128)(2,1)S(1)} %fusion.119) | copy-start | bytes 1572868
  45.4 239.6 %copy-start.36 = (bf16[1024,256]{0,1:T(8,128)(2,1)}, bf16[1024,256]{0,1:T(8,128)(2,1)S(1)}, u32[]{:S(2)}) copy-start(bf16[1024,256]{0,1:T(8,128)(2,1)S(1)} %fusion.120) | copy-start | bytes 1572868
  360.2 8.9 %copy-start.11 = (bf16[1,1,2048,1024]{3,2,1,0:T(8,128)(2,1)S(1)}, bf16[1,1,2048,1024]{3,2,1,0:T(8,128)(2,1)}, u32[]{:S(2)}) copy-start(bf16[1,1,2048,1024]{3,2,1,0:T(8,128)(2,1)} %all-gather.18.cloned.1.call-done) | copy-start | bytes 12582916
  360.2 8.9 %copy-start.28 = (bf16[1024,1024]{1,0:T(8,128)(2,1)S(1)}, bf16[1024,1024]{1,0:T(8,128)(2,1)}, u32[]{:S(2)}) copy-start(bf16[1024,1024]{1,0:T(8,128)(2,1)} %add_convert_fusion.4) | copy-start | bytes 6291460
  384.4 10.3 %copy-start.14 = (bf16[256,2048]{1,0:T(8,128)(2,1)S(1)}, bf16[256,2048]{1,0:T(8,128)(2,1)}, u32[]{:S(2)}) copy-start(bf16[256,2048]{1,0:T(8,128)(2,1)} %get-tuple-element.15) | copy-start | bytes 3145732
  420.0 155.8 %reduce-scatter.15.cloned.1.call-start = ((), (), s32[]{:S(2)}) async-start(), calls=%async_computation.11 | async-start | bytes 2621440 | tf_op jit(solution)/shard_map/reduce_scatter | solution.py:258
  442.9 132.9 %reduce-scatter.11.cloned.1.call-start = ((), (), s32[]{:S(2)}) async-start(), calls=%async_computation.9 | async-start | bytes 5242880 | tf_op jit(solution)/shard_map/reduce_scatter | solution.py:235
  457.9 140.9 %reduce-scatter.13.cloned.1.call-start = ((), (), s32[]{:S(2)}) async-start(), calls=%async_computation.10 | async-start | bytes 5242880 | tf_op jit(solution)/shard_map/reduce_scatter | solution.py:235
  457.9 7.4 copy-start.7
  473.1 181.1 %reduce-scatter.9.cloned.1.call-start = ((), (), s32[]{:S(2)}) async-start(), calls=%async_computation.8 | async-start | bytes 5242880 | tf_op jit(solution)/shard_map/reduce_scatter | solution.py:229
  483.3 226.5 %reduce-scatter.7.cloned.1.call-start = ((), (), s32[]{:S(2)}) async-start(), calls=%async_computation.7 | async-start | bytes 5242880 | tf_op jit(solution)/shard_map/reduce_scatter | solution.py:229
  493.7 287.3 %all-reduce.3.cloned.1.call-start = ((), (), s32[]{:S(2)}) async-start(), calls=%async_computation.17 | async-start | bytes 4718592 | tf_op jit(solution)/shard_map/psum | solution.py:260
  575.8 134.0 %copy-start.19 = (bf16[512,1024]{1,0:T(8,128)(2,1)S(1)}, bf16[512,1024]{1,0:T(8,128)(2,1)}, u32[]{:S(2)}) copy-start(bf16[512,1024]{1,0:T(8,128)(2,1)} %reduce-scatter.11.cloned.1.call-done) | copy-start | bytes 3145732
  715.1 75.6 %copy-start.1 = (bf16[1024,128]{1,0:T(8,128)(2,1)S(1)}, bf16[1024,128]{1,0:T(8,128)(2,1)}, u32[]{:S(2)}) copy-start(bf16[1024,128]{1,0:T(8,128)(2,1)} %param.30) | copy-start | bytes 786436
  781.0 9.0 %copy-start.39 = (f32[2,32,1024]{2,1,0:T(8,128)S(1)}, f32[2,32,1024]{2,1,0:T(8,128)}, u32[]{:S(2)}) copy-start(f32[2,32,1024]{2,1,0:T(8,128)} %get-tuple-element.132) | copy-start | bytes 786436
  (37 other events, 160.7 us)
Sparse Core Ops, SparseCore 0:
  9.9 30.6 all-gather.9
  42.4 52.5 all-gather.15
  96.8 52.5 all-gather.11
  151.1 52.5 all-gather.17
  205.4 52.5 all-gather.13
  420.1 27.8 reduce-scatter.16
  451.0 35.1 reduce-scatter.14
  489.2 53.9 reduce-scatter.10
  546.1 52.5 reduce-scatter.12
  601.6 52.5 reduce-scatter.8
  657.2 52.5 reduce-scatter.6
  713.7 67.2 all-reduce.2

commit v2 on v1

--- a/solution.py
+++ b/solution.py
@@ -25,8 +25,7 @@
 
 def attention_kernel(heads, lo_ref, lin_ref, g_ref, cos_ref, sin_ref, segq_ref, segk_ref,
                      ctx_ref, dlin_ref, qt, kt, vt, kn, vn, qz, acc, s_scr, e_scr):
-    width = heads * HEAD
-    length = lin_ref.shape[1]
+    length = lin_ref.shape[2]
     blocks = length // TILE
 
     def rotate(z, cos, sin):
@@ -38,9 +37,9 @@
         cos, sin = cos_ref[:, cols], sin_ref[:, cols]
         for h in range(heads):
             rows = pl.ds(h * HEAD, HEAD)
-            q = rotate(lin_ref[pl.ds(h * HEAD, HEAD), cols], cos, sin).astype(BF).astype(F32) * 0.125
-            k = rotate(lin_ref[pl.ds(width + h * HEAD, HEAD), cols], cos, sin)
-            v = lin_ref[pl.ds(2 * width + h * HEAD, HEAD), cols]
+            q = rotate(lin_ref[0, pl.ds(h * HEAD, HEAD), cols], cos, sin).astype(BF).astype(F32) * 0.125
+            k = rotate(lin_ref[1, pl.ds(h * HEAD, HEAD), cols], cos, sin)
+            v = lin_ref[2, pl.ds(h * HEAD, HEAD), cols]
             qt[rows, cols] = q.astype(BF)
             kt[rows, cols] = k.astype(BF)
             vt[rows, cols] = v.astype(BF)
@@ -117,7 +116,7 @@
                             tuple(jnp.zeros((HEAD, TILE), F32) for _ in range(heads)))
         cos, sin = cos_ref[:, qcols], sin_ref[:, qcols]
         for h in range(heads):
-            dlin_ref[pl.ds(h * HEAD, HEAD), qcols] = rotate(dqs[h] * 0.125, cos, -sin).astype(BF)
+            dlin_ref[0, pl.ds(h * HEAD, HEAD), qcols] = rotate(dqs[h] * 0.125, cos, -sin).astype(BF)
         return carry
 
     lax.fori_loop(0, blocks, query_block, 0)
@@ -127,8 +126,8 @@
         cos, sin = cos_ref[:, cols], sin_ref[:, cols]
         for h in range(heads):
             both = jnp.transpose(acc[h, cols, :])
-            dlin_ref[pl.ds(width + h * HEAD, HEAD), cols] = rotate(both[HEAD:], cos, -sin).astype(BF)
-            dlin_ref[pl.ds(2 * width + h * HEAD, HEAD), cols] = both[:HEAD].astype(BF)
+            dlin_ref[1, pl.ds(h * HEAD, HEAD), cols] = rotate(both[HEAD:], cos, -sin).astype(BF)
+            dlin_ref[2, pl.ds(h * HEAD, HEAD), cols] = both[:HEAD].astype(BF)
         return carry
 
     lax.fori_loop(0, blocks, finish, 0)
@@ -136,23 +135,27 @@
 
 def attention(lin, g, cos, sin, segment, keep):
     width, length = g.shape
-    heads = width // HEAD
+    heads = min(4, width // HEAD)
+    wide = heads * HEAD
     starts = jnp.sum(segment[None, :] < jnp.arange(N_DOCS, dtype=jnp.int32)[:, None], axis=1)
     firsts = segment[::TILE]
     lo = jnp.sum(jnp.where(firsts[:, None] == jnp.arange(N_DOCS)[None, :], starts[None, :], 0), axis=1)
     lo = (lo // TILE).astype(jnp.int32)
     segk = jnp.where(keep == 1, segment, -1)[:, None]
     vmem = pl.BlockSpec(memory_space=pltpu.VMEM)
+    three = pl.BlockSpec((3, wide, length), lambda i, lo: (0, i, 0))
+    single = pl.BlockSpec((wide, length), lambda i, lo: (i, 0))
     return pl.pallas_call(
         functools.partial(attention_kernel, heads),
         grid_spec=pltpu.PrefetchScalarGridSpec(
             num_scalar_prefetch=1,
-            in_specs=[vmem] * 6,
-            out_specs=[vmem] * 2,
+            grid=(width // wide,),
+            in_specs=[three, single] + [vmem] * 4,
+            out_specs=[single, three],
             scratch_shapes=[
-                pltpu.VMEM((width, length), BF),
-                pltpu.VMEM((width, length), BF),
-                pltpu.VMEM((width, length), BF),
+                pltpu.VMEM((wide, length), BF),
+                pltpu.VMEM((wide, length), BF),
+                pltpu.VMEM((wide, length), BF),
                 pltpu.VMEM((heads, length, HEAD), BF),
                 pltpu.VMEM((heads, length, HEAD), BF),
                 pltpu.VMEM((heads, length, 2 * HEAD), BF),
@@ -160,11 +163,11 @@
                 pltpu.VMEM((heads, SLOTS, TILE, TILE), F32),
                 pltpu.VMEM((heads, SLOTS, TILE, TILE), BF),
             ]),
-        out_shape=[jax.ShapeDtypeStruct((width, length), BF), jax.ShapeDtypeStruct((3 * width, length), BF)],
+        out_shape=[jax.ShapeDtypeStruct((width, length), BF), jax.ShapeDtypeStruct((3, width, length), BF)],
         compiler_params=pltpu.CompilerParams(vmem_limit_bytes=60 << 20),
         name="attention",
-        cost_estimate=pl.CostEstimate(flops=20 * heads * length * 768 * 64, transcendentals=heads * length * 768,
-                                      bytes_accessed=13 * width * length * 2),
+        cost_estimate=pl.CostEstimate(flops=10 * width * length * 768, transcendentals=width * length * 12,
+                                      bytes_accessed=26 * width * length),
     )(lo, lin, g, cos, sin, segment[None, :], segk)
 
 
@@ -187,7 +190,7 @@
     return centered * inverse, inverse
 
 
-def on_device(x, gy, segment, keep, gain, bias, w_qkv, w_out, w_up, w_down,
+def by_features(x, gy, segment, keep, gain, bias, w_qkv, w_out, w_up, w_down,
               a_in, b_qkv, b_up, a_out, a_down, b_out):
     width = w_qkv.shape[2]
     micro = x.shape[0]
@@ -217,7 +220,8 @@
         g_ctx = dot(m_out, gg, 1, 1).astype(BF)
         low_grad = (SCALE * dot(gg, b_both, 1, 1)).astype(BF)
         cos, sin = rotary_tables(seg)
-        ctx, d_lin = attention(lin, g_ctx, cos, sin, seg, keep[m, 0])
+        ctx, d_lin = attention(lin.reshape(3, width, -1), g_ctx, cos, sin, seg, keep[m, 0])
+        d_lin = d_lin.reshape(3 * width, -1)
 
         pre = dot(n2, m_up, 1, 0)
         cdf = 0.5 * (1.0 + lax.erf(pre * math.sqrt(0.5)))
@@ -263,6 +267,465 @@
     return (jnp.stack(outs)[:, None], jnp.stack(grads)[:, None], norms[:2], norms[2:],
             jnp.transpose(d_a_in, (1, 2, 0)), d_b_qkv, d_b_up, d_a_out, d_a_down,
             jnp.transpose(d_b_out, (1, 0, 2)))
+
+
+RANK = 128
+
+
+MESH = pl.DeviceIdType.MESH
+
+
+def place():
+    d = lax.axis_index("dp")
+    return d // 2, d % 2, lax.axis_index("tensor")
+
+
+def meet(z, c, t):
+    barrier = pltpu.get_barrier_semaphore()
+    for h in (0, 1):
+        for k in range(4):
+            if h or k:
+                pl.semaphore_signal(barrier, 1, device_id=(2 * z + (c ^ h), t ^ k), device_id_type=MESH)
+    pl.semaphore_wait(barrier, 7)
+
+
+def remote(src, dst, send_sem, recv_sem, device):
+    return pltpu.make_async_remote_copy(src_ref=src, dst_ref=dst, send_sem=send_sem, recv_sem=recv_sem,
+                                        device_id=device, device_id_type=MESH)
+
+
+class Rows:
+    def __init__(self, v, full, sems, stage, local, z, c, t):
+        self.v, self.full, self.sems, self.stage, self.local = v, full, sems, stage, local
+        self.z, self.c, self.t = z, c, t
+
+    def rows(self, s, h):
+        return self.full.at[pl.ds(pl.multiple_of(s * 512 + h * 256, 256), 256)]
+
+    def block(self, m, h):
+        return self.v.at[m, pl.ds(pl.multiple_of(h * 256, 256), 256)]
+
+    def copy(self, m, other):
+        h = self.c ^ other
+        return remote(self.block(m, h), self.rows(self.t, h), self.sems.at[2 * m + other], self.sems.at[4 + self.t],
+                      (2 * self.z + h, 2 * m + self.c))
+
+    def forward(self, s):
+        part = self.rows(s, self.c)
+        return remote(part, part, self.sems.at[8 + s], self.sems.at[12 + s], (2 * self.z + (self.c ^ 1), self.t))
+
+    def start(self):
+        for m in (0, 1):
+            away = 2 * m + self.c != self.t
+
+            @pl.when(away)
+            def _():
+                self.copy(m, 0).start()
+
+            self.copy(m, 1).start()
+
+            @pl.when(jnp.logical_not(away))
+            def _():
+                pltpu.make_async_copy(self.block(m, self.c), self.stage, self.local.at[0]).start()
+
+    def relay(self):
+        mine = self.t % 2 == self.c
+
+        @pl.when(mine)
+        def _():
+            pltpu.make_async_copy(self.block(0, self.c), self.stage, self.local.at[0]).wait()
+            pltpu.make_async_copy(self.stage, self.rows(self.t, self.c), self.sems.at[4 + self.t]).start()
+
+        for k in (0, 1, 2, 3):
+            s = self.t ^ k
+            pltpu.make_async_copy(self.stage, self.rows(s, self.c), self.sems.at[4 + s]).wait()
+            self.forward(s).start()
+
+    def finish(self):
+        for s in range(4):
+            part = self.rows(s, self.c ^ 1)
+            remote(part, part, self.sems.at[8 + s], self.sems.at[12 + s], (2 * self.z + (self.c ^ 1), self.t)).wait_recv()
+            self.forward(s).wait_send()
+        for m in (0, 1):
+            @pl.when(2 * m + self.c != self.t)
+            def _():
+                self.copy(m, 0).wait_send()
+
+            self.copy(m, 1).wait_send()
+
+
+class Blocks:
+    def __init__(self, own, where, sems, stage, local, halves, z, c, t):
+        self.own, self.where, self.sems, self.stage, self.local = own, where, sems, stage, local
+        self.halves, self.t, self.d = halves, t, 2 * z + c
+
+    def first(self, k):
+        return remote(self.own, self.where(self.t), self.sems.at[k - 1], self.sems.at[3 + k - 1], (self.d, self.t ^ k))
+
+    def arrival(self, k):
+        spot = self.where(self.t ^ k)
+        return remote(spot, spot, self.sems.at[k - 1], self.sems.at[3 + k - 1], (self.d, self.t ^ k))
+
+    def second(self, k):
+        part = self.halves(self.where(self.t ^ (3 - k)), k - 1)
+        return remote(part, part, self.sems.at[6 + k - 1], self.sems.at[8 + k - 1], (self.d, self.t ^ k))
+
+    def start(self):
+        for k in ((1, 2) if self.halves else (1, 2, 3)):
+            self.first(k).start()
+        pltpu.make_async_copy(self.own, self.stage, self.local.at[0]).start()
+
+    def store(self):
+        pltpu.make_async_copy(self.own, self.stage, self.local.at[0]).wait()
+        pltpu.make_async_copy(self.stage, self.where(self.t), self.local.at[1]).start()
+
+    def relay(self):
+        if self.halves:
+            for k in (1, 2):
+                self.arrival(3 - k).wait_recv()
+                self.second(k).start()
+
+    def finish(self):
+        pltpu.make_async_copy(self.stage, self.where(self.t), self.local.at[1]).wait()
+        if self.halves:
+            for k in (1, 2):
+                part = self.halves(self.where(self.t ^ 3), k - 1)
+                remote(part, part, self.sems.at[6 + k - 1], self.sems.at[8 + k - 1], (self.d, self.t ^ k)).wait_recv()
+                self.first(k).wait_send()
+                self.second(k).wait_send()
+        else:
+            for k in (1, 2, 3):
+                self.arrival(k).wait_recv()
+                self.first(k).wait_send()
+
+
+def aligned(i, n):
+    return pl.ds(pl.multiple_of(i * n, n), n)
+
+
+def front_kernel(x, g, wq, wo, ain, bq, ao, bo,
+                 xf, gf, wqf, wof, ainf, bqf, aof, bof,
+                 row_sems, sems, local, xs, gs, wqs, wos, ains, bqs, aos, bos):
+    z, c, t = place()
+    meet(z, c, t)
+    at = dict(z=z, c=c, t=t)
+    x_rows = Rows(x, xf, row_sems.at[0], xs, local.at[0], **at)
+    g_rows = Rows(g, gf, row_sems.at[1], gs, local.at[1], **at)
+    qkv = Blocks(wq.at[:, :, aligned(c, 128)], lambda i: wqf.at[:, :, aligned(i, 128)], sems.at[0], wqs, local.at[2],
+                 lambda v, h: v.at[:, pl.ds(h * 512, 512)], **at)
+    into = Blocks(ain, lambda i: ainf.at[:, aligned(i, 32)], sems.at[1], ains, local.at[3], None, **at)
+    second = Blocks(bq.at[:, :, aligned(c, 128)], lambda i: bqf.at[:, :, aligned(i, 128)], sems.at[2], bqs, local.at[4],
+                    None, **at)
+    out = Blocks(wo.at[aligned(c, 128)], lambda i: wof.at[aligned(i, 128)], sems.at[3], wos, local.at[5],
+                 lambda v, h: v.at[pl.ds(h * 64, 64)], **at)
+    a_out = Blocks(ao.at[aligned(c, 128)], lambda i: aof.at[aligned(i, 128)], sems.at[4], aos, local.at[6], None, **at)
+    b_out = Blocks(bo, lambda i: bof.at[:, aligned(i, 32)], sems.at[5], bos, local.at[7], None, **at)
+    x_rows.start()
+    into.start()
+    second.start()
+    qkv.start()
+    x_rows.relay()
+    for v in (into, second, qkv):
+        v.store()
+    g_rows.start()
+    qkv.relay()
+    for v in (b_out, a_out, out):
+        v.start()
+    g_rows.relay()
+    for v in (b_out, a_out, out):
+        v.store()
+    out.relay()
+    for v in (x_rows, into, second, qkv, g_rows, b_out, a_out, out):
+        v.finish()
+
+
+def front(x, g, wq, wo, ain, bq, ao, bo):
+    shapes = [(2048, 1024), (2048, 1024), (3, 1024, 512), (512, 1024), (4, 128, 1024), (3, 128, 512), (512, 128),
+              (2, 128, 1024)]
+    anywhere = pl.BlockSpec(memory_space=pl.ANY)
+    return pl.pallas_call(
+        front_kernel,
+        in_specs=[anywhere] * 8,
+        out_specs=[anywhere] * 8,
+        out_shape=[jax.ShapeDtypeStruct(s, BF) for s in shapes],
+        scratch_shapes=[
+            pltpu.SemaphoreType.DMA((2, 16)),
+            pltpu.SemaphoreType.DMA((6, 10)),
+            pltpu.SemaphoreType.DMA((8, 2)),
+            pltpu.VMEM((256, 1024), BF),
+            pltpu.VMEM((256, 1024), BF),
+            pltpu.VMEM((3, 1024, 128), BF),
+            pltpu.VMEM((128, 1024), BF),
+            pltpu.VMEM((4, 32, 1024), BF),
+            pltpu.VMEM((3, 128, 128), BF),
+            pltpu.VMEM((128, 128), BF),
+            pltpu.VMEM((2, 32, 1024), BF),
+        ],
+        compiler_params=pltpu.CompilerParams(collective_id=0, has_side_effects=True),
+        name="front",
+    )(x, g, wq, wo, ain, bq, ao, bo)
+
+
+def back_kernel(rows, dbq, dbu, dao, dad, dsh, dno,
+                out, obq, obu, oao, oad, osh, ono,
+                row_sems, share_sems, cross_sems, z_sems, last_sems, norm_sems,
+                sh_in, sh, rbq, rbu, rao, rad, rsh, pbq, pbu, pao, pad, psh, qbq, qbu, qao, qad, qsh, no_in, no_sum):
+    z, c, t = place()
+    meet_all(z, c, t)
+    d = 2 * z + c
+    sibling = (2 * z + (c ^ 1), t)
+
+    home = t % 2
+    local = home == c
+    spot = aligned(c, 256)
+
+    def row(k):
+        return remote(rows.at[t ^ k], out.at[t // 2, spot], row_sems.at[k], row_sems.at[4 + (t // 2) * 2 + c],
+                      (2 * z + home, t ^ k))
+
+    def own_row():
+        return pltpu.make_async_copy(rows.at[t], out.at[t // 2, spot], row_sems.at[4 + (t // 2) * 2 + c])
+
+    @pl.when(local)
+    def _():
+        own_row().start()
+
+    @pl.when(jnp.logical_not(local))
+    def _():
+        row(0).start()
+
+    for k in (1, 2, 3):
+        row(k).start()
+
+    peers = (sibling, (d, t ^ 1), (d, t ^ 2), (d ^ 2, t), (d ^ 4, t))
+
+    def norm(i):
+        return remote(dno if i == 0 else no_sum.at[i - 1], no_in.at[i], norm_sems.at[0, i], norm_sems.at[1, i], peers[i])
+
+    def norm_next(i):
+        norm(i).wait_recv()
+        total = (dno[...] if i == 0 else no_sum[i - 1]) + no_in[i]
+        if i < 4:
+            no_sum[i] = total
+            norm(i + 1).start()
+        else:
+            ono[...] = total
+
+    norm(0).start()
+
+    def share():
+        return remote(dsh.at[:, :, aligned(c ^ 1, 512)], sh_in, share_sems.at[0], share_sems.at[1], sibling)
+
+    share().start()
+    share().wait_recv()
+    norm_next(0)
+    for i in range(6):
+        sh[i] = (dsh[i, :, aligned(c, 512)].astype(F32) + sh_in[i].astype(F32)).astype(BF)
+
+    def parts(j):
+        return (dbq.at[:, :, aligned(j, 128)], dbu.at[:, aligned(j, 512)], dao.at[aligned(j, 128)],
+                dad.at[aligned(j, 512)], sh.at[:, aligned(j, 32)])
+
+    got = (rbq, rbu, rao, rad, rsh)
+
+    def cross(k, i):
+        return remote(parts(t ^ k)[i], got[i].at[k - 1], cross_sems.at[0, k - 1, i], cross_sems.at[1, k - 1, i], (d, t ^ k))
+
+    for k in (1, 2, 3):
+        for i in range(5):
+            cross(k, i).start()
+    norm_next(1)
+    norm_next(2)
+    sums = (pbq, pbu, pao, pad, psh)
+    for i in range(5):
+        for k in (1, 2, 3):
+            cross(k, i).wait_recv()
+        total = parts(t)[i][...].astype(F32)
+        for k in (0, 1, 2):
+            total = total + got[i][k].astype(F32)
+        sums[i][0] = total.astype(BF)
+
+    halves = (qbq, qbu, qao, qad, qsh)
+
+    def along(step, i):
+        return remote(sums[i].at[step], halves[i].at[step], z_sems.at[0, step, i], z_sems.at[1, step, i],
+                      (d ^ (2 << step), t))
+
+    for i in range(5):
+        along(0, i).start()
+    norm_next(3)
+    for i in range(5):
+        along(0, i).wait_recv()
+        sums[i][1] = (sums[i][0].astype(F32) + halves[i][0].astype(F32)).astype(BF)
+        along(1, i).start()
+    norm_next(4)
+    result = (obq.at[:, :, aligned(c, 128)], obu.at[:, aligned(c, 512)], oao.at[aligned(c, 128)],
+              oad.at[aligned(c, 512)], osh.at[:, :, aligned(c, 512)])
+    theirs = (obq.at[:, :, aligned(c ^ 1, 128)], obu.at[:, aligned(c ^ 1, 512)], oao.at[aligned(c ^ 1, 128)],
+              oad.at[aligned(c ^ 1, 512)], osh.at[:, :, aligned(c ^ 1, 512)])
+
+    def last(i):
+        return remote(result[i], result[i], last_sems.at[0, i], last_sems.at[1, i], sibling)
+
+    for i in range(5):
+        along(1, i).wait_recv()
+        result[i][...] = sums[i][1].astype(F32) + halves[i][1].astype(F32)
+        last(i).start()
+
+    for i in range(5):
+        remote(theirs[i], theirs[i], last_sems.at[0, i], last_sems.at[1, i], sibling).wait_recv()
+        last(i).wait_send()
+        along(0, i).wait_send()
+        along(1, i).wait_send()
+        for k in (1, 2, 3):
+            cross(k, i).wait_send()
+    share().wait_send()
+    for i in range(5):
+        norm(i).wait_send()
+    for k in (1, 2, 3):
+        row(k).wait_send()
+
+    @pl.when(jnp.logical_not(local))
+    def _():
+        row(0).wait_send()
+
+    for m in (0, 1):
+        for h in (0, 1):
+            pltpu.make_async_copy(rows.at[0], out.at[m, pl.ds(256 * h, 256)], row_sems.at[4 + 2 * m + h]).wait()
+
+
+def meet_all(z, c, t):
+    barrier = pltpu.get_barrier_semaphore()
+    for h in (0, 1):
+        for k in range(4):
+            if h or k:
+                pl.semaphore_signal(barrier, 1, device_id=(2 * z + (c ^ h), t ^ k), device_id_type=MESH)
+    for k in (1, 2):
+        pl.semaphore_signal(barrier, 1, device_id=(2 * (z ^ k) + c, t), device_id_type=MESH)
+    pl.semaphore_wait(barrier, 9)
+
+
+def back(rows, dbq, dbu, dao, dad, dsh, dno):
+    vmem = pl.BlockSpec(memory_space=pltpu.VMEM)
+    part = [(3, 128, 128), (128, 512), (128, 128), (512, 128), (6, 32, 512)]
+    outs = [((2, 512, 1024), BF), ((3, 128, 256), F32), ((128, 1024), F32), ((256, 128), F32), ((1024, 128), F32),
+            ((6, 32, 1024), F32), ((4, 1024), F32)]
+    return pl.pallas_call(
+        back_kernel,
+        in_specs=[vmem] * 7,
+        out_specs=[pl.BlockSpec(memory_space=pl.ANY)] + [vmem] * 6,
+        out_shape=[jax.ShapeDtypeStruct(s, d) for s, d in outs],
+        scratch_shapes=[
+            pltpu.SemaphoreType.DMA((8,)),
+            pltpu.SemaphoreType.DMA((2,)),
+            pltpu.SemaphoreType.DMA((2, 3, 5)),
+            pltpu.SemaphoreType.DMA((2, 2, 5)),
+            pltpu.SemaphoreType.DMA((2, 5)),
+            pltpu.SemaphoreType.DMA((2, 5)),
+            pltpu.VMEM((6, 128, 512), BF),
+            pltpu.VMEM((6, 128, 512), BF),
+        ] + [pltpu.VMEM((3,) + s, BF) for s in part] + [pltpu.VMEM((2,) + s, BF) for s in part + part] + [
+            pltpu.VMEM((5, 4, 1024), F32),
+            pltpu.VMEM((4, 4, 1024), F32),
+        ],
+        compiler_params=pltpu.CompilerParams(collective_id=1, has_side_effects=True),
+        name="back",
+    )(rows, dbq, dbu, dao, dad, dsh, dno)
+
+
+def swap(v, k=1):
+    return lax.ppermute(v, "dp", [(i, i ^ k) for i in range(lax.axis_size("dp"))])
+
+
+def pick(v, axis, index, size):
+    return lax.dynamic_slice_in_dim(v, index * size, size, axis)
+
+
+def half_rows(v, c):
+    return pick(v.reshape(4, 2, 256, -1), 1, c, 1)[:, 0]
+
+
+def from_group(own, c):
+    got = lax.all_to_all(own, "tensor", 0, 0, tiled=True).reshape(2, 2, 256, -1)
+    mine = pick(got, 1, c, 1)[:, 0]
+    other = swap(pick(got, 1, 1 - c, 1)[:, 0])
+    return jnp.where(c == 0, jnp.stack([mine, other], 1), jnp.stack([other, mine], 1)).reshape(2, 512, -1)
+
+
+def by_groups(x, gy, segment, keep, gain, bias, w_qkv, w_out, w_up, w_down,
+              a_in, b_qkv, b_up, a_out, a_down, b_out):
+    z, c, t = place()
+    tables = jnp.stack([segment[:, 0], keep[:, 0]], 1)
+    pair = jnp.where(t % 2 == c, tables, swap(tables))
+    seg, kept = jnp.where(t // 2 == 0, pair[0], pair[1])
+
+    x_full, g_full, qkv, out, a_full, b_qkv_all, a_out_all, b_full = front(
+        x[:, 0], gy[:, 0], w_qkv, w_out, jnp.swapaxes(a_in, 1, 2), b_qkv, a_out, b_out)
+    up, down = lax.optimization_barrier((
+        jnp.concatenate([pick(w_up, 1, c, 512), pick(b_up, 1, c, 512)], axis=0),
+        jnp.concatenate([pick(w_down, 0, c, 512), pick(a_down, 0, c, 512)], axis=1), x_full))[:2]
+    up = lax.all_gather(up, "tensor", axis=0)
+    down = lax.all_gather(down, "tensor", axis=0, tiled=True)
+    w_up_all = jnp.concatenate([up[i, :1024] for i in range(4)], axis=1)
+    b_up_all = jnp.concatenate([up[i, 1024:] for i in range(4)], axis=1)
+    w_down_all, a_down_all = down[:, :1024], down[:, 1024:]
+
+    m_qkv = (qkv.astype(F32) + SCALE * jnp.einsum("nrk,nrc->nkc", a_full[:3], b_qkv_all,
+                                                  preferred_element_type=F32)).astype(BF)
+    m_up = (w_up_all.astype(F32) + SCALE * dot(a_full[3], b_up_all, 0, 0)).astype(BF)
+    m_out = (out.astype(F32) + SCALE * dot(a_out_all, b_full[0], 1, 0)).astype(BF)
+    m_down = (w_down_all.astype(F32) + SCALE * dot(a_down_all, b_full[1], 1, 0)).astype(BF)
+    a_three = a_full[:3].reshape(3 * RANK, 1024)
+    b_both = b_full.reshape(2 * RANK, 1024)
+
+    standard, inverse = normalized(x_full.astype(F32))
+    n1 = (standard * gain[0] + bias[0]).astype(BF)
+    n2 = (standard * gain[1] + bias[1]).astype(BF)
+    lin = jnp.einsum("nkc,sk->ncs", m_qkv, n1, preferred_element_type=F32)
+    low3 = dot(n1, a_three, 1, 1).astype(BF)
+    low1 = dot(n2, a_full[3], 1, 1).astype(BF)
+    g_ctx = dot(m_out, g_full, 1, 1).astype(BF)
+    low_grad = (SCALE * dot(g_full, b_both, 1, 1)).astype(BF)
+    cos, sin = rotary_tables(seg)
+    ctx, d_lin = attention(lin, g_ctx, cos, sin, seg, kept)
+
+    pre = dot(n2, m_up, 1, 0)
+    cdf = 0.5 * (1.0 + lax.erf(pre * math.sqrt(0.5)))
+    hidden = (pre * cdf).astype(BF)
+    slope = cdf + pre * (math.sqrt(0.5 / math.pi) * jnp.exp(-0.5 * pre * pre))
+    d_pre = (dot(g_full, m_down, 1, 1) * slope).astype(BF)
+
+    part = dot(ctx, m_out, 0, 0) + dot(hidden, m_down, 1, 0)
+    theirs = swap(half_rows(part, 1 - c).astype(BF))
+    y = half_rows(x_full, c).astype(F32) + half_rows(part, c) + theirs.astype(F32)
+    y = from_group(y.astype(BF), c)
+
+    one = jnp.einsum("ncs,nkc->sk", d_lin, m_qkv, preferred_element_type=F32)
+    two = dot(d_pre, m_up, 1, 1)
+    total = gain[0] * one + gain[1] * two
+    theirs = swap(half_rows(total, 1 - c).astype(BF))
+    total = half_rows(total, c) + theirs.astype(F32)
+    own = half_rows(standard, c)
+    grad = total - jnp.mean(total, axis=-1, keepdims=True)
+    grad = grad - own * jnp.mean(total * own, axis=-1, keepdims=True)
+    grad = half_rows(g_full, c).astype(F32) + grad * half_rows(inverse, c)
+
+    norms = jnp.stack([jnp.sum(one * standard, axis=0), jnp.sum(two * standard, axis=0),
+                       jnp.sum(one, axis=0), jnp.sum(two, axis=0)])
+    lo_ctx = dot(ctx, a_out_all, 0, 0).astype(BF)
+    lo_hid = dot(hidden, a_down_all, 1, 0).astype(BF)
+    d_a_out = dot(ctx, low_grad[:, :RANK], 1, 0).astype(BF)
+    d_a_down = dot(hidden, low_grad[:, RANK:], 0, 0).astype(BF)
+    d_b_qkv = jnp.stack([(SCALE * dot(low3[:, RANK * i:RANK * (i + 1)], d_lin[i], 0, 1)).astype(BF) for i in range(3)])
+    d_b_up = (SCALE * dot(low1, d_pre, 0, 0)).astype(BF)
+    back3 = [(SCALE * dot(d_lin[i], b_qkv_all[i], 0, 1)).astype(BF) for i in range(3)]
+    back1 = (SCALE * dot(d_pre, b_up_all, 1, 1)).astype(BF)
+    shared = jnp.stack([dot(v, n1, 0, 0).astype(BF) for v in back3] + [dot(back1, n2, 0, 0).astype(BF)]
+                       + [(SCALE * dot(v, g_full, 0, 0)).astype(BF) for v in (lo_ctx, lo_hid)])
+    grad, r_b_qkv, r_b_up, r_a_out, r_a_down, rest, norms = back(
+        grad.astype(BF), d_b_qkv, d_b_up, d_a_out, d_a_down, shared, norms)
+    r_a_in = jnp.swapaxes(rest[:4], 1, 2)
+    return (y[:, None], grad[:, None], norms[:2], norms[2:], r_a_in, r_b_qkv, r_b_up, r_a_out, r_a_down, rest[4:])
 
 
 def solution(mesh):
@@ -296,6 +759,7 @@
         P("tensor", None),
         P(None, "tensor", None),
     )
+    small = mesh.shape["tensor"] == 4 and mesh.shape["dp"] == 8
     return jax.shard_map(
-        on_device, mesh=mesh, in_specs=in_specs, out_specs=out_specs, check_vma=False
+        by_groups if small else by_features, mesh=mesh, in_specs=in_specs, out_specs=out_specs, check_vma=False
     )

time: 805 us -> 571 us (0.71)
  waiting for transfers between devices: 340 us -> 6.11 us
  Pallas kernels: 96.1 us -> 290 us
  blocking collectives: 54.9 us -> 0 us
  matrix products: 223 us -> 175 us
  local copies, waits for them, and re-layouts: 26.7 us -> 37.6 us
    pallas_call x0 -> x2, Pallas kernels: none -> 203 us  [the longest x1 110 us: front(): pl.pallas_call(front_kernel, in_specs=[anywhere] * 8, out_specs=[anywhere...]
    all_gather x5 -> x2, waiting for transfers between devices: 144 us -> 0.01 us  [the longest x1 0.01 us: by_groups(): up = lax.all_gather(up, 'tensor', axis=0)]
    reduce_scatter x6 -> x0, waiting for transfers between devices: 129 us -> none  [the longest x2 109 us: on_device(): lax.psum_scatter(part.astype(BF), 'tensor', scatter_dimension=0, tiled=True)]
    dot_general x50 -> x23, matrix products: 223 us -> 147 us  [dot(): lax.dot_general(a, b, (((ca,), (cb,)), ((), ())), preferred_element_type=...]
    psum x1 -> x0, waiting for transfers between devices: 64.4 us -> none  [on_device(): lax.psum((d_a_in, d_b_qkv, d_b_up, d_a_out, d_a_down, d_b_out), 'dp')]
    psum x1 -> x0, blocking collectives: 41.8 us -> none  [on_device(): norms = lax.psum(norms, ('dp', 'tensor'))]
    dot_general x0 -> x3, matrix products: none -> 28.2 us  [the longest x1 17.6 us: by_groups(): one = jnp.einsum('ncs,nkc->sk', d_lin, m_qkv, preferred_element_type=F32)]
    all_gather x1 -> x0, blocking collectives: 13.2 us -> none  [on_device(): b_full = lax.all_gather(b_out, 'tensor', axis=1, tiled=True)]
  transfers between devices with their start and end apart: 12 -> 7, of which waited for: 7 -> 1; matrix products, arithmetic and copies ran while one was open for 25% -> 26% of each run, Pallas kernels for 6% -> 32%
where the time goes in v2:
time: 571 us; the launch traced here: 565 us
  Pallas kernels  290 us (51%)
  matrix products  175 us (31%)
  local copies, waits for them, and re-layouts  37.6 us (7%)
  other arithmetic  33.8 us (6%)
  between operations  15 us (3%)
  starting transfers between devices  7.87 us (1%)
  waiting for transfers between devices  6.11 us (1%)
    dot_general x23, matrix products, dot(): lax.dot_general(a, b, (((ca,), (cb,)), ((), ())), preferred_element_type=...  147 us
    pallas_call x1, Pallas kernels, front(): pl.pallas_call(front_kernel, in_specs=[anywhere] * 8, out_specs=[anywhere...  110 us
    pallas_call x1, Pallas kernels, back(): pl.pallas_call(back_kernel, in_specs=[vmem] * 7, out_specs=[pl.BlockSpec(...  93.3 us
    pallas_call x1, Pallas kernels, attention(): pl.pallas_call(functools.partial(attention_kernel, heads), grid_spec=pltp...  86.8 us
    dot_general x1, matrix products, by_groups(): one = jnp.einsum('ncs,nkc->sk', d_lin, m_qkv, preferred_element_type=F32)  17.6 us
    unnamed x104, local copies, waits for them, and re-layouts  13.5 us
  transfers between devices with their start and end apart: 7, of which 1 were waited for; matrix products, arithmetic and copies ran while one was open for 26% of the time, Pallas kernels for 32%

profile of v2, /device:TPU:0, one launch (start us, length us, event | category | flops | bytes accessed | tf_op | source)
XLA Modules:
  0.0 565.2 jit_solution(10693506580139411525)
XLA Ops:
  12.9 109.8 %front.1 = (bf16[2048,1024]{1,0:T(8,128)(2,1)}, bf16[2048,1024]{1,0:T(8,128)(2,1)}, bf16[3,1024,512]{2,1,0:T(8,128)(2,1)}, bf16[512,1024]{1,0:T(8,128)(2,1)}, bf...) custom-call(bf16[2,512,1024]{2,1,0:T(8,128)(2,1)} %bitcast.248, ...), custom_call_target="tpu_custom_call" | custom-call | tf_op jit(solution)/shard_map/front/pallas_call | solution.py:446
  130.1 5.6 fusion.19
  147.9 9.4 %fusion.17.lin_ref = f32[3,512,2048]{2,1,0:T(8,128)} fusion(bf16[3,1024,512]{2,1,0:T(8,128)(2,1)S(1)} %add_convert_fusion.4, bf16[2048,1024]{1,0:T(8,128)(2,1)S(1)} %get-tuple-element.96), kind=kOutput, calls=%fused_computation.37 | convolution fusion | flops 6442450944 | bytes 19922944 | tf_op jit(solution)/shard_map/nkc,sk->ncs/dot_general | solution.py:684
  162.0 86.8 %attention.1 = (bf16[512,2048]{1,0:T(8,128)(2,1)}, bf16[3,512,2048]{2,1,0:T(8,128)(2,1)}) custom-call(s32[8]{0:T(128)} %and_select_fusion.lo_ref, f32[3,512,2048]{2,1,0:T(8,128)} %fusion.17.lin_ref, bf16[512,2048]{1,0:T(8,128)(2,1)} %convolution_convert_fusion.g_ref, f32[8,2048]{1,0:T(8,128)} %get-tuple-element.106.cos_ref, ...), custom_call_target="tpu_custom_call" | custom-call | flops 8053063680 | bytes 27262976 | tf_op jit(solution)/shard_map/attention/pallas_call | solution.py:148
  258.8 5.6 fusion.45
  264.4 5.6 fusion.47
  269.9 5.6 fusion.49
  285.2 14.2 %multiply_convert_fusion = (bf16[2048,2048]{1,0:T(8,128)(2,1)}, f32[2048,2048]{1,0:T(8,128)}) fusion(bf16[2048,1024]{1,0:T(8,128)(2,1)S(1)} %copy-done.7, bf16[1024,2048]{1,0:T(8,128)(2,1)S(1)} %add_convert_fusion.1), kind=kOutput, calls=%fused_computation.7 | convolution fusion | flops 8610906112 | bytes 33554432 | tf_op jit(solution)/shard_map/dot_general | solution.py:23
  303.3 17.6 %fusion.5 = bf16[2048,2048]{1,0:T(8,128)(2,1)S(1)} fusion(f32[2048,2048]{1,0:T(8,128)} %get-tuple-element.112, bf16[2048,1024]{1,0:T(8,128)(2,1)S(1)} %copy-done.10, bf16[2048,1024]{1,0:T(8,128)(2,1)S(1)} %add_convert_fusion), kind=kOutput, calls=%fused_computation.6 | convolution fusion | flops 8631877632 | bytes 33554432 | tf_op jit(solution)/shard_map/dot_general | solution.py:23
  324.2 13.0 %fusion.136 = f32[2048,1024]{1,0:T(8,128)} fusion(bf16[2048,2048]{1,0:T(8,128)(2,1)S(1)} %fusion.5, bf16[1024,2048]{1,0:T(8,128)(2,1)} %copy-done.48), kind=kOutput, calls=%fused_computation.189 | convolution fusion | flops 8589934592 | bytes 20971520 | tf_op jit(solution)/shard_map/dot_general | solution.py:23
  337.1 17.6 %fusion.10 = (f32[1024]{0:T(1024)}, f32[1024]{0:T(1024)}, f32[1024]{0:T(1024)}, f32[1024]{0:T(1024)}, f32[2048,1024]{1,0:T(8,128)}, /*index=5*/f32[2048,1024]{1,0:T(8,128)}) fusion(bf16[2048,1024]{1,0:T(8,128)(2,1)S(1)} %copy-done.4, f32[2048]{0:T(1024)S(1)} %add_rsqrt_fusion, f32[2048]{0:T(1024)S(1)} %broadcast_multiply_fusion, f32[2048,1024]{1,0:T(8,128)} %fusion.136, ...), kind=kOutput, calls=%fused_computation.18 | convolution fusion | flops 6467612672 | bytes 38838272 | tf_op jit(solution)/shard_map/ncs,nkc->sk/dot_general | solution.py:703
  354.8 12.7 %fusion.135 = f32[2048,1024]{1,0:T(8,128)S(1)} fusion(bf16[2048,2048]{1,0:T(8,128)(2,1)} %get-tuple-element.111, bf16[2048,1024]{1,0:T(8,128)(2,1)} %copy-done.47), kind=kOutput, calls=%fused_computation.188 | convolution fusion | flops 8589934592 | bytes 20971520 | tf_op jit(solution)/shard_map/dot_general | solution.py:23
  370.1 6.9 %fusion.26 = bf16[4,256,1024]{2,1,0:T(8,128)(2,1)} fusion(f32[4,2,256,1024]{3,2,1,0:T(8,128)} %bitcast.240, s32[]{:T(128)S(6)} %select_n.112), kind=kLoop, calls=%fused_computation.59 | loop fusion | bytes 4194308 | tf_op jit(solution)/shard_map/convert_element_type | solution.py:706
  379.1 9.6 %fusion.20.dbu = bf16[128,2048]{1,0:T(8,128)(2,1)} fusion(bf16[2048,2048]{1,0:T(8,128)(2,1)} %copy-done.12, bf16[2048,1024]{1,0:T(8,128)(2,1)} %get-tuple-element.97, bf16[4,128,1024]{2,1,0:T(8,128)(2,1)S(1)} %copy-done.18), kind=kOutput, calls=%fused_computation.51 | convolution fusion | flops 1611399168 | bytes 13369344 | tf_op jit(solution)/shard_map/dot_general | solution.py:23
  388.7 9.1 %fusion.51 = bf16[6,128,1024]{2,1,0:T(8,128)(2,1)} fusion(bf16[6,128,1024]{2,1,0:T(8,128)(2,1)} %fusion.49, bf16[2048,1024]{1,0:T(8,128)(2,1)} %get-tuple-element.97, bf16[2048,2048]{1,0:T(8,128)(2,1)} %copy-done.12, bf16[128,512]{1,0:T(8,128)(2,1)S(1)} %get-tuple-element.88, bf16[128,512]{1,0:T(8,128)(2,1)S(1)} %get-tuple-element.89, ...), kind=kOutput, calls=%fused_computation.94 | convolution fusion | flops 1613365248 | bytes 13369344 | tf_op jit(solution)/shard_map/dot_general | solution.py:23
  397.8 7.0 %convolution_convert_fusion.3.dad = bf16[2048,128]{1,0:T(8,128)(2,1)} fusion(bf16[2048,2048]{1,0:T(8,128)(2,1)} %get-tuple-element.111, bf16[2048,256]{1,0:T(8,128)(2,1)S(1)} %copy-done.45), kind=kOutput, calls=%fused_computation.50 | convolution fusion | flops 1074003968 | bytes 9437184 | tf_op jit(solution)/shard_map/dot_general | solution.py:23
  404.8 5.3 fusion.16
  410.2 7.1 %all-to-all-start = ((bf16[4,256,1024]{2,1,0:T(8,128)(2,1)}), bf16[4,256,1024]{2,1,0:T(8,128)(2,1)}, u32[]{:S(2)}, u32[]{:S(2)}) async-start(bf16[4,256,1024]{2,1,0:T(8,128)(2,1)} %fusion.16), calls=%async_computation | async-start | bytes 4194304 | tf_op jit(solution)/shard_map/all_to_all | solution.py:649
  418.0 4.9 fusion.55
  422.9 9.1 %fusion.53.dsh = bf16[6,128,1024]{2,1,0:T(8,128)(2,1)} fusion(bf16[6,128,1024]{2,1,0:T(8,128)(2,1)} %fusion.55, bf16[2048,1024]{1,0:T(8,128)(2,1)} %get-tuple-element.36, bf16[2048,2048]{1,0:T(8,128)(2,1)} %get-tuple-element.111, bf16[2048,1152]{1,0:T(8,128)(2,1)} %all-gather.4.cloned.1.call-done), kind=kOutput, calls=%fused_computation.96 | convolution fusion | flops 1611137024 | bytes 13369344 | tf_op jit(solution)/shard_map/dot_general | solution.py:23
  432.1 4.9 fusion.89
  437.0 5.5 all-to-all-done
  445.3 5.7 %fusion.15.rows = bf16[4,256,1024]{2,1,0:T(8,128)(2,1)} fusion(f32[4,2,256,1024]{3,2,1,0:T(8,128)} %bitcast.245, s32[]{:T(128)S(6)} %select_n.99, f32[4,256]{1,0:T(4,128)S(1)} %bitcast.259, f32[4,256]{1,0:T(4,128)S(1)} %get-tuple-element.113, f32[4,256]{1,0:T(4,128)S(1)} %get-tuple-element.114, bf16[4,2,256,1024]{3,2,1,0:T(8,128)(2,1)S(1)} %bitcast.243, ...), kind=kLoop, calls=%fused_computation.31 | loop fusion | flops 9437184 | bytes 14692356 | tf_op jit(solution)/shard_map/convert_element_type | solution.py:726
  451.0 93.3 %back.1 = (bf16[2,512,1024]{2,1,0:T(8,128)(2,1)}, f32[3,128,256]{2,1,0:T(8,128)}, f32[128,1024]{1,0:T(8,128)}, f32[256,128]{1,0:T(8,128)}, f32[1024,128]{1,0:T(8...) custom-call(bf16[4,256,1024]{2,1,0:T(8,128)(2,1)} %fusion.15.rows, bf16[3,128,512]{2,1,0:T(8,128)(2,1)} %pad_maximum_fusion.3.dbq, ...), custom_call_target="tpu_custom_call" | custom-call | tf_op jit(solution)/shard_map/back/pallas_call | solution.py:613
  (169 shorter events, 78.2 us)
Async XLA Ops:
  7.2 268.3 %all-gather.6.cloned.1.call-start = ((), (), s32[]{:S(2)}) async-start(), calls=%async_computation.2 | async-start | bytes 5898240 | tf_op jit(solution)/shard_map/all_gather | solution.py:667
  12.9 109.9 %copy-start.27 = (s32[2,1,2048]{2,1,0:T(1,128)S(1)}, s32[2,1,2048]{2,1,0:T(1,128)}, u32[]{:S(2)}) copy-start(s32[2,1,2048]{2,1,0:T(1,128)} %param.19) | copy-start | bytes 49156
  12.9 109.9 %copy-start.28 = (s32[2,1,2048]{2,1,0:T(1,128)S(1)}, s32[2,1,2048]{2,1,0:T(1,128)}, u32[]{:S(2)}) copy-start(s32[2,1,2048]{2,1,0:T(1,128)} %param.18) | copy-start | bytes 49156
  122.8 176.6 %all-gather.4.cloned.1.call-start = ((), (), s32[]{:S(2)}) async-start(), calls=%async_computation.1 | async-start | bytes 5898240 | tf_op jit(solution)/shard_map/all_gather | solution.py:668
  122.9 35.0 %collective-permute-start = (s32[2,2,2048]{2,1,0:T(2,128)S(1)}, s32[2,2,2048]{2,1,0:T(2,128)S(1)}, u32[]{:S(2)}, u32[]{:S(2)}) collective-permute-start(s32[2,2,2048]{2,1,0:T(2,128)S(1)} %pad_add_fusion), channel_id=1, source_target_pairs={{0,4},{4,0},{8,12},{12,8},{16,20},{20,16},{24,28},{28,24},{1,5},{5... | collective-permute-start | bytes 98312 | tf_op jit(solution)/shard_map/ppermute | solution.py:637
  126.6 14.0 %copy-start.30 = (f32[1,1024]{1,0:T(1,128)}, f32[1,1024]{1,0:T(1,128)S(1)}, u32[]{:S(2)}) copy-start(f32[1,1024]{1,0:T(1,128)S(1)} %get-tuple-element.107) | copy-start | bytes 12292
  126.6 14.0 %copy-start.32 = (f32[1,1024]{1,0:T(1,128)}, f32[1,1024]{1,0:T(1,128)S(1)}, u32[]{:S(2)}) copy-start(f32[1,1024]{1,0:T(1,128)S(1)} %get-tuple-element.108) | copy-start | bytes 12292
  140.6 7.3 %copy-start.43 = (bf16[3,1024,512]{2,1,0:T(8,128)(2,1)}, bf16[3,1024,512]{2,1,0:T(8,128)(2,1)S(1)}, u32[]{:S(2)}) copy-start(bf16[3,1024,512]{2,1,0:T(8,128)(2,1)S(1)} %add_convert_fusion.4) | copy-start | bytes 9437188
  147.9 100.9 %copy-start.46 = (bf16[2048,384]{1,0:T(8,128)(2,1)}, bf16[2048,384]{1,0:T(8,128)(2,1)S(1)}, u32[]{:S(2)}) copy-start(bf16[2048,384]{1,0:T(8,128)(2,1)S(1)} %convolution_convert_fusion.1) | copy-start | bytes 4718596
  303.2 17.7 %copy-start.47 = (bf16[2048,1024]{1,0:T(8,128)(2,1)}, bf16[2048,1024]{1,0:T(8,128)(2,1)S(1)}, u32[]{:S(2)}) copy-start(bf16[2048,1024]{1,0:T(8,128)(2,1)S(1)} %add_convert_fusion) | copy-start | bytes 12582916
  324.2 13.0 %copy-start.4 = (bf16[2048,1024]{1,0:T(8,128)(2,1)S(1)}, bf16[2048,1024]{1,0:T(8,128)(2,1)}, u32[]{:S(2)}) copy-start(bf16[2048,1024]{1,0:T(8,128)(2,1)} %get-tuple-element.29) | copy-start | bytes 12582916
  324.2 13.0 %copy-start.31 = (f32[1,1024]{1,0:T(1,128)S(1)}, f32[1,1024]{1,0:T(1,128)}, u32[]{:S(2)}) copy-start(f32[1,1024]{1,0:T(1,128)} %copy-done.30) | copy-start | bytes 12292
  324.2 13.0 %copy-start.33 = (f32[1,1024]{1,0:T(1,128)S(1)}, f32[1,1024]{1,0:T(1,128)}, u32[]{:S(2)}) copy-start(f32[1,1024]{1,0:T(1,128)} %copy-done.32) | copy-start | bytes 12292
  354.8 12.8 %copy-start.15 = (bf16[512,1024]{1,0:T(8,128)(2,1)S(1)}, bf16[512,1024]{1,0:T(8,128)(2,1)}, u32[]{:S(2)}) copy-start(bf16[512,1024]{1,0:T(8,128)(2,1)} %copy-done.14) | copy-start | bytes 3145732
  370.1 8.5 %copy-start.6 = (f32[2048,1024]{1,0:T(8,128)}, f32[2048,1024]{1,0:T(8,128)S(1)}, u32[]{:S(2)}) copy-start(f32[2048,1024]{1,0:T(8,128)S(1)} %convolution_add_fusion) | copy-start | bytes 25165828
  378.6 26.2 %collective-permute-start.1 = (bf16[4,256,1024]{2,1,0:T(8,128)(2,1)}, bf16[4,256,1024]{2,1,0:T(8,128)(2,1)}, u32[]{:S(2)}, u32[]{:S(2)}) collective-permute-start(bf16[4,256,1024]{2,1,0:T(8,128)(2,1)} %fusion.25), channel_id=1, source_target_pairs={{0,4},{4,0},{8,12},{12,8},{16,20},{20,16},{24,28},{28,24},{1,5},{5... | collective-permute-start | bytes 6291464 | tf_op jit(solution)/shard_map/ppermute | solution.py:637
  378.6 53.5 %collective-permute-start.3 = (bf16[4,256,1024]{2,1,0:T(8,128)(2,1)}, bf16[4,256,1024]{2,1,0:T(8,128)(2,1)}, u32[]{:S(2)}, u32[]{:S(2)}) collective-permute-start(bf16[4,256,1024]{2,1,0:T(8,128)(2,1)} %fusion.26), channel_id=1, source_target_pairs={{0,4},{4,0},{8,12},{12,8},{16,20},{20,16},{24,28},{28,24},{1,5},{5... | collective-permute-start | bytes 6291464 | tf_op jit(solution)/shard_map/ppermute | solution.py:637
  388.7 9.1 %copy-start.45 = (bf16[2048,256]{1,0:T(8,128)(2,1)S(1)}, bf16[2048,256]{1,0:T(8,128)(2,1)}, u32[]{:S(2)}) copy-start(bf16[2048,256]{1,0:T(8,128)(2,1)} %fusion.19) | copy-start | bytes 3145732
  410.2 7.8 %copy-start.21 = (bf16[512,128]{1,0:T(8,128)(2,1)S(1)}, bf16[512,128]{1,0:T(8,128)(2,1)}, u32[]{:S(2)}) copy-start(bf16[512,128]{1,0:T(8,128)(2,1)} %get-tuple-element.34) | copy-start | bytes 393220
  410.2 32.3 %all-to-all-start = ((bf16[4,256,1024]{2,1,0:T(8,128)(2,1)}), bf16[4,256,1024]{2,1,0:T(8,128)(2,1)}, u32[]{:S(2)}, u32[]{:S(2)}) async-start(bf16[4,256,1024]{2,1,0:T(8,128)(2,1)} %fusion.16), calls=%async_computation | async-start | bytes 4194304 | tf_op jit(solution)/shard_map/all_to_all | solution.py:649
  437.0 7.6 %copy-start.29 = (f32[4,1,256,1]{2,0,1,3:T(4,128)S(1)}, f32[4,1,256,1]{2,0,1,3:T(4,128)}, u32[]{:S(2)}) copy-start(f32[4,1,256,1]{2,0,1,3:T(4,128)} %copy.59) | copy-start | bytes 12292
  444.4 105.0 %collective-permute-start.2 = (bf16[2,256,1024]{2,1,0:T(8,128)(2,1)S(1)}, bf16[2,256,1024]{2,1,0:T(8,128)(2,1)S(1)}, u32[]{:S(2)}, u32[]{:S(2)}) collective-permute-start(bf16[2,256,1024]{2,1,0:T(8,128)(2,1)S(1)} %get-tuple-element.99), channel_id=1, source_target_pairs={{0,4},{4,0},{8,12},{12,8},{16,20},{20,16},{24,28},{28,24},{1,5},{5... | collective-permute-start | bytes 3145736 | tf_op jit(solution)/shard_map/ppermute | solution.py:637
  544.3 9.4 %copy-start.16 = (bf16[2,512,1024]{2,1,0:T(8,128)(2,1)S(1)}, bf16[2,512,1024]{2,1,0:T(8,128)(2,1)}, u32[]{:S(2)}) copy-start(bf16[2,512,1024]{2,1,0:T(8,128)(2,1)} %get-tuple-element.41) | copy-start | bytes 6291460
  550.4 7.7 %copy-start.1 = (bf16[1024,1024]{1,0:T(8,128)(2,1)S(1)}, bf16[1024,1024]{1,0:T(8,128)(2,1)}, u32[]{:S(2)}) copy-start(bf16[1024,1024]{1,0:T(8,128)(2,1)} %param.24) | copy-start | bytes 6291460
  (32 other events, 145.9 us)
Sparse Core Ops, SparseCore 0:
  122.9 58.2 all-gather.5
  183.0 56.8 all-gather.3

commit v3 on v2

--- a/solution.py
+++ b/solution.py
@@ -524,7 +524,7 @@
 
     def parts(j):
         return (dbq.at[:, :, aligned(j, 128)], dbu.at[:, aligned(j, 512)], dao.at[aligned(j, 128)],
-                dad.at[aligned(j, 512)], sh.at[:, aligned(j, 32)])
+                dad.at[:, aligned(j, 512)], sh.at[:, aligned(j, 32)])
 
     got = (rbq, rbu, rao, rad, rsh)
 
@@ -536,7 +536,29 @@
             cross(k, i).start()
     norm_next(1)
     norm_next(2)
+
     sums = (pbq, pbu, pao, pad, psh)
+    halves = (qbq, qbu, qao, qad, qsh)
+    low = z % 2
+
+    def half(v, i, j):
+        if i == 0:
+            return v.at[:, aligned(j, 64)]
+        if i == 4:
+            return v.at[:, aligned(j, 16)]
+        return v.at[aligned(j, 64)]
+
+    def along(step, i):
+        j = low ^ 1 if step == 0 else low
+        dst = sums[i].at[2] if step == 2 else halves[i].at[step]
+        return remote(half(sums[i].at[step], i, j), half(dst, i, j), z_sems.at[0, step, i], z_sems.at[1, step, i],
+                      (d ^ (4 if step == 1 else 2), t))
+
+    def arrived(step, i):
+        j = low ^ 1 if step == 2 else low
+        dst = sums[i].at[2] if step == 2 else halves[i].at[step]
+        return remote(half(dst, i, j), half(dst, i, j), z_sems.at[0, step, i], z_sems.at[1, step, i], (d, t ^ 1))
+
     for i in range(5):
         for k in (1, 2, 3):
             cross(k, i).wait_recv()
@@ -544,39 +566,34 @@
         for k in (0, 1, 2):
             total = total + got[i][k].astype(F32)
         sums[i][0] = total.astype(BF)
-
-    halves = (qbq, qbu, qao, qad, qsh)
-
-    def along(step, i):
-        return remote(sums[i].at[step], halves[i].at[step], z_sems.at[0, step, i], z_sems.at[1, step, i],
-                      (d ^ (2 << step), t))
-
-    for i in range(5):
         along(0, i).start()
     norm_next(3)
-    for i in range(5):
-        along(0, i).wait_recv()
-        sums[i][1] = (sums[i][0].astype(F32) + halves[i][0].astype(F32)).astype(BF)
-        along(1, i).start()
-    norm_next(4)
+    for step in (0, 1):
+        for i in range(5):
+            arrived(step, i).wait_recv()
+            mine, other = half(sums[i].at[step], i, low), half(halves[i].at[step], i, low)
+            half(sums[i].at[step + 1], i, low)[...] = (mine[...].astype(F32) + other[...].astype(F32)).astype(BF)
+            along(step + 1, i).start()
+        if step == 0:
+            norm_next(4)
     result = (obq.at[:, :, aligned(c, 128)], obu.at[:, aligned(c, 512)], oao.at[aligned(c, 128)],
-              oad.at[aligned(c, 512)], osh.at[:, :, aligned(c, 512)])
+              oad.at[:, aligned(c, 512)], osh.at[:, :, aligned(c, 512)])
     theirs = (obq.at[:, :, aligned(c ^ 1, 128)], obu.at[:, aligned(c ^ 1, 512)], oao.at[aligned(c ^ 1, 128)],
-              oad.at[aligned(c ^ 1, 512)], osh.at[:, :, aligned(c ^ 1, 512)])
+              oad.at[:, aligned(c ^ 1, 512)], osh.at[:, :, aligned(c ^ 1, 512)])
 
     def last(i):
         return remote(result[i], result[i], last_sems.at[0, i], last_sems.at[1, i], sibling)
 
     for i in range(5):
-        along(1, i).wait_recv()
-        result[i][...] = sums[i][1].astype(F32) + halves[i][1].astype(F32)
+        arrived(2, i).wait_recv()
+        result[i][...] = sums[i][2].astype(F32)
         last(i).start()
 
     for i in range(5):
         remote(theirs[i], theirs[i], last_sems.at[0, i], last_sems.at[1, i], sibling).wait_recv()
         last(i).wait_send()
-        along(0, i).wait_send()
-        along(1, i).wait_send()
+        for step in (0, 1, 2):
+            along(step, i).wait_send()
         for k in (1, 2, 3):
             cross(k, i).wait_send()
     share().wait_send()
@@ -607,8 +624,8 @@
 
 def back(rows, dbq, dbu, dao, dad, dsh, dno):
     vmem = pl.BlockSpec(memory_space=pltpu.VMEM)
-    part = [(3, 128, 128), (128, 512), (128, 128), (512, 128), (6, 32, 512)]
-    outs = [((2, 512, 1024), BF), ((3, 128, 256), F32), ((128, 1024), F32), ((256, 128), F32), ((1024, 128), F32),
+    part = [(3, 128, 128), (128, 512), (128, 128), (128, 512), (6, 32, 512)]
+    outs = [((2, 512, 1024), BF), ((3, 128, 256), F32), ((128, 1024), F32), ((256, 128), F32), ((128, 1024), F32),
             ((6, 32, 1024), F32), ((4, 1024), F32)]
     return pl.pallas_call(
         back_kernel,
@@ -619,12 +636,12 @@
             pltpu.SemaphoreType.DMA((8,)),
             pltpu.SemaphoreType.DMA((2,)),
             pltpu.SemaphoreType.DMA((2, 3, 5)),
-            pltpu.SemaphoreType.DMA((2, 2, 5)),
+            pltpu.SemaphoreType.DMA((2, 3, 5)),
             pltpu.SemaphoreType.DMA((2, 5)),
             pltpu.SemaphoreType.DMA((2, 5)),
             pltpu.VMEM((6, 128, 512), BF),
             pltpu.VMEM((6, 128, 512), BF),
-        ] + [pltpu.VMEM((3,) + s, BF) for s in part] + [pltpu.VMEM((2,) + s, BF) for s in part + part] + [
+        ] + [pltpu.VMEM((3,) + s, BF) for s in part + part] + [pltpu.VMEM((2,) + s, BF) for s in part] + [
             pltpu.VMEM((5, 4, 1024), F32),
             pltpu.VMEM((4, 4, 1024), F32),
         ],
@@ -682,10 +699,10 @@
     n1 = (standard * gain[0] + bias[0]).astype(BF)
     n2 = (standard * gain[1] + bias[1]).astype(BF)
     lin = jnp.einsum("nkc,sk->ncs", m_qkv, n1, preferred_element_type=F32)
-    low3 = dot(n1, a_three, 1, 1).astype(BF)
-    low1 = dot(n2, a_full[3], 1, 1).astype(BF)
+    low3 = dot(a_three, n1, 1, 1).astype(BF).reshape(3, RANK, 2048)
+    low1 = dot(a_full[3], n2, 1, 1).astype(BF)
     g_ctx = dot(m_out, g_full, 1, 1).astype(BF)
-    low_grad = (SCALE * dot(g_full, b_both, 1, 1)).astype(BF)
+    low_grad = (SCALE * dot(b_both, g_full, 1, 1)).astype(BF)
     cos, sin = rotary_tables(seg)
     ctx, d_lin = attention(lin, g_ctx, cos, sin, seg, kept)
 
@@ -712,20 +729,19 @@
 
     norms = jnp.stack([jnp.sum(one * standard, axis=0), jnp.sum(two * standard, axis=0),
                        jnp.sum(one, axis=0), jnp.sum(two, axis=0)])
-    lo_ctx = dot(ctx, a_out_all, 0, 0).astype(BF)
-    lo_hid = dot(hidden, a_down_all, 1, 0).astype(BF)
-    d_a_out = dot(ctx, low_grad[:, :RANK], 1, 0).astype(BF)
-    d_a_down = dot(hidden, low_grad[:, RANK:], 0, 0).astype(BF)
-    d_b_qkv = jnp.stack([(SCALE * dot(low3[:, RANK * i:RANK * (i + 1)], d_lin[i], 0, 1)).astype(BF) for i in range(3)])
-    d_b_up = (SCALE * dot(low1, d_pre, 0, 0)).astype(BF)
-    back3 = [(SCALE * dot(d_lin[i], b_qkv_all[i], 0, 1)).astype(BF) for i in range(3)]
-    back1 = (SCALE * dot(d_pre, b_up_all, 1, 1)).astype(BF)
-    shared = jnp.stack([dot(v, n1, 0, 0).astype(BF) for v in back3] + [dot(back1, n2, 0, 0).astype(BF)]
-                       + [(SCALE * dot(v, g_full, 0, 0)).astype(BF) for v in (lo_ctx, lo_hid)])
+    lo = jnp.concatenate([dot(a_out_all, ctx, 0, 0), dot(a_down_all, hidden, 0, 1)], axis=0).astype(BF)
+    d_a_out = dot(ctx, low_grad[:RANK], 1, 1).astype(BF)
+    d_a_down = dot(low_grad[RANK:], hidden, 1, 0).astype(BF)
+    d_b_qkv = (SCALE * jnp.einsum("nrs,ncs->nrc", low3, d_lin, preferred_element_type=F32)).astype(BF)
+    d_b_up = (SCALE * dot(low1, d_pre, 1, 0)).astype(BF)
+    back3 = (SCALE * jnp.einsum("nrc,ncs->nrs", b_qkv_all, d_lin, preferred_element_type=F32)).astype(BF)
+    back1 = (SCALE * dot(b_up_all, d_pre, 1, 1)).astype(BF)
+    shared = jnp.concatenate([dot(back3.reshape(3 * RANK, 2048), n1, 1, 0).astype(BF), dot(back1, n2, 1, 0).astype(BF),
+                              (SCALE * dot(lo, g_full, 1, 0)).astype(BF)], axis=0).reshape(6, RANK, 1024)
     grad, r_b_qkv, r_b_up, r_a_out, r_a_down, rest, norms = back(
         grad.astype(BF), d_b_qkv, d_b_up, d_a_out, d_a_down, shared, norms)
     r_a_in = jnp.swapaxes(rest[:4], 1, 2)
-    return (y[:, None], grad[:, None], norms[:2], norms[2:], r_a_in, r_b_qkv, r_b_up, r_a_out, r_a_down, rest[4:])
+    return (y[:, None], grad[:, None], norms[:2], norms[2:], r_a_in, r_b_qkv, r_b_up, r_a_out, jnp.transpose(r_a_down), rest[4:])
 
 
 def solution(mesh):

time: 571 us -> 531 us (0.930)
  Pallas kernels: 290 us -> 264 us
  matrix products: 175 us -> 157 us
  starting transfers between devices: 7.87 us -> 17.5 us
    dot_general x23 -> x19, matrix products: 147 us -> 123 us  [dot(): lax.dot_general(a, b, (((ca,), (cb,)), ((), ())), preferred_element_type=...]
    pallas_call x1, Pallas kernels: 93.3 us -> 76.3 us  [back(): pl.pallas_call(back_kernel, in_specs=[vmem] * 7, out_specs=[pl.BlockSpec(...]
    all_to_all x1, starting transfers between devices: 7.14 us -> 16.8 us  [from_group(): got = lax.all_to_all(own, 'tensor', 0, 0, tiled=True).reshape(2, 2, 256, -1)]
    pallas_call x1, Pallas kernels: 86.8 us -> 77.8 us  [attention(): pl.pallas_call(functools.partial(attention_kernel, heads), grid_spec=pltp...]
    dot_general x0 -> x2, matrix products: none -> 6.9 us  [the longest x1 3.92 us: by_groups(): jnp.einsum('nrc,ncs->nrs', b_qkv_all, d_lin, preferred_element_type=F32)]
    unnamed x104 -> x94, local copies, waits for them, and re-layouts: 13.5 us -> 11.2 us
  transfers between devices with their start and end apart: 7 -> 7, of which waited for: 1 -> 1; matrix products, arithmetic and copies ran while one was open for 26% -> 26% of each run, Pallas kernels for 32% -> 29%
where the time goes in v3:
time: 531 us; the launch traced here: 528 us
  Pallas kernels  264 us (50%)
  matrix products  157 us (30%)
  other arithmetic  34.4 us (6%)
  local copies, waits for them, and re-layouts  32.5 us (6%)
  starting transfers between devices  17.5 us (3%)
  between operations  15 us (3%)
  waiting for transfers between devices  7.53 us (1%)
    dot_general x19, matrix products, dot(): lax.dot_general(a, b, (((ca,), (cb,)), ((), ())), preferred_element_type=...  123 us
    pallas_call x1, Pallas kernels, front(): pl.pallas_call(front_kernel, in_specs=[anywhere] * 8, out_specs=[anywhere...  110 us
    pallas_call x1, Pallas kernels, attention(): pl.pallas_call(functools.partial(attention_kernel, heads), grid_spec=pltp...  77.8 us
    pallas_call x1, Pallas kernels, back(): pl.pallas_call(back_kernel, in_specs=[vmem] * 7, out_specs=[pl.BlockSpec(...  76.3 us
    all_to_all x1, starting transfers between devices, from_group(): got = lax.all_to_all(own, 'tensor', 0, 0, tiled=True).reshape(2, 2, 256, -1)  16.8 us
    dot_general x1, matrix products, by_groups(): one = jnp.einsum('ncs,nkc->sk', d_lin, m_qkv, preferred_element_type=F32)  16.5 us
    unnamed x94, local copies, waits for them, and re-layouts  11.2 us
  transfers between devices with their start and end apart: 7, of which 1 were waited for; matrix products, arithmetic and copies ran while one was open for 26% of the time, Pallas kernels for 29%

profile of v3, /device:TPU:0, one launch (start us, length us, event | category | flops | bytes accessed | tf_op | source)
XLA Modules:
  0.0 527.6 jit_solution(9529520701890478195)
XLA Ops:
  12.9 109.8 %front.1 = (bf16[2048,1024]{1,0:T(8,128)(2,1)}, bf16[2048,1024]{1,0:T(8,128)(2,1)}, bf16[3,1024,512]{2,1,0:T(8,128)(2,1)}, bf16[512,1024]{1,0:T(8,128)(2,1)}, bf...) custom-call(bf16[2,512,1024]{2,1,0:T(8,128)(2,1)} %bitcast.179, ...), custom_call_target="tpu_custom_call" | custom-call | tf_op jit(solution)/shard_map/front/pallas_call | solution.py:446
  130.3 5.3 fusion.19
  147.3 9.2 %fusion.17.lin_ref = f32[3,512,2048]{2,1,0:T(8,128)} fusion(bf16[3,1024,512]{2,1,0:T(8,128)(2,1)S(1)} %add_convert_fusion.4, bf16[2048,1024]{1,0:T(8,128)(2,1)S(1)} %get-tuple-element.96), kind=kOutput, calls=%fused_computation.37 | convolution fusion | flops 6442450944 | bytes 19922944 | tf_op jit(solution)/shard_map/nkc,sk->ncs/dot_general | solution.py:701
  161.2 77.8 %attention.1 = (bf16[512,2048]{1,0:T(8,128)(2,1)}, bf16[3,512,2048]{2,1,0:T(8,128)(2,1)}) custom-call(s32[8]{0:T(128)} %and_select_fusion.lo_ref, f32[3,512,2048]{2,1,0:T(8,128)} %fusion.17.lin_ref, bf16[512,2048]{1,0:T(8,128)(2,1)} %convolution_convert_fusion.g_ref, f32[8,2048]{1,0:T(8,128)} %get-tuple-element.106.cos_ref, ...), custom_call_target="tpu_custom_call" | custom-call | flops 8053063680 | bytes 27262976 | tf_op jit(solution)/shard_map/attention/pallas_call | solution.py:148
  245.1 3.9 multiply_convert_fusion.1
  258.6 4.8 add_convert_fusion.1
  265.4 14.0 %multiply_convert_fusion = (bf16[2048,2048]{1,0:T(8,128)(2,1)}, f32[2048,2048]{1,0:T(8,128)}) fusion(bf16[2048,1024]{1,0:T(8,128)(2,1)S(1)} %copy-done.6, bf16[1024,2048]{1,0:T(8,128)(2,1)S(1)} %add_convert_fusion.1), kind=kOutput, calls=%fused_computation.7 | convolution fusion | flops 8610906112 | bytes 33554432 | tf_op jit(solution)/shard_map/dot_general | solution.py:23
  279.4 3.8 add_convert_fusion
  283.2 17.5 %fusion.5 = bf16[2048,2048]{1,0:T(8,128)(2,1)} fusion(f32[2048,2048]{1,0:T(8,128)} %get-tuple-element.112, bf16[2048,1024]{1,0:T(8,128)(2,1)} %get-tuple-element.36, bf16[2048,1024]{1,0:T(8,128)(2,1)S(1)} %add_convert_fusion), kind=kOutput, calls=%fused_computation.6 | convolution fusion | flops 8631877632 | bytes 33554432 | tf_op jit(solution)/shard_map/dot_general | solution.py:23
  300.8 9.0 %fusion.54 = f32[2048,1024]{1,0:T(8,128)S(1)} fusion(bf16[2048,2048]{1,0:T(8,128)(2,1)S(1)} %bitcast.163, bf16[2048,1024]{1,0:T(8,128)(2,1)S(1)} %add_convert_fusion), kind=kOutput, calls=%fused_computation.134 | convolution fusion | flops 8589934592 | bytes 20971520 | tf_op jit(solution)/shard_map/dot_general | solution.py:23
  309.8 5.9 %convolution_add_fusion = f32[2048,1024]{1,0:T(8,128)} fusion(f32[2048,1024]{1,0:T(8,128)S(1)} %fusion.54, bf16[512,2048]{1,0:T(8,128)(2,1)S(1)} %copy-done.7, bf16[512,1024]{1,0:T(8,128)(2,1)S(1)} %add_convert_fusion.5), kind=kOutput, calls=%fused_computation.39 | convolution fusion | flops 2149580800 | bytes 19922944 | tf_op jit(solution)/shard_map/dot_general | solution.py:23
  315.7 14.9 %fusion.55 = f32[2048,1024]{1,0:T(8,128)} fusion(bf16[2048,2048]{1,0:T(8,128)(2,1)} %fusion.5, bf16[1024,2048]{1,0:T(8,128)(2,1)} %copy-done.39), kind=kOutput, calls=%fused_computation.135 | convolution fusion | flops 8589934592 | bytes 20971520 | tf_op jit(solution)/shard_map/dot_general | solution.py:23
  330.7 16.5 %fusion.10 = (f32[1024]{0:T(1024)S(1)}, f32[1024]{0:T(1024)S(1)}, f32[1024]{0:T(1024)S(1)}, f32[1024]{0:T(1024)S(1)}, f32[2048,1024]{1,0:T(8,128)}, /*index=5*/f32[2048,1024]{1,0:T(8,128)}) fusion(bf16[2048,1024]{1,0:T(8,128)(2,1)S(1)} %copy-done.4, f32[2048]{0:T(1024)S(1)} %add_rsqrt_fusion, f32[2048]{0:T(1024)S(1)} %broadcast_multiply_fusion, ...), kind=kOutput, calls=%fused_computation.18 | convolution fusion | flops 6467612672 | bytes 38838272 | tf_op jit(solution)/shard_map/ncs,nkc->sk/dot_general | solution.py:720
  349.8 3.8 fusion.23
  354.7 6.5 %convolution_convert_fusion.2 = bf16[128,2048]{1,0:T(8,128)(2,1)S(1)} fusion(bf16[2048,2048]{1,0:T(8,128)(2,1)} %get-tuple-element.111, bf16[2048,1152]{1,0:T(8,128)(2,1)} %all-gather.4.cloned.1.call-done), kind=kOutput, calls=%fused_computation.47 | convolution fusion | flops 1074003968 | bytes 9437184 | tf_op jit(solution)/shard_map/dot_general | solution.py:23
  361.3 8.3 %convolution_convert_fusion.7 = bf16[128,1024]{1,0:T(8,128)(2,1)S(1)} fusion(bf16[2048,1024]{1,0:T(8,128)(2,1)} %get-tuple-element.97, bf16[2048,2048]{1,0:T(8,128)(2,1)} %fusion.5, bf16[128,512]{1,0:T(8,128)(2,1)} %copy-done.24, bf16[128,512]{1,0:T(8,128)(2,1)} %copy-done.25, bf16[128,512]{1,0:T(8,128)(2,1)} %copy-done.26, ...), kind=kOutput, calls=%fused_computation.63 | convolution fusion | flops 1613365248 | bytes 13369344 | tf_op jit(solution)/shard_map/dot_general | solution.py:23
  374.5 5.3 %fusion.16 = bf16[4,256,1024]{2,1,0:T(8,128)(2,1)} fusion(bf16[4,256,1024]{2,1,0:T(8,128)(2,1)} %collective-permute-done.1, f32[4,2,256,1024]{3,2,1,0:T(8,128)} %bitcast.166, s32[]{:T(128)S(6)} %select_n.99, bf16[4,2,256,1024]{3,2,1,0:T(8,128)(2,1)S(1)} %bitcast.164), kind=kLoop, calls=%fused_computation.36 | loop fusion | flops 5242880 | bytes 10485764 | tf_op jit(solution)/shard_map/convert_element_type | solution.py:718
  379.9 16.8 %all-to-all-start = ((bf16[4,256,1024]{2,1,0:T(8,128)(2,1)}), bf16[4,256,1024]{2,1,0:T(8,128)(2,1)S(1)}, u32[]{:S(2)}, u32[]{:S(2)}) async-start(bf16[4,256,1024]{2,1,0:T(8,128)(2,1)} %fusion.16), calls=%async_computation | async-start | bytes 4194304 | tf_op jit(solution)/shard_map/all_to_all | solution.py:666
  396.6 5.4 %convolution_convert_fusion.3.dad = bf16[128,2048]{1,0:T(8,128)(2,1)} fusion(bf16[2048,2048]{1,0:T(8,128)(2,1)} %get-tuple-element.111, bf16[256,2048]{1,0:T(8,128)(2,1)S(1)} %copy-done.15), kind=kOutput, calls=%fused_computation.48 | convolution fusion | flops 1074003968 | bytes 9437184 | tf_op jit(solution)/shard_map/dot_general | solution.py:23
  402.1 8.2 %fusion.20.dbu = bf16[128,2048]{1,0:T(8,128)(2,1)} fusion(bf16[2048,2048]{1,0:T(8,128)(2,1)} %fusion.5, bf16[2048,1024]{1,0:T(8,128)(2,1)} %get-tuple-element.97, bf16[4,128,1024]{2,1,0:T(8,128)(2,1)} %get-tuple-element.31), kind=kOutput, calls=%fused_computation.49 | convolution fusion | flops 1611399168 | bytes 13369344 | tf_op jit(solution)/shard_map/dot_general | solution.py:23
  410.2 4.9 fusion.26
  415.1 6.9 %all-to-all-done = bf16[4,256,1024]{2,1,0:T(8,128)(2,1)S(1)} async-done(((bf16[4,256,1024]{2,1,0:T(8,128)(2,1)}), bf16[4,256,1024]{2,1,0:T(8,128)(2,1)S(1)}, u32[]{:S(2)}, u32[]{:S(2)}) %all-to-all-start) | async-done | bytes 2097184 | tf_op jit(solution)/shard_map/all_to_all | solution.py:666
  424.6 5.7 %fusion.15.rows = bf16[4,256,1024]{2,1,0:T(8,128)(2,1)} fusion(f32[4,2,256,1024]{3,2,1,0:T(8,128)} %bitcast.173, s32[]{:T(128)S(6)} %select_n.99, f32[4,256]{1,0:T(4,128)S(1)} %bitcast.192, f32[4,256]{1,0:T(4,128)S(1)} %get-tuple-element.113, f32[4,256]{1,0:T(4,128)S(1)} %get-tuple-element.114, bf16[4,2,256,1024]{3,2,1,0:T(8,128)(2,1)S(1)} %bitcast.184, ...), kind=kLoop, calls=%fused_computation.31 | loop fusion | flops 9437184 | bytes 14692356 | tf_op jit(solution)/shard_map/convert_element_type | solution.py:742
  430.3 76.3 %back.1 = (bf16[2,512,1024]{2,1,0:T(8,128)(2,1)}, f32[3,128,256]{2,1,0:T(8,128)}, f32[128,1024]{1,0:T(8,128)}, f32[256,128]{1,0:T(8,128)}, f32[128,1024]{1,0:T(8...) custom-call(bf16[4,256,1024]{2,1,0:T(8,128)(2,1)} %fusion.15.rows, bf16[3,128,512]{2,1,0:T(8,128)(2,1)} %fusion.25.dbq, ...), custom_call_target="tpu_custom_call" | custom-call | tf_op jit(solution)/shard_map/back/pallas_call | solution.py:630
  (159 shorter events, 72.0 us)
Async XLA Ops:
  7.2 247.6 %all-gather.6.cloned.1.call-start = ((), (), s32[]{:S(2)}) async-start(), calls=%async_computation.2 | async-start | bytes 5898240 | tf_op jit(solution)/shard_map/all_gather | solution.py:684
  12.9 109.9 %copy-start.27 = (s32[2,1,2048]{2,1,0:T(1,128)S(1)}, s32[2,1,2048]{2,1,0:T(1,128)}, u32[]{:S(2)}) copy-start(s32[2,1,2048]{2,1,0:T(1,128)} %param.19) | copy-start | bytes 49156
  12.9 109.9 %copy-start.28 = (s32[2,1,2048]{2,1,0:T(1,128)S(1)}, s32[2,1,2048]{2,1,0:T(1,128)}, u32[]{:S(2)}) copy-start(s32[2,1,2048]{2,1,0:T(1,128)} %param.18) | copy-start | bytes 49156
  122.8 156.6 %all-gather.4.cloned.1.call-start = ((), (), s32[]{:S(2)}) async-start(), calls=%async_computation.1 | async-start | bytes 5898240 | tf_op jit(solution)/shard_map/all_gather | solution.py:685
  122.9 34.3 %collective-permute-start = (s32[2,2,2048]{2,1,0:T(2,128)S(1)}, s32[2,2,2048]{2,1,0:T(2,128)S(1)}, u32[]{:S(2)}, u32[]{:S(2)}) collective-permute-start(s32[2,2,2048]{2,1,0:T(2,128)S(1)} %pad_add_fusion), channel_id=1, source_target_pairs={{0,4},{4,0},{8,12},{12,8},{16,20},{20,16},{24,28},{28,24},{1,5},{5... | collective-permute-start | bytes 98312 | tf_op jit(solution)/shard_map/ppermute | solution.py:654
  126.6 13.9 %copy-start.30 = (f32[1,1024]{1,0:T(1,128)}, f32[1,1024]{1,0:T(1,128)S(1)}, u32[]{:S(2)}) copy-start(f32[1,1024]{1,0:T(1,128)S(1)} %get-tuple-element.107) | copy-start | bytes 12292
  126.6 13.9 %copy-start.32 = (f32[1,1024]{1,0:T(1,128)}, f32[1,1024]{1,0:T(1,128)S(1)}, u32[]{:S(2)}) copy-start(f32[1,1024]{1,0:T(1,128)S(1)} %get-tuple-element.108) | copy-start | bytes 12292
  239.1 10.0 %slice-start.2 = ((s8[6291456]{0:T(1024)(128)(4,1)}), s8[4194304]{0:T(1024)(128)(4,1)S(1)}, s32[]{:S(2)}) async-start(s8[6291456]{0:T(1024)(128)(4,1)} %bitcast.167), calls=%async_computation.5 | async-start | bytes 8388608
  265.4 14.0 %copy-start.22 = (bf16[2,128,1024]{2,1,0:T(8,128)(2,1)S(1)}, bf16[2,128,1024]{2,1,0:T(8,128)(2,1)}, u32[]{:S(2)}) copy-start(bf16[2,128,1024]{2,1,0:T(8,128)(2,1)} %get-tuple-element.35) | copy-start | bytes 1572868
  279.4 21.3 %slice-start = ((s8[8388608]{0:T(1024)(128)(4,1)}), s8[4194304]{0:T(1024)(128)(4,1)S(1)}, s32[]{:S(2)}) async-start(s8[8388608]{0:T(1024)(128)(4,1)} %bitcast.162), calls=%async_computation.3 | async-start | bytes 8388608
  283.2 17.6 %slice-start.1 = ((s8[8388608]{0:T(1024)(128)(4,1)}), s8[4194304]{0:T(1024)(128)(4,1)S(1)}, s32[]{:S(2)}) async-start(s8[8388608]{0:T(1024)(128)(4,1)} %bitcast.162), calls=%async_computation.4 | async-start | bytes 8388608
  300.8 9.0 %copy-start.7 = (bf16[512,2048]{1,0:T(8,128)(2,1)S(1)}, bf16[512,2048]{1,0:T(8,128)(2,1)}, u32[]{:S(2)}) copy-start(bf16[512,2048]{1,0:T(8,128)(2,1)} %get-tuple-element.37) | copy-start | bytes 6291460
  315.7 14.9 %copy-start.4 = (bf16[2048,1024]{1,0:T(8,128)(2,1)S(1)}, bf16[2048,1024]{1,0:T(8,128)(2,1)}, u32[]{:S(2)}) copy-start(bf16[2048,1024]{1,0:T(8,128)(2,1)} %get-tuple-element.29) | copy-start | bytes 12582916
  315.7 14.9 %copy-start.31 = (f32[1,1024]{1,0:T(1,128)S(1)}, f32[1,1024]{1,0:T(1,128)}, u32[]{:S(2)}) copy-start(f32[1,1024]{1,0:T(1,128)} %copy-done.30) | copy-start | bytes 12292
  315.7 14.9 %copy-start.33 = (f32[1,1024]{1,0:T(1,128)S(1)}, f32[1,1024]{1,0:T(1,128)}, u32[]{:S(2)}) copy-start(f32[1,1024]{1,0:T(1,128)} %copy-done.32) | copy-start | bytes 12292
  315.7 14.9 %copy-start.38 = (bf16[3,1024,512]{2,1,0:T(8,128)(2,1)S(1)}, bf16[3,1024,512]{2,1,0:T(8,128)(2,1)}, u32[]{:S(2)}) copy-start(bf16[3,1024,512]{2,1,0:T(8,128)(2,1)} %copy-done.37) | copy-start | bytes 9437188
  349.7 24.8 %collective-permute-start.1 = (bf16[4,256,1024]{2,1,0:T(8,128)(2,1)S(1)}, bf16[4,256,1024]{2,1,0:T(8,128)(2,1)}, u32[]{:S(2)}, u32[]{:S(2)}) collective-permute-start(bf16[4,256,1024]{2,1,0:T(8,128)(2,1)S(1)} %fusion.22), channel_id=1, source_target_pairs={{0,4},{4,0},{8,12},{12,8},{16,20},{20,16},{24,28},{28,24},{1,5},{5... | collective-permute-start | bytes 6291464 | tf_op jit(solution)/shard_map/ppermute | solution.py:654
  353.6 56.6 %collective-permute-start.3 = (bf16[4,256,1024]{2,1,0:T(8,128)(2,1)}, bf16[4,256,1024]{2,1,0:T(8,128)(2,1)}, u32[]{:S(2)}, u32[]{:S(2)}) collective-permute-start(bf16[4,256,1024]{2,1,0:T(8,128)(2,1)} %fusion.23), channel_id=1, source_target_pairs={{0,4},{4,0},{8,12},{12,8},{16,20},{20,16},{24,28},{28,24},{1,5},{5... | collective-permute-start | bytes 6291464 | tf_op jit(solution)/shard_map/ppermute | solution.py:654
  361.2 8.3 %copy-start.18 = (bf16[128,2048]{1,0:T(8,128)(2,1)S(1)}, bf16[128,2048]{1,0:T(8,128)(2,1)}, u32[]{:S(2)}) copy-start(bf16[128,2048]{1,0:T(8,128)(2,1)} %convolution_convert_fusion.4) | copy-start | bytes 1572868
  379.9 16.8 %copy-start.15 = (bf16[256,2048]{1,0:T(8,128)(2,1)S(1)}, bf16[256,2048]{1,0:T(8,128)(2,1)}, u32[]{:S(2)}) copy-start(bf16[256,2048]{1,0:T(8,128)(2,1)} %fusion.19) | copy-start | bytes 3145732
  379.9 42.2 %all-to-all-start = ((bf16[4,256,1024]{2,1,0:T(8,128)(2,1)}), bf16[4,256,1024]{2,1,0:T(8,128)(2,1)S(1)}, u32[]{:S(2)}, u32[]{:S(2)}) async-start(bf16[4,256,1024]{2,1,0:T(8,128)(2,1)} %fusion.16), calls=%async_computation | async-start | bytes 4194304 | tf_op jit(solution)/shard_map/all_to_all | solution.py:666
  415.1 8.2 %copy-start.29 = (f32[4,1,256,1]{2,0,1,3:T(4,128)S(1)}, f32[4,1,256,1]{2,0,1,3:T(4,128)}, u32[]{:S(2)}) copy-start(f32[4,1,256,1]{2,0,1,3:T(4,128)} %copy.62) | copy-start | bytes 12292
  423.3 90.4 %collective-permute-start.2 = (bf16[2,256,1024]{2,1,0:T(8,128)(2,1)}, bf16[2,256,1024]{2,1,0:T(8,128)(2,1)}, u32[]{:S(2)}, u32[]{:S(2)}) collective-permute-start(bf16[2,256,1024]{2,1,0:T(8,128)(2,1)} %get-tuple-element.99), channel_id=1, source_target_pairs={{0,4},{4,0},{8,12},{12,8},{16,20},{20,16},{24,28},{28,24},{1,5},{5... | collective-permute-start | bytes 3145736 | tf_op jit(solution)/shard_map/ppermute | solution.py:654
  513.7 6.9 %copy-start.1 = (bf16[1024,1024]{1,0:T(8,128)(2,1)S(1)}, bf16[1024,1024]{1,0:T(8,128)(2,1)}, u32[]{:S(2)}) copy-start(bf16[1024,1024]{1,0:T(8,128)(2,1)} %param.24) | copy-start | bytes 6291460
  (27 other events, 111.7 us)
Sparse Core Ops, SparseCore 0:
  122.9 58.1 all-gather.5
  183.0 56.9 all-gather.3

commit v4 on v3

--- a/solution.py
+++ b/solution.py
@@ -24,7 +24,7 @@
 
 
 def attention_kernel(heads, lo_ref, lin_ref, g_ref, cos_ref, sin_ref, segq_ref, segk_ref,
-                     ctx_ref, dlin_ref, qt, kt, vt, kn, vn, qz, acc, s_scr, e_scr):
+                     ctx_ref, dlin_ref, qt, kt, vt, kn, vn, acc, s_scr, e_scr, p_scr, row):
     length = lin_ref.shape[2]
     blocks = length // TILE
 
@@ -45,9 +45,7 @@
             vt[rows, cols] = v.astype(BF)
             kn[h, cols, :] = jnp.transpose(k).astype(BF)
             vn[h, cols, :] = jnp.transpose(v).astype(BF)
-            qn = jnp.transpose(q)
-            qz[h, cols, :] = jnp.concatenate([jnp.zeros_like(qn), qn], axis=1).astype(BF)
-            acc[h, cols, :] = jnp.zeros((TILE, 2 * HEAD), F32)
+            acc[h, :, cols] = jnp.zeros((2 * HEAD, TILE), F32)
         return carry
 
     lax.fori_loop(0, blocks, prepare, 0)
@@ -57,21 +55,24 @@
         qcols = pl.ds(pl.multiple_of(qb * TILE, TILE), TILE)
         segq = segq_ref[:, qcols]
 
-        def scores(kb, tops):
+        def scores(kb, tops, last=False):
             krows = pl.ds(pl.multiple_of(kb * TILE, TILE), TILE)
-            kpos = kb * TILE + lax.broadcasted_iota(jnp.int32, (TILE, TILE), 0)
-            qpos = qb * TILE + lax.broadcasted_iota(jnp.int32, (TILE, TILE), 1)
-            allowed = ((segk_ref[krows, :] == segq) & (kpos <= qpos)) | (kpos == qpos)
+            allowed = segk_ref[krows, :] == segq
+            if last:
+                k, q = (lax.broadcasted_iota(jnp.int32, (TILE, TILE), i) for i in (0, 1))
+                allowed = (allowed & (k < q)) | (k == q)
             out = []
             for h in range(heads):
-                s = dot(kn[h, krows, :], qt[pl.ds(h * HEAD, HEAD), qcols], 1, 0)
+                rows = pl.ds(h * HEAD, HEAD)
+                s = dot(kn[h, krows, :], qt[rows, qcols], 1, 0)
                 s = jnp.where(allowed, s, -1e30)
                 s_scr[h, kb - lo] = s
+                p_scr[h, kb - lo] = dot(vn[h, krows, :], g_ref[rows, qcols], 1, 0)
                 out.append(jnp.maximum(tops[h], jnp.max(s, axis=0, keepdims=True)))
             return tuple(out)
 
-        tops = lax.fori_loop(lo, qb + 1, scores,
-                             tuple(jnp.full((1, TILE), -1e30, F32) for _ in range(heads)))
+        tops = lax.fori_loop(lo, qb, scores, tuple(jnp.full((1, TILE), -1e30, F32) for _ in range(heads)))
+        tops = scores(qb, tops, True)
 
         def weights(kb, sums):
             kcols = pl.ds(pl.multiple_of(kb * TILE, TILE), TILE)
@@ -80,43 +81,39 @@
                 e = jnp.exp(s_scr[h, kb - lo] - tops[h])
                 low = e.astype(BF)
                 e_scr[h, kb - lo] = low
-                total, ctx = sums[h]
-                out.append((total + jnp.sum(e, axis=0, keepdims=True),
-                            ctx + dot(vt[pl.ds(h * HEAD, HEAD), kcols], low, 1, 0)))
+                out.append(sums[h] + jnp.sum(e, axis=0, keepdims=True))
+                row[h] += dot(vt[pl.ds(h * HEAD, HEAD), kcols], low, 1, 0)
             return tuple(out)
 
-        sums = lax.fori_loop(lo, qb + 1, weights,
-                             tuple((jnp.zeros((1, TILE), F32), jnp.zeros((HEAD, TILE), F32))
-                                   for _ in range(heads)))
-        gts, gzs, terms = [], [], []
+        row[...] = jnp.zeros_like(row)
+        sums = lax.fori_loop(lo, qb + 1, weights, tuple(jnp.zeros((1, TILE), F32) for _ in range(heads)))
+        gts, terms, scales = [], [], []
         for h in range(heads):
             rows = pl.ds(h * HEAD, HEAD)
-            inverse = 1.0 / sums[h][0]
-            ctx = sums[h][1] * inverse
+            inverse = 1.0 / sums[h]
+            ctx = row[h] * inverse
             ctx_ref[rows, qcols] = ctx.astype(BF)
             g = g_ref[rows, qcols].astype(F32)
-            terms.append(jnp.sum(g * ctx, axis=0, keepdims=True) * inverse)
-            g = g * inverse
-            gts.append(g.astype(BF))
-            gn = jnp.transpose(g)
-            gzs.append(jnp.concatenate([gn, jnp.zeros_like(gn)], axis=1).astype(BF))
-
-        def backward(kb, dqs):
+            terms.append(jnp.sum(g * ctx, axis=0, keepdims=True))
+            scales.append(inverse)
+            gts.append((g * inverse).astype(BF))
+
+        row[...] = jnp.zeros_like(row)
+
+        def backward(kb, carry):
             krows = pl.ds(pl.multiple_of(kb * TILE, TILE), TILE)
-            out = []
             for h in range(heads):
                 low = e_scr[h, kb - lo]
-                dp = dot(vn[h, krows, :], gts[h], 1, 0)
-                ds = (low.astype(F32) * (dp - terms[h])).astype(BF)
-                acc[h, krows, :] += dot(low, gzs[h], 1, 0) + dot(ds, qz[h, qcols, :], 1, 0)
-                out.append(dqs[h] + dot(kt[pl.ds(h * HEAD, HEAD), krows], ds, 1, 0))
-            return tuple(out)
-
-        dqs = lax.fori_loop(lo, qb + 1, backward,
-                            tuple(jnp.zeros((HEAD, TILE), F32) for _ in range(heads)))
+                ds = (low.astype(F32) * ((p_scr[h, kb - lo] - terms[h]) * scales[h])).astype(BF)
+                acc[h, :HEAD, krows] += dot(gts[h], low, 1, 1)
+                acc[h, HEAD:, krows] += dot(qt[pl.ds(h * HEAD, HEAD), qcols], ds, 1, 1)
+                row[h] += dot(kt[pl.ds(h * HEAD, HEAD), krows], ds, 1, 0)
+            return carry
+
+        lax.fori_loop(lo, qb + 1, backward, 0)
         cos, sin = cos_ref[:, qcols], sin_ref[:, qcols]
         for h in range(heads):
-            dlin_ref[0, pl.ds(h * HEAD, HEAD), qcols] = rotate(dqs[h] * 0.125, cos, -sin).astype(BF)
+            dlin_ref[0, pl.ds(h * HEAD, HEAD), qcols] = rotate(row[h] * 0.125, cos, -sin).astype(BF)
         return carry
 
     lax.fori_loop(0, blocks, query_block, 0)
@@ -125,7 +122,7 @@
         cols = pl.ds(pl.multiple_of(c * TILE, TILE), TILE)
         cos, sin = cos_ref[:, cols], sin_ref[:, cols]
         for h in range(heads):
-            both = jnp.transpose(acc[h, cols, :])
+            both = acc[h, :, cols]
             dlin_ref[1, pl.ds(h * HEAD, HEAD), cols] = rotate(both[HEAD:], cos, -sin).astype(BF)
             dlin_ref[2, pl.ds(h * HEAD, HEAD), cols] = both[:HEAD].astype(BF)
         return carry
@@ -158,10 +155,11 @@
                 pltpu.VMEM((wide, length), BF),
                 pltpu.VMEM((heads, length, HEAD), BF),
                 pltpu.VMEM((heads, length, HEAD), BF),
-                pltpu.VMEM((heads, length, 2 * HEAD), BF),
-                pltpu.VMEM((heads, length, 2 * HEAD), F32),
+                pltpu.VMEM((heads, 2 * HEAD, length), F32),
                 pltpu.VMEM((heads, SLOTS, TILE, TILE), F32),
                 pltpu.VMEM((heads, SLOTS, TILE, TILE), BF),
+                pltpu.VMEM((heads, SLOTS, TILE, TILE), F32),
+                pltpu.VMEM((heads, HEAD, TILE), F32),
             ]),
         out_shape=[jax.ShapeDtypeStruct((width, length), BF), jax.ShapeDtypeStruct((3, width, length), BF)],
         compiler_params=pltpu.CompilerParams(vmem_limit_bytes=60 << 20),
@@ -280,13 +278,15 @@
     return d // 2, d % 2, lax.axis_index("tensor")
 
 
-def meet(z, c, t):
+def meet(z, c, t, planes):
     barrier = pltpu.get_barrier_semaphore()
     for h in (0, 1):
         for k in range(4):
             if h or k:
                 pl.semaphore_signal(barrier, 1, device_id=(2 * z + (c ^ h), t ^ k), device_id_type=MESH)
-    pl.semaphore_wait(barrier, 7)
+    for k in planes:
+        pl.semaphore_signal(barrier, 1, device_id=(2 * (z ^ k) + c, t), device_id_type=MESH)
+    pl.semaphore_wait(barrier, 7 + len(planes))
 
 
 def remote(src, dst, send_sem, recv_sem, device):
@@ -355,23 +355,34 @@
 
 
 class Blocks:
-    def __init__(self, own, where, sems, stage, local, halves, z, c, t):
+    def __init__(self, own, where, sems, stage, local, cut, quarter, z, c, t):
         self.own, self.where, self.sems, self.stage, self.local = own, where, sems, stage, local
-        self.halves, self.t, self.d = halves, t, 2 * z + c
+        self.cut, self.quarter, self.t, self.d, self.half = cut, quarter, t, 2 * z + c, z % 2
+
+    def spot(self, k, other=0):
+        return self.cut(self.where(self.t ^ k), self.half ^ other)
 
     def first(self, k):
-        return remote(self.own, self.where(self.t), self.sems.at[k - 1], self.sems.at[3 + k - 1], (self.d, self.t ^ k))
+        return remote(self.cut(self.own, self.half), self.spot(0), self.sems.at[k - 1], self.sems.at[2 + k],
+                      (self.d, self.t ^ k))
 
     def arrival(self, k):
-        spot = self.where(self.t ^ k)
-        return remote(spot, spot, self.sems.at[k - 1], self.sems.at[3 + k - 1], (self.d, self.t ^ k))
+        return remote(self.spot(k), self.spot(k), self.sems.at[k - 1], self.sems.at[2 + k], (self.d, self.t ^ k))
 
     def second(self, k):
-        part = self.halves(self.where(self.t ^ (3 - k)), k - 1)
-        return remote(part, part, self.sems.at[6 + k - 1], self.sems.at[8 + k - 1], (self.d, self.t ^ k))
+        part = self.quarter(self.spot(3 - k), k - 1)
+        return remote(part, part, self.sems.at[5 + k], self.sems.at[7 + k], (self.d, self.t ^ k))
+
+    def last(self, k):
+        part = self.quarter(self.spot(3), k - 1)
+        return remote(part, part, self.sems.at[5 + k], self.sems.at[7 + k], (self.d, self.t ^ k))
+
+    def across(self, k, other=0):
+        return remote(self.spot(k, other), self.spot(k, other), self.sems.at[9 + k], self.sems.at[12 + k],
+                      (self.d ^ 2, self.t))
 
     def start(self):
-        for k in ((1, 2) if self.halves else (1, 2, 3)):
+        for k in ((1, 2) if self.quarter else (1, 2, 3)):
             self.first(k).start()
         pltpu.make_async_copy(self.own, self.stage, self.local.at[0]).start()
 
@@ -380,23 +391,29 @@
         pltpu.make_async_copy(self.stage, self.where(self.t), self.local.at[1]).start()
 
     def relay(self):
-        if self.halves:
+        for k in (1, 2):
+            self.arrival(3 - k).wait_recv()
+            if self.quarter:
+                self.second(k).start()
+            self.across(3 - k).start()
+
+    def pass_on(self):
+        if self.quarter:
             for k in (1, 2):
-                self.arrival(3 - k).wait_recv()
-                self.second(k).start()
+                self.last(k).wait_recv()
+        else:
+            self.arrival(3).wait_recv()
+        self.across(3).start()
 
     def finish(self):
         pltpu.make_async_copy(self.stage, self.where(self.t), self.local.at[1]).wait()
-        if self.halves:
-            for k in (1, 2):
-                part = self.halves(self.where(self.t ^ 3), k - 1)
-                remote(part, part, self.sems.at[6 + k - 1], self.sems.at[8 + k - 1], (self.d, self.t ^ k)).wait_recv()
+        for k in (1, 2, 3):
+            self.across(k, 1).wait_recv()
+            self.across(k).wait_send()
+            if k < 3 or not self.quarter:
                 self.first(k).wait_send()
+            if k < 3 and self.quarter:
                 self.second(k).wait_send()
-        else:
-            for k in (1, 2, 3):
-                self.arrival(k).wait_recv()
-                self.first(k).wait_send()
 
 
 def aligned(i, n):
@@ -407,35 +424,35 @@
                  xf, gf, wqf, wof, ainf, bqf, aof, bof,
                  row_sems, sems, local, xs, gs, wqs, wos, ains, bqs, aos, bos):
     z, c, t = place()
-    meet(z, c, t)
+    meet(z, c, t, (1,))
     at = dict(z=z, c=c, t=t)
     x_rows = Rows(x, xf, row_sems.at[0], xs, local.at[0], **at)
     g_rows = Rows(g, gf, row_sems.at[1], gs, local.at[1], **at)
     qkv = Blocks(wq.at[:, :, aligned(c, 128)], lambda i: wqf.at[:, :, aligned(i, 128)], sems.at[0], wqs, local.at[2],
-                 lambda v, h: v.at[:, pl.ds(h * 512, 512)], **at)
-    into = Blocks(ain, lambda i: ainf.at[:, aligned(i, 32)], sems.at[1], ains, local.at[3], None, **at)
+                 lambda v, h: v.at[:, aligned(h, 512)], lambda v, h: v.at[:, pl.ds(h * 256, 256)], **at)
+    into = Blocks(ain, lambda i: ainf.at[:, aligned(i, 32)], sems.at[1], ains, local.at[3],
+                  lambda v, h: v.at[pl.ds(2 * h, 2)], None, **at)
     second = Blocks(bq.at[:, :, aligned(c, 128)], lambda i: bqf.at[:, :, aligned(i, 128)], sems.at[2], bqs, local.at[4],
-                    None, **at)
+                    lambda v, h: v.at[:, aligned(h, 64)], None, **at)
     out = Blocks(wo.at[aligned(c, 128)], lambda i: wof.at[aligned(i, 128)], sems.at[3], wos, local.at[5],
-                 lambda v, h: v.at[pl.ds(h * 64, 64)], **at)
-    a_out = Blocks(ao.at[aligned(c, 128)], lambda i: aof.at[aligned(i, 128)], sems.at[4], aos, local.at[6], None, **at)
-    b_out = Blocks(bo, lambda i: bof.at[:, aligned(i, 32)], sems.at[5], bos, local.at[7], None, **at)
+                 lambda v, h: v.at[aligned(h, 64)], lambda v, h: v.at[pl.ds(h * 32, 32)], **at)
+    a_out = Blocks(ao.at[aligned(c, 128)], lambda i: aof.at[aligned(i, 128)], sems.at[4], aos, local.at[6],
+                   lambda v, h: v.at[aligned(h, 64)], None, **at)
+    b_out = Blocks(bo, lambda i: bof.at[:, aligned(i, 32)], sems.at[5], bos, local.at[7],
+                   lambda v, h: v.at[pl.ds(h, 1)], None, **at)
     x_rows.start()
-    into.start()
-    second.start()
-    qkv.start()
+    for v in (into, second, qkv, b_out, a_out, out):
+        v.start()
+    g_rows.start()
     x_rows.relay()
-    for v in (into, second, qkv):
+    for v in (into, second, qkv, b_out, a_out, out):
         v.store()
-    g_rows.start()
-    qkv.relay()
-    for v in (b_out, a_out, out):
-        v.start()
+    for v in (into, second, qkv, b_out, a_out, out):
+        v.relay()
+    for v in (into, second, qkv, b_out, a_out, out):
+        v.pass_on()
     g_rows.relay()
-    for v in (b_out, a_out, out):
-        v.store()
-    out.relay()
-    for v in (x_rows, into, second, qkv, g_rows, b_out, a_out, out):
+    for v in (x_rows, into, second, qkv, b_out, a_out, out, g_rows):
         v.finish()
 
 
@@ -450,7 +467,7 @@
         out_shape=[jax.ShapeDtypeStruct(s, BF) for s in shapes],
         scratch_shapes=[
             pltpu.SemaphoreType.DMA((2, 16)),
-            pltpu.SemaphoreType.DMA((6, 10)),
+            pltpu.SemaphoreType.DMA((6, 16)),
             pltpu.SemaphoreType.DMA((8, 2)),
             pltpu.VMEM((256, 1024), BF),
             pltpu.VMEM((256, 1024), BF),
@@ -471,7 +488,7 @@
                 row_sems, share_sems, cross_sems, z_sems, last_sems, norm_sems,
                 sh_in, sh, rbq, rbu, rao, rad, rsh, pbq, pbu, pao, pad, psh, qbq, qbu, qao, qad, qsh, no_in, no_sum):
     z, c, t = place()
-    meet_all(z, c, t)
+    meet(z, c, t, (1, 2))
     d = 2 * z + c
     sibling = (2 * z + (c ^ 1), t)
 
@@ -609,17 +626,6 @@
     for m in (0, 1):
         for h in (0, 1):
             pltpu.make_async_copy(rows.at[0], out.at[m, pl.ds(256 * h, 256)], row_sems.at[4 + 2 * m + h]).wait()
-
-
-def meet_all(z, c, t):
-    barrier = pltpu.get_barrier_semaphore()
-    for h in (0, 1):
-        for k in range(4):
-            if h or k:
-                pl.semaphore_signal(barrier, 1, device_id=(2 * z + (c ^ h), t ^ k), device_id_type=MESH)
-    for k in (1, 2):
-        pl.semaphore_signal(barrier, 1, device_id=(2 * (z ^ k) + c, t), device_id_type=MESH)
-    pl.semaphore_wait(barrier, 9)
 
 
 def back(rows, dbq, dbu, dao, dad, dsh, dno):

time: 531 us -> 494 us (0.930)
  Pallas kernels: 264 us -> 231 us
    pallas_call x1, Pallas kernels: 77.8 us -> 59.8 us  [attention(): pl.pallas_call(functools.partial(attention_kernel, heads), grid_spec=pltp...]
    pallas_call x1, Pallas kernels: 110 us -> 94 us  [front(): pl.pallas_call(front_kernel, in_specs=[anywhere] * 8, out_specs=[anywhere...]
  transfers between devices with their start and end apart: 7 -> 7, of which waited for: 1 -> 1; matrix products, arithmetic and copies ran while one was open for 26% -> 27% of each run, Pallas kernels for 29% -> 28%
where the time goes in v4:
time: 494 us; the launch traced here: 492 us
  Pallas kernels  231 us (47%)
  matrix products  157 us (32%)
  other arithmetic  34.4 us (7%)
  local copies, waits for them, and re-layouts  32.5 us (7%)
  between operations  15 us (3%)
  starting transfers between devices  14 us (3%)
  waiting for transfers between devices  7.95 us (2%)
    dot_general x19, matrix products, dot(): lax.dot_general(a, b, (((ca,), (cb,)), ((), ())), preferred_element_type=...  123 us
    pallas_call x1, Pallas kernels, front(): pl.pallas_call(front_kernel, in_specs=[anywhere] * 8, out_specs=[anywhere...  94 us
    pallas_call x1, Pallas kernels, back(): pl.pallas_call(back_kernel, in_specs=[vmem] * 7, out_specs=[pl.BlockSpec(...  77.6 us
    pallas_call x1, Pallas kernels, attention(): pl.pallas_call(functools.partial(attention_kernel, heads), grid_spec=pltp...  59.8 us
    dot_general x1, matrix products, by_groups(): one = jnp.einsum('ncs,nkc->sk', d_lin, m_qkv, preferred_element_type=F32)  16.5 us
    all_to_all x1, starting transfers between devices, from_group(): got = lax.all_to_all(own, 'tensor', 0, 0, tiled=True).reshape(2, 2, 256, -1)  13.3 us
    unnamed x94, local copies, waits for them, and re-layouts  11.2 us
  transfers between devices with their start and end apart: 7, of which 1 were waited for; matrix products, arithmetic and copies ran while one was open for 27% of the time, Pallas kernels for 28%

profile of v4, /device:TPU:0, one launch (start us, length us, event | category | flops | bytes accessed | tf_op | source)
XLA Modules:
  0.0 492.3 jit_solution(16130232671522418933)
XLA Ops:
  12.9 94.0 %front.1 = (bf16[2048,1024]{1,0:T(8,128)(2,1)}, bf16[2048,1024]{1,0:T(8,128)(2,1)}, bf16[3,1024,512]{2,1,0:T(8,128)(2,1)}, bf16[512,1024]{1,0:T(8,128)(2,1)}, bf...) custom-call(bf16[2,512,1024]{2,1,0:T(8,128)(2,1)} %bitcast.179, ...), custom_call_target="tpu_custom_call" | custom-call | tf_op jit(solution)/shard_map/front/pallas_call | solution.py:463
  114.5 5.5 %fusion.19 = bf16[256,2048]{1,0:T(8,128)(2,1)} fusion(bf16[256,1024]{1,0:T(8,128)(2,1)} %bitcast.188, bf16[2048,1024]{1,0:T(8,128)(2,1)} %get-tuple-element.36), kind=kOutput, calls=%fused_computation.44 | convolution fusion | flops 1074790400 | bytes 5767168 | tf_op jit(solution)/shard_map/dot_general | solution.py:23
  131.8 9.2 %fusion.17.lin_ref = f32[3,512,2048]{2,1,0:T(8,128)} fusion(bf16[3,1024,512]{2,1,0:T(8,128)(2,1)S(1)} %add_convert_fusion.4, bf16[2048,1024]{1,0:T(8,128)(2,1)S(1)} %get-tuple-element.96), kind=kOutput, calls=%fused_computation.37 | convolution fusion | flops 6442450944 | bytes 19922944 | tf_op jit(solution)/shard_map/nkc,sk->ncs/dot_general | solution.py:707
  145.7 59.8 %attention.1 = (bf16[512,2048]{1,0:T(8,128)(2,1)}, bf16[3,512,2048]{2,1,0:T(8,128)(2,1)}) custom-call(s32[8]{0:T(128)} %and_select_fusion.lo_ref, f32[3,512,2048]{2,1,0:T(8,128)} %fusion.17.lin_ref, bf16[512,2048]{1,0:T(8,128)(2,1)} %convolution_convert_fusion.g_ref, f32[8,2048]{1,0:T(8,128)} %get-tuple-element.106.cos_ref, ...), custom_call_target="tpu_custom_call" | custom-call | flops 8053063680 | bytes 27262976 | tf_op jit(solution)/shard_map/attention/pallas_call | solution.py:145
  211.5 3.9 multiply_convert_fusion.1
  225.0 4.9 add_convert_fusion.1
  231.8 14.0 %multiply_convert_fusion = (bf16[2048,2048]{1,0:T(8,128)(2,1)}, f32[2048,2048]{1,0:T(8,128)}) fusion(bf16[2048,1024]{1,0:T(8,128)(2,1)S(1)} %copy-done.6, bf16[1024,2048]{1,0:T(8,128)(2,1)S(1)} %add_convert_fusion.1), kind=kOutput, calls=%fused_computation.7 | convolution fusion | flops 8610906112 | bytes 33554432 | tf_op jit(solution)/shard_map/dot_general | solution.py:23
  245.8 3.8 add_convert_fusion
  249.6 17.5 %fusion.5 = bf16[2048,2048]{1,0:T(8,128)(2,1)} fusion(f32[2048,2048]{1,0:T(8,128)} %get-tuple-element.112, bf16[2048,1024]{1,0:T(8,128)(2,1)} %get-tuple-element.36, bf16[2048,1024]{1,0:T(8,128)(2,1)S(1)} %add_convert_fusion), kind=kOutput, calls=%fused_computation.6 | convolution fusion | flops 8631877632 | bytes 33554432 | tf_op jit(solution)/shard_map/dot_general | solution.py:23
  267.2 9.0 %fusion.54 = f32[2048,1024]{1,0:T(8,128)S(1)} fusion(bf16[2048,2048]{1,0:T(8,128)(2,1)S(1)} %bitcast.163, bf16[2048,1024]{1,0:T(8,128)(2,1)S(1)} %add_convert_fusion), kind=kOutput, calls=%fused_computation.134 | convolution fusion | flops 8589934592 | bytes 20971520 | tf_op jit(solution)/shard_map/dot_general | solution.py:23
  276.2 5.9 %convolution_add_fusion = f32[2048,1024]{1,0:T(8,128)} fusion(f32[2048,1024]{1,0:T(8,128)S(1)} %fusion.54, bf16[512,2048]{1,0:T(8,128)(2,1)S(1)} %copy-done.7, bf16[512,1024]{1,0:T(8,128)(2,1)S(1)} %add_convert_fusion.5), kind=kOutput, calls=%fused_computation.39 | convolution fusion | flops 2149580800 | bytes 19922944 | tf_op jit(solution)/shard_map/dot_general | solution.py:23
  282.2 14.9 %fusion.55 = f32[2048,1024]{1,0:T(8,128)} fusion(bf16[2048,2048]{1,0:T(8,128)(2,1)} %fusion.5, bf16[1024,2048]{1,0:T(8,128)(2,1)} %copy-done.39), kind=kOutput, calls=%fused_computation.135 | convolution fusion | flops 8589934592 | bytes 20971520 | tf_op jit(solution)/shard_map/dot_general | solution.py:23
  297.1 16.5 %fusion.10 = (f32[1024]{0:T(1024)S(1)}, f32[1024]{0:T(1024)S(1)}, f32[1024]{0:T(1024)S(1)}, f32[1024]{0:T(1024)S(1)}, f32[2048,1024]{1,0:T(8,128)}, /*index=5*/f32[2048,1024]{1,0:T(8,128)}) fusion(bf16[2048,1024]{1,0:T(8,128)(2,1)S(1)} %copy-done.4, f32[2048]{0:T(1024)S(1)} %add_rsqrt_fusion, f32[2048]{0:T(1024)S(1)} %broadcast_multiply_fusion, ...), kind=kOutput, calls=%fused_computation.18 | convolution fusion | flops 6467612672 | bytes 38838272 | tf_op jit(solution)/shard_map/ncs,nkc->sk/dot_general | solution.py:726
  316.2 3.8 fusion.23
  321.2 6.5 %convolution_convert_fusion.2 = bf16[128,2048]{1,0:T(8,128)(2,1)S(1)} fusion(bf16[2048,2048]{1,0:T(8,128)(2,1)} %get-tuple-element.111, bf16[2048,1152]{1,0:T(8,128)(2,1)} %all-gather.4.cloned.1.call-done), kind=kOutput, calls=%fused_computation.47 | convolution fusion | flops 1074003968 | bytes 9437184 | tf_op jit(solution)/shard_map/dot_general | solution.py:23
  327.7 8.3 %convolution_convert_fusion.7 = bf16[128,1024]{1,0:T(8,128)(2,1)S(1)} fusion(bf16[2048,1024]{1,0:T(8,128)(2,1)} %get-tuple-element.97, bf16[2048,2048]{1,0:T(8,128)(2,1)} %fusion.5, bf16[128,512]{1,0:T(8,128)(2,1)} %copy-done.24, bf16[128,512]{1,0:T(8,128)(2,1)} %copy-done.25, bf16[128,512]{1,0:T(8,128)(2,1)} %copy-done.26, ...), kind=kOutput, calls=%fused_computation.63 | convolution fusion | flops 1613365248 | bytes 13369344 | tf_op jit(solution)/shard_map/dot_general | solution.py:23
  340.9 5.3 %fusion.16 = bf16[4,256,1024]{2,1,0:T(8,128)(2,1)} fusion(bf16[4,256,1024]{2,1,0:T(8,128)(2,1)} %collective-permute-done.1, f32[4,2,256,1024]{3,2,1,0:T(8,128)} %bitcast.166, s32[]{:T(128)S(6)} %select_n.99, bf16[4,2,256,1024]{3,2,1,0:T(8,128)(2,1)S(1)} %bitcast.164), kind=kLoop, calls=%fused_computation.36 | loop fusion | flops 5242880 | bytes 10485764 | tf_op jit(solution)/shard_map/convert_element_type | solution.py:724
  346.3 13.3 %all-to-all-start = ((bf16[4,256,1024]{2,1,0:T(8,128)(2,1)}), bf16[4,256,1024]{2,1,0:T(8,128)(2,1)S(1)}, u32[]{:S(2)}, u32[]{:S(2)}) async-start(bf16[4,256,1024]{2,1,0:T(8,128)(2,1)} %fusion.16), calls=%async_computation | async-start | bytes 4194304 | tf_op jit(solution)/shard_map/all_to_all | solution.py:672
  359.6 5.4 %convolution_convert_fusion.3.dad = bf16[128,2048]{1,0:T(8,128)(2,1)} fusion(bf16[2048,2048]{1,0:T(8,128)(2,1)} %get-tuple-element.111, bf16[256,2048]{1,0:T(8,128)(2,1)S(1)} %copy-done.15), kind=kOutput, calls=%fused_computation.48 | convolution fusion | flops 1074003968 | bytes 9437184 | tf_op jit(solution)/shard_map/dot_general | solution.py:23
  365.0 8.2 %fusion.20.dbu = bf16[128,2048]{1,0:T(8,128)(2,1)} fusion(bf16[2048,2048]{1,0:T(8,128)(2,1)} %fusion.5, bf16[2048,1024]{1,0:T(8,128)(2,1)} %get-tuple-element.97, bf16[4,128,1024]{2,1,0:T(8,128)(2,1)} %get-tuple-element.31), kind=kOutput, calls=%fused_computation.49 | convolution fusion | flops 1611399168 | bytes 13369344 | tf_op jit(solution)/shard_map/dot_general | solution.py:23
  373.2 4.9 fusion.26
  378.1 7.4 %all-to-all-done = bf16[4,256,1024]{2,1,0:T(8,128)(2,1)S(1)} async-done(((bf16[4,256,1024]{2,1,0:T(8,128)(2,1)}), bf16[4,256,1024]{2,1,0:T(8,128)(2,1)S(1)}, u32[]{:S(2)}, u32[]{:S(2)}) %all-to-all-start) | async-done | bytes 2097184 | tf_op jit(solution)/shard_map/all_to_all | solution.py:672
  388.0 5.7 %fusion.15.rows = bf16[4,256,1024]{2,1,0:T(8,128)(2,1)} fusion(f32[4,2,256,1024]{3,2,1,0:T(8,128)} %bitcast.173, s32[]{:T(128)S(6)} %select_n.99, f32[4,256]{1,0:T(4,128)S(1)} %bitcast.192, f32[4,256]{1,0:T(4,128)S(1)} %get-tuple-element.113, f32[4,256]{1,0:T(4,128)S(1)} %get-tuple-element.114, bf16[4,2,256,1024]{3,2,1,0:T(8,128)(2,1)S(1)} %bitcast.184, ...), kind=kLoop, calls=%fused_computation.31 | loop fusion | flops 9437184 | bytes 14692356 | tf_op jit(solution)/shard_map/convert_element_type | solution.py:748
  393.7 77.6 %back.1 = (bf16[2,512,1024]{2,1,0:T(8,128)(2,1)}, f32[3,128,256]{2,1,0:T(8,128)}, f32[128,1024]{1,0:T(8,128)}, f32[256,128]{1,0:T(8,128)}, f32[128,1024]{1,0:T(8...) custom-call(bf16[4,256,1024]{2,1,0:T(8,128)(2,1)} %fusion.15.rows, bf16[3,128,512]{2,1,0:T(8,128)(2,1)} %fusion.25.dbq, ...), custom_call_target="tpu_custom_call" | custom-call | tf_op jit(solution)/shard_map/back/pallas_call | solution.py:636
  (159 shorter events, 72.0 us)
Async XLA Ops:
  7.2 214.0 %all-gather.6.cloned.1.call-start = ((), (), s32[]{:S(2)}) async-start(), calls=%async_computation.2 | async-start | bytes 5898240 | tf_op jit(solution)/shard_map/all_gather | solution.py:690
  12.9 94.1 %copy-start.27 = (s32[2,1,2048]{2,1,0:T(1,128)S(1)}, s32[2,1,2048]{2,1,0:T(1,128)}, u32[]{:S(2)}) copy-start(s32[2,1,2048]{2,1,0:T(1,128)} %param.19) | copy-start | bytes 49156
  12.9 94.1 %copy-start.28 = (s32[2,1,2048]{2,1,0:T(1,128)S(1)}, s32[2,1,2048]{2,1,0:T(1,128)}, u32[]{:S(2)}) copy-start(s32[2,1,2048]{2,1,0:T(1,128)} %param.18) | copy-start | bytes 49156
  107.0 138.9 %all-gather.4.cloned.1.call-start = ((), (), s32[]{:S(2)}) async-start(), calls=%async_computation.1 | async-start | bytes 5898240 | tf_op jit(solution)/shard_map/all_gather | solution.py:691
  107.1 34.6 %collective-permute-start = (s32[2,2,2048]{2,1,0:T(2,128)S(1)}, s32[2,2,2048]{2,1,0:T(2,128)S(1)}, u32[]{:S(2)}, u32[]{:S(2)}) collective-permute-start(s32[2,2,2048]{2,1,0:T(2,128)S(1)} %pad_add_fusion), channel_id=1, source_target_pairs={{0,4},{4,0},{8,12},{12,8},{16,20},{20,16},{24,28},{28,24},{1,5},{5... | collective-permute-start | bytes 98312 | tf_op jit(solution)/shard_map/ppermute | solution.py:660
  110.7 14.2 %copy-start.30 = (f32[1,1024]{1,0:T(1,128)}, f32[1,1024]{1,0:T(1,128)S(1)}, u32[]{:S(2)}) copy-start(f32[1,1024]{1,0:T(1,128)S(1)} %get-tuple-element.107) | copy-start | bytes 12292
  110.8 14.2 %copy-start.32 = (f32[1,1024]{1,0:T(1,128)}, f32[1,1024]{1,0:T(1,128)S(1)}, u32[]{:S(2)}) copy-start(f32[1,1024]{1,0:T(1,128)S(1)} %get-tuple-element.108) | copy-start | bytes 12292
  113.0 7.1 %copy-start.11 = (bf16[2048,1024]{1,0:T(8,128)(2,1)S(1)}, bf16[2048,1024]{1,0:T(8,128)(2,1)}, u32[]{:S(2)}) copy-start(bf16[2048,1024]{1,0:T(8,128)(2,1)} %get-tuple-element.36) | copy-start | bytes 12582916
  205.5 10.0 %slice-start.2 = ((s8[6291456]{0:T(1024)(128)(4,1)}), s8[4194304]{0:T(1024)(128)(4,1)S(1)}, s32[]{:S(2)}) async-start(s8[6291456]{0:T(1024)(128)(4,1)} %bitcast.167), calls=%async_computation.5 | async-start | bytes 8388608
  231.8 14.0 %copy-start.22 = (bf16[2,128,1024]{2,1,0:T(8,128)(2,1)S(1)}, bf16[2,128,1024]{2,1,0:T(8,128)(2,1)}, u32[]{:S(2)}) copy-start(bf16[2,128,1024]{2,1,0:T(8,128)(2,1)} %get-tuple-element.35) | copy-start | bytes 1572868
  245.8 21.3 %slice-start = ((s8[8388608]{0:T(1024)(128)(4,1)}), s8[4194304]{0:T(1024)(128)(4,1)S(1)}, s32[]{:S(2)}) async-start(s8[8388608]{0:T(1024)(128)(4,1)} %bitcast.162), calls=%async_computation.3 | async-start | bytes 8388608
  249.6 17.6 %slice-start.1 = ((s8[8388608]{0:T(1024)(128)(4,1)}), s8[4194304]{0:T(1024)(128)(4,1)S(1)}, s32[]{:S(2)}) async-start(s8[8388608]{0:T(1024)(128)(4,1)} %bitcast.162), calls=%async_computation.4 | async-start | bytes 8388608
  267.2 9.0 %copy-start.7 = (bf16[512,2048]{1,0:T(8,128)(2,1)S(1)}, bf16[512,2048]{1,0:T(8,128)(2,1)}, u32[]{:S(2)}) copy-start(bf16[512,2048]{1,0:T(8,128)(2,1)} %get-tuple-element.37) | copy-start | bytes 6291460
  282.2 14.9 %copy-start.4 = (bf16[2048,1024]{1,0:T(8,128)(2,1)S(1)}, bf16[2048,1024]{1,0:T(8,128)(2,1)}, u32[]{:S(2)}) copy-start(bf16[2048,1024]{1,0:T(8,128)(2,1)} %get-tuple-element.29) | copy-start | bytes 12582916
  282.2 14.9 %copy-start.31 = (f32[1,1024]{1,0:T(1,128)S(1)}, f32[1,1024]{1,0:T(1,128)}, u32[]{:S(2)}) copy-start(f32[1,1024]{1,0:T(1,128)} %copy-done.30) | copy-start | bytes 12292
  282.2 14.9 %copy-start.33 = (f32[1,1024]{1,0:T(1,128)S(1)}, f32[1,1024]{1,0:T(1,128)}, u32[]{:S(2)}) copy-start(f32[1,1024]{1,0:T(1,128)} %copy-done.32) | copy-start | bytes 12292
  282.2 14.9 %copy-start.38 = (bf16[3,1024,512]{2,1,0:T(8,128)(2,1)S(1)}, bf16[3,1024,512]{2,1,0:T(8,128)(2,1)}, u32[]{:S(2)}) copy-start(bf16[3,1024,512]{2,1,0:T(8,128)(2,1)} %copy-done.37) | copy-start | bytes 9437188
  316.1 24.8 %collective-permute-start.1 = (bf16[4,256,1024]{2,1,0:T(8,128)(2,1)S(1)}, bf16[4,256,1024]{2,1,0:T(8,128)(2,1)}, u32[]{:S(2)}, u32[]{:S(2)}) collective-permute-start(bf16[4,256,1024]{2,1,0:T(8,128)(2,1)S(1)} %fusion.22), channel_id=1, source_target_pairs={{0,4},{4,0},{8,12},{12,8},{16,20},{20,16},{24,28},{28,24},{1,5},{5... | collective-permute-start | bytes 6291464 | tf_op jit(solution)/shard_map/ppermute | solution.py:660
  320.1 53.1 %collective-permute-start.3 = (bf16[4,256,1024]{2,1,0:T(8,128)(2,1)}, bf16[4,256,1024]{2,1,0:T(8,128)(2,1)}, u32[]{:S(2)}, u32[]{:S(2)}) collective-permute-start(bf16[4,256,1024]{2,1,0:T(8,128)(2,1)} %fusion.23), channel_id=1, source_target_pairs={{0,4},{4,0},{8,12},{12,8},{16,20},{20,16},{24,28},{28,24},{1,5},{5... | collective-permute-start | bytes 6291464 | tf_op jit(solution)/shard_map/ppermute | solution.py:660
  327.7 8.3 %copy-start.18 = (bf16[128,2048]{1,0:T(8,128)(2,1)S(1)}, bf16[128,2048]{1,0:T(8,128)(2,1)}, u32[]{:S(2)}) copy-start(bf16[128,2048]{1,0:T(8,128)(2,1)} %convolution_convert_fusion.4) | copy-start | bytes 1572868
  346.3 13.3 %copy-start.15 = (bf16[256,2048]{1,0:T(8,128)(2,1)S(1)}, bf16[256,2048]{1,0:T(8,128)(2,1)}, u32[]{:S(2)}) copy-start(bf16[256,2048]{1,0:T(8,128)(2,1)} %fusion.19) | copy-start | bytes 3145732
  346.3 39.2 %all-to-all-start = ((bf16[4,256,1024]{2,1,0:T(8,128)(2,1)}), bf16[4,256,1024]{2,1,0:T(8,128)(2,1)S(1)}, u32[]{:S(2)}, u32[]{:S(2)}) async-start(bf16[4,256,1024]{2,1,0:T(8,128)(2,1)} %fusion.16), calls=%async_computation | async-start | bytes 4194304 | tf_op jit(solution)/shard_map/all_to_all | solution.py:672
  378.1 8.6 %copy-start.29 = (f32[4,1,256,1]{2,0,1,3:T(4,128)S(1)}, f32[4,1,256,1]{2,0,1,3:T(4,128)}, u32[]{:S(2)}) copy-start(f32[4,1,256,1]{2,0,1,3:T(4,128)} %copy.62) | copy-start | bytes 12292
  386.7 91.7 %collective-permute-start.2 = (bf16[2,256,1024]{2,1,0:T(8,128)(2,1)}, bf16[2,256,1024]{2,1,0:T(8,128)(2,1)}, u32[]{:S(2)}, u32[]{:S(2)}) collective-permute-start(bf16[2,256,1024]{2,1,0:T(8,128)(2,1)} %get-tuple-element.99), channel_id=1, source_target_pairs={{0,4},{4,0},{8,12},{12,8},{16,20},{20,16},{24,28},{28,24},{1,5},{5... | collective-permute-start | bytes 3145736 | tf_op jit(solution)/shard_map/ppermute | solution.py:660
  (27 other events, 111.8 us)
Sparse Core Ops, SparseCore 0:
  107.1 56.9 all-gather.5
  165.9 56.9 all-gather.3

commit v5 on v4

--- a/solution.py
+++ b/solution.py
@@ -483,61 +483,47 @@
     )(x, g, wq, wo, ain, bq, ao, bo)
 
 
-def back_kernel(rows, dbq, dbu, dao, dad, dsh, dno,
+def back_kernel(dl, dp, mq, mu, xf, gf, gain, dbq, dbu, dao, dad, dsh,
                 out, obq, obu, oao, oad, osh, ono,
-                row_sems, share_sems, cross_sems, z_sems, last_sems, norm_sems,
-                sh_in, sh, rbq, rbu, rao, rad, rsh, pbq, pbu, pao, pad, psh, qbq, qbu, qao, qad, qsh, no_in, no_sum):
+                row_sems, share_sems, cross_sems, z_sems, last_sems, norm_sems, local, weight_sems,
+                sh_in, sh, rbq, rbu, rao, rad, rsh, pbq, pbu, pao, pad, psh, qbq, qbu, qao, qad, qsh,
+                no_plane, no_z, no_own, no_mid, wq, wu, dlb, dpb, xb, gb, dlt, one, two, std, inv, sends, gets, rows):
     z, c, t = place()
-    meet(z, c, t, (1, 2))
     d = 2 * z + c
     sibling = (2 * z + (c ^ 1), t)
 
+    def first_row(j):
+        return (t ^ (j % 4)) * 512 + ((c + 1 + j // 4) % 2) * 256
+
+    def loads(j):
+        n = j % 2
+        at = pl.ds(pl.multiple_of(first_row(j), 256), 256)
+        return [pltpu.make_async_copy(v, w.at[n], local.at[i, n]) for i, (v, w) in enumerate((
+            (dl.at[:, :, at], dlb), (dp.at[at], dpb), (xf.at[at], xb), (gf.at[at], gb)))]
+
+    weights = (pltpu.make_async_copy(mq, wq, weight_sems.at[0]), pltpu.make_async_copy(mu, wu, weight_sems.at[1]))
+    for v in loads(0):
+        v.start()
+    for v in weights:
+        v.start()
+    meet(z, c, t, (1, 2, 3))
+
     home = t % 2
-    local = home == c
-    spot = aligned(c, 256)
+    local_row = home == c
+    slot = (t // 2) * 2 + c
 
     def row(k):
-        return remote(rows.at[t ^ k], out.at[t // 2, spot], row_sems.at[k], row_sems.at[4 + (t // 2) * 2 + c],
+        return remote(rows.at[k], out.at[t // 2, aligned(c, 256)], row_sems.at[k], row_sems.at[4 + slot],
                       (2 * z + home, t ^ k))
 
     def own_row():
-        return pltpu.make_async_copy(rows.at[t], out.at[t // 2, spot], row_sems.at[4 + (t // 2) * 2 + c])
-
-    @pl.when(local)
-    def _():
-        own_row().start()
-
-    @pl.when(jnp.logical_not(local))
-    def _():
-        row(0).start()
-
-    for k in (1, 2, 3):
-        row(k).start()
-
-    peers = (sibling, (d, t ^ 1), (d, t ^ 2), (d ^ 2, t), (d ^ 4, t))
-
-    def norm(i):
-        return remote(dno if i == 0 else no_sum.at[i - 1], no_in.at[i], norm_sems.at[0, i], norm_sems.at[1, i], peers[i])
-
-    def norm_next(i):
-        norm(i).wait_recv()
-        total = (dno[...] if i == 0 else no_sum[i - 1]) + no_in[i]
-        if i < 4:
-            no_sum[i] = total
-            norm(i + 1).start()
-        else:
-            ono[...] = total
-
-    norm(0).start()
+        return pltpu.make_async_copy(rows.at[0], out.at[t // 2, aligned(c, 256)], row_sems.at[4 + slot])
+
+    def give(k):
+        return remote(sends.at[k], gets.at[k], row_sems.at[8 + k], row_sems.at[12 + k], sibling)
 
     def share():
         return remote(dsh.at[:, :, aligned(c ^ 1, 512)], sh_in, share_sems.at[0], share_sems.at[1], sibling)
-
-    share().start()
-    share().wait_recv()
-    norm_next(0)
-    for i in range(6):
-        sh[i] = (dsh[i, :, aligned(c, 512)].astype(F32) + sh_in[i].astype(F32)).astype(BF)
 
     def parts(j):
         return (dbq.at[:, :, aligned(j, 128)], dbu.at[:, aligned(j, 512)], dao.at[aligned(j, 128)],
@@ -547,12 +533,6 @@
 
     def cross(k, i):
         return remote(parts(t ^ k)[i], got[i].at[k - 1], cross_sems.at[0, k - 1, i], cross_sems.at[1, k - 1, i], (d, t ^ k))
-
-    for k in (1, 2, 3):
-        for i in range(5):
-            cross(k, i).start()
-    norm_next(1)
-    norm_next(2)
 
     sums = (pbq, pbu, pao, pad, psh)
     halves = (qbq, qbu, qao, qad, qsh)
@@ -576,23 +556,6 @@
         dst = sums[i].at[2] if step == 2 else halves[i].at[step]
         return remote(half(dst, i, j), half(dst, i, j), z_sems.at[0, step, i], z_sems.at[1, step, i], (d, t ^ 1))
 
-    for i in range(5):
-        for k in (1, 2, 3):
-            cross(k, i).wait_recv()
-        total = parts(t)[i][...].astype(F32)
-        for k in (0, 1, 2):
-            total = total + got[i][k].astype(F32)
-        sums[i][0] = total.astype(BF)
-        along(0, i).start()
-    norm_next(3)
-    for step in (0, 1):
-        for i in range(5):
-            arrived(step, i).wait_recv()
-            mine, other = half(sums[i].at[step], i, low), half(halves[i].at[step], i, low)
-            half(sums[i].at[step + 1], i, low)[...] = (mine[...].astype(F32) + other[...].astype(F32)).astype(BF)
-            along(step + 1, i).start()
-        if step == 0:
-            norm_next(4)
     result = (obq.at[:, :, aligned(c, 128)], obu.at[:, aligned(c, 512)], oao.at[aligned(c, 128)],
               oad.at[:, aligned(c, 512)], osh.at[:, :, aligned(c, 512)])
     theirs = (obq.at[:, :, aligned(c ^ 1, 128)], obu.at[:, aligned(c ^ 1, 512)], oao.at[aligned(c ^ 1, 128)],
@@ -601,11 +564,144 @@
     def last(i):
         return remote(result[i], result[i], last_sems.at[0, i], last_sems.at[1, i], sibling)
 
+    share().start()
+    for v in weights:
+        v.wait()
+    no_own[...] = jnp.zeros_like(no_own)
+
+    def block(j, carry):
+        n, k = j % 2, j % 4
+        for v in loads(j):
+            v.wait()
+
+        @pl.when(j < 7)
+        def _():
+            for v in loads(j + 1):
+                v.start()
+
+        for i in range(3):
+            dlt[i] = jnp.transpose(dlb[n, i])
+
+        def columns(m, carry):
+            at = aligned(m, 256)
+            one[:, at] = (dot(dlt[0], wq[0, at, :], 1, 1) + dot(dlt[1], wq[1, at, :], 1, 1)
+                          + dot(dlt[2], wq[2, at, :], 1, 1))
+            two[:, at] = dot(dpb[n], wu[at, :], 1, 1)
+            return carry
+
+        lax.fori_loop(0, 4, columns, 0)
+
+        def norms(r, carry):
+            at = aligned(r, 32)
+            v = xb[n, at, :].astype(F32)
+            v = v - jnp.mean(v, axis=1, keepdims=True)
+            inverse = lax.rsqrt(jnp.mean(v * v, axis=1, keepdims=True) + EPSILON)
+            v = v * inverse
+            a, b = one[at, :], two[at, :]
+            for i, w in enumerate((a * v, b * v, a, b)):
+                no_own[i] += jnp.sum(w.reshape(4, 8, 1024), axis=0)
+            one[at, :] = gain[0:1, :] * a + gain[1:2, :] * b
+            std[at, :] = v
+            inv[at, :] = inverse
+            return carry
+
+        lax.fori_loop(0, 8, norms, 0)
+
+        @pl.when(j < 4)
+        def _():
+            sends[k] = one[...].astype(BF)
+            give(k).start()
+
+        @pl.when(j >= 4)
+        def _():
+            give(k).wait_recv()
+
+            def finish(r, carry):
+                at = aligned(r, 32)
+                v, own = one[at, :] + gets[k, at, :].astype(F32), std[at, :]
+                v = v - jnp.mean(v, axis=1, keepdims=True) - own * jnp.mean(v * own, axis=1, keepdims=True)
+                rows[k, at, :] = (gb[n, at, :].astype(F32) + v * inv[at, :]).astype(BF)
+                return carry
+
+            lax.fori_loop(0, 8, finish, 0)
+            here = (k == 0) & local_row
+
+            @pl.when(here)
+            def _():
+                own_row().start()
+
+            @pl.when(jnp.logical_not(here))
+            def _():
+                row(k).start()
+
+        @pl.when(j == 0)
+        def _():
+            share().wait_recv()
+            for i in range(6):
+                sh[i] = (dsh[i, :, aligned(c, 512)].astype(F32) + sh_in[i].astype(F32)).astype(BF)
+            for i in range(5):
+                for p in (1, 2, 3):
+                    cross(p, i).start()
+
+        @pl.when(j == 3)
+        def _():
+            for i in range(5):
+                for p in (1, 2, 3):
+                    cross(p, i).wait_recv()
+                total = parts(t)[i][...].astype(F32)
+                for p in (0, 1, 2):
+                    total = total + got[i][p].astype(F32)
+                sums[i][0] = total.astype(BF)
+                along(0, i).start()
+
+        for step, when in ((0, 4), (1, 6)):
+            @pl.when(j == when)
+            def _():
+                for i in range(5):
+                    arrived(step, i).wait_recv()
+                    mine, other = half(sums[i].at[step], i, low), half(halves[i].at[step], i, low)
+                    half(sums[i].at[step + 1], i, low)[...] = (mine[...].astype(F32) + other[...].astype(F32)).astype(BF)
+                    along(step + 1, i).start()
+
+        return carry
+
+    lax.fori_loop(0, 8, block, 0)
+
+    plane = [(h, k) for h in (0, 1) for k in range(4) if h or k]
+
+    def norm(n):
+        h, k = plane[n]
+        return remote(no_mid.at[0], no_plane.at[2 * t + c], norm_sems.at[0, n], norm_sems.at[1, n], (2 * z + (c ^ h), t ^ k))
+
+    def norm_from(n):
+        h, k = plane[n]
+        spot = no_plane.at[2 * (t ^ k) + (c ^ h)]
+        return remote(spot, spot, norm_sems.at[0, n], norm_sems.at[1, n], sibling)
+
+    def norm_z(k):
+        return remote(no_mid.at[1], no_z.at[z], norm_sems.at[0, 6 + k], norm_sems.at[1, 6 + k], (d ^ (2 * k), t))
+
+    def norm_z_from(k):
+        return remote(no_z.at[z ^ k], no_z.at[z ^ k], norm_sems.at[0, 6 + k], norm_sems.at[1, 6 + k], sibling)
+
+    own = jnp.sum(no_own[...], axis=1)
+    no_mid[0] = own
+    for n in range(7):
+        norm(n).start()
+    no_plane[2 * t + c] = own
     for i in range(5):
         arrived(2, i).wait_recv()
         result[i][...] = sums[i][2].astype(F32)
         last(i).start()
-
+    for n in range(7):
+        norm_from(n).wait_recv()
+    own = no_plane[0]
+    for n in range(1, 8):
+        own = own + no_plane[n]
+    no_mid[1] = own
+    for k in (1, 2, 3):
+        norm_z(k).start()
+    no_z[z] = own
     for i in range(5):
         remote(theirs[i], theirs[i], last_sems.at[0, i], last_sems.at[1, i], sibling).wait_recv()
         last(i).wait_send()
@@ -614,12 +710,18 @@
         for k in (1, 2, 3):
             cross(k, i).wait_send()
     share().wait_send()
-    for i in range(5):
-        norm(i).wait_send()
     for k in (1, 2, 3):
+        norm_z_from(k).wait_recv()
+    ono[...] = ((no_z[0] + no_z[1]) + no_z[2]) + no_z[3]
+    for n in range(7):
+        norm(n).wait_send()
+    for k in (1, 2, 3):
+        norm_z(k).wait_send()
         row(k).wait_send()
-
-    @pl.when(jnp.logical_not(local))
+    for k in range(4):
+        give(k).wait_send()
+
+    @pl.when(jnp.logical_not(local_row))
     def _():
         row(0).wait_send()
 
@@ -628,32 +730,51 @@
             pltpu.make_async_copy(rows.at[0], out.at[m, pl.ds(256 * h, 256)], row_sems.at[4 + 2 * m + h]).wait()
 
 
-def back(rows, dbq, dbu, dao, dad, dsh, dno):
+def back(dl, dp, mq, mu, xf, gf, gain, dbq, dbu, dao, dad, dsh):
     vmem = pl.BlockSpec(memory_space=pltpu.VMEM)
+    anywhere = pl.BlockSpec(memory_space=pl.ANY)
     part = [(3, 128, 128), (128, 512), (128, 128), (128, 512), (6, 32, 512)]
     outs = [((2, 512, 1024), BF), ((3, 128, 256), F32), ((128, 1024), F32), ((256, 128), F32), ((128, 1024), F32),
             ((6, 32, 1024), F32), ((4, 1024), F32)]
     return pl.pallas_call(
         back_kernel,
-        in_specs=[vmem] * 7,
-        out_specs=[pl.BlockSpec(memory_space=pl.ANY)] + [vmem] * 6,
+        in_specs=[anywhere] * 6 + [vmem] * 6,
+        out_specs=[anywhere] + [vmem] * 6,
         out_shape=[jax.ShapeDtypeStruct(s, d) for s, d in outs],
         scratch_shapes=[
-            pltpu.SemaphoreType.DMA((8,)),
+            pltpu.SemaphoreType.DMA((16,)),
             pltpu.SemaphoreType.DMA((2,)),
             pltpu.SemaphoreType.DMA((2, 3, 5)),
             pltpu.SemaphoreType.DMA((2, 3, 5)),
             pltpu.SemaphoreType.DMA((2, 5)),
-            pltpu.SemaphoreType.DMA((2, 5)),
+            pltpu.SemaphoreType.DMA((2, 10)),
+            pltpu.SemaphoreType.DMA((4, 2)),
+            pltpu.SemaphoreType.DMA((2,)),
             pltpu.VMEM((6, 128, 512), BF),
             pltpu.VMEM((6, 128, 512), BF),
         ] + [pltpu.VMEM((3,) + s, BF) for s in part + part] + [pltpu.VMEM((2,) + s, BF) for s in part] + [
-            pltpu.VMEM((5, 4, 1024), F32),
+            pltpu.VMEM((8, 4, 1024), F32),
             pltpu.VMEM((4, 4, 1024), F32),
+            pltpu.VMEM((4, 8, 1024), F32),
+            pltpu.VMEM((2, 4, 1024), F32),
+            pltpu.VMEM((3, 1024, 512), BF),
+            pltpu.VMEM((1024, 2048), BF),
+            pltpu.VMEM((2, 3, 512, 256), BF),
+            pltpu.VMEM((2, 256, 2048), BF),
+            pltpu.VMEM((2, 256, 1024), BF),
+            pltpu.VMEM((2, 256, 1024), BF),
+            pltpu.VMEM((3, 256, 512), BF),
+            pltpu.VMEM((256, 1024), F32),
+            pltpu.VMEM((256, 1024), F32),
+            pltpu.VMEM((256, 1024), F32),
+            pltpu.VMEM((256, 1), F32),
+            pltpu.VMEM((4, 256, 1024), BF),
+            pltpu.VMEM((4, 256, 1024), BF),
+            pltpu.VMEM((4, 256, 1024), BF),
         ],
-        compiler_params=pltpu.CompilerParams(collective_id=1, has_side_effects=True),
+        compiler_params=pltpu.CompilerParams(collective_id=1, has_side_effects=True, vmem_limit_bytes=56 << 20),
         name="back",
-    )(rows, dbq, dbu, dao, dad, dsh, dno)
+    )(dl, dp, mq, mu, xf, gf, gain, dbq, dbu, dao, dad, dsh)
 
 
 def swap(v, k=1):
@@ -701,7 +822,7 @@
     a_three = a_full[:3].reshape(3 * RANK, 1024)
     b_both = b_full.reshape(2 * RANK, 1024)
 
-    standard, inverse = normalized(x_full.astype(F32))
+    standard, _ = normalized(x_full.astype(F32))
     n1 = (standard * gain[0] + bias[0]).astype(BF)
     n2 = (standard * gain[1] + bias[1]).astype(BF)
     lin = jnp.einsum("nkc,sk->ncs", m_qkv, n1, preferred_element_type=F32)
@@ -723,18 +844,6 @@
     y = half_rows(x_full, c).astype(F32) + half_rows(part, c) + theirs.astype(F32)
     y = from_group(y.astype(BF), c)
 
-    one = jnp.einsum("ncs,nkc->sk", d_lin, m_qkv, preferred_element_type=F32)
-    two = dot(d_pre, m_up, 1, 1)
-    total = gain[0] * one + gain[1] * two
-    theirs = swap(half_rows(total, 1 - c).astype(BF))
-    total = half_rows(total, c) + theirs.astype(F32)
-    own = half_rows(standard, c)
-    grad = total - jnp.mean(total, axis=-1, keepdims=True)
-    grad = grad - own * jnp.mean(total * own, axis=-1, keepdims=True)
-    grad = half_rows(g_full, c).astype(F32) + grad * half_rows(inverse, c)
-
-    norms = jnp.stack([jnp.sum(one * standard, axis=0), jnp.sum(two * standard, axis=0),
-                       jnp.sum(one, axis=0), jnp.sum(two, axis=0)])
     lo = jnp.concatenate([dot(a_out_all, ctx, 0, 0), dot(a_down_all, hidden, 0, 1)], axis=0).astype(BF)
     d_a_out = dot(ctx, low_grad[:RANK], 1, 1).astype(BF)
     d_a_down = dot(low_grad[RANK:], hidden, 1, 0).astype(BF)
@@ -745,7 +854,7 @@
     shared = jnp.concatenate([dot(back3.reshape(3 * RANK, 2048), n1, 1, 0).astype(BF), dot(back1, n2, 1, 0).astype(BF),
                               (SCALE * dot(lo, g_full, 1, 0)).astype(BF)], axis=0).reshape(6, RANK, 1024)
     grad, r_b_qkv, r_b_up, r_a_out, r_a_down, rest, norms = back(
-        grad.astype(BF), d_b_qkv, d_b_up, d_a_out, d_a_down, shared, norms)
+        d_lin, d_pre, m_qkv, m_up, x_full, g_full, gain, d_b_qkv, d_b_up, d_a_out, d_a_down, shared)
     r_a_in = jnp.swapaxes(rest[:4], 1, 2)
     return (y[:, None], grad[:, None], norms[:2], norms[2:], r_a_in, r_b_qkv, r_b_up, r_a_out, jnp.transpose(r_a_down), rest[4:])
 

time: 494 us -> 450 us (0.911)
  matrix products: 157 us -> 122 us
  Pallas kernels: 231 us -> 245 us
  other arithmetic: 34.4 us -> 20.5 us
  local copies, waits for them, and re-layouts: 32.5 us -> 23.6 us
    dot_general x19 -> x18, matrix products: 123 us -> 105 us  [dot(): lax.dot_general(a, b, (((ca,), (cb,)), ((), ())), preferred_element_type=...]
    dot_general x1 -> x0, matrix products: 16.5 us -> none  [by_groups(): one = jnp.einsum('ncs,nkc->sk', d_lin, m_qkv, preferred_element_type=F32)]
    pallas_call x1, Pallas kernels: 77.6 us -> 91.6 us  [back(): pl.pallas_call(back_kernel, in_specs=[anywhere] * 6 + [vmem] * 6, out_spe...]
    convert_element_type x1 -> x0, other arithmetic: 5.67 us -> none  [by_groups(): grad.astype(BF)]
    unnamed x94 -> x89, local copies, waits for them, and re-layouts: 11.2 us -> 8.38 us
  transfers between devices with their start and end apart: 7 -> 6, of which waited for: 1 -> 1; matrix products, arithmetic and copies ran while one was open for 27% -> 29% of each run, Pallas kernels for 28% -> 34%
where the time goes in v5:
time: 450 us; the launch traced here: 444 us
  Pallas kernels  245 us (54%)
  matrix products  122 us (27%)
  local copies, waits for them, and re-layouts  23.6 us (5%)
  other arithmetic  20.5 us (5%)
  between operations  15.1 us (3%)
  starting transfers between devices  10.9 us (2%)
  waiting for transfers between devices  6.58 us (1%)
    dot_general x18, matrix products, dot(): lax.dot_general(a, b, (((ca,), (cb,)), ((), ())), preferred_element_type=...  105 us
    pallas_call x1, Pallas kernels, front(): pl.pallas_call(front_kernel, in_specs=[anywhere] * 8, out_specs=[anywhere...  94 us
    pallas_call x1, Pallas kernels, back(): pl.pallas_call(back_kernel, in_specs=[anywhere] * 6 + [vmem] * 6, out_spe...  91.6 us
    pallas_call x1, Pallas kernels, attention(): pl.pallas_call(functools.partial(attention_kernel, heads), grid_spec=pltp...  59.5 us
    all_to_all x1, starting transfers between devices, from_group(): got = lax.all_to_all(own, 'tensor', 0, 0, tiled=True).reshape(2, 2, 256, -1)  10.6 us
    dot_general x1, matrix products, by_groups(): lin = jnp.einsum('nkc,sk->ncs', m_qkv, n1, preferred_element_type=F32)  9.27 us
  transfers between devices with their start and end apart: 6, of which 1 were waited for; matrix products, arithmetic and copies ran while one was open for 29% of the time, Pallas kernels for 34%

profile of v5, /device:TPU:0, one launch (start us, length us, event | category | flops | bytes accessed | tf_op | source)
XLA Modules:
  0.0 444.1 jit_solution(10569703492369177514)
XLA Ops:
  12.9 94.0 %front.1 = (bf16[2048,1024]{1,0:T(8,128)(2,1)}, bf16[2048,1024]{1,0:T(8,128)(2,1)}, bf16[3,1024,512]{2,1,0:T(8,128)(2,1)}, bf16[512,1024]{1,0:T(8,128)(2,1)}, bf...) custom-call(bf16[2,512,1024]{2,1,0:T(8,128)(2,1)} %bitcast.118, ...), custom_call_target="tpu_custom_call" | custom-call | tf_op jit(solution)/shard_map/front/pallas_call | solution.py:463
  107.7 3.0 convert_reduce_fusion
  115.9 3.7 convolution_convert_fusion.g_ref
  120.8 3.8 fusion.11
  126.5 9.3 %fusion.16.lin_ref = f32[3,512,2048]{2,1,0:T(8,128)} fusion(bf16[3,1024,512]{2,1,0:T(8,128)(2,1)S(1)} %add_convert_fusion.2.mq, bf16[2048,1024]{1,0:T(8,128)(2,1)S(1)} %get-tuple-element.86), kind=kOutput, calls=%fused_computation.26 | convolution fusion | flops 6442450944 | bytes 19922944 | tf_op jit(solution)/shard_map/nkc,sk->ncs/dot_general | solution.py:828
  139.8 59.5 %attention.1 = (bf16[512,2048]{1,0:T(8,128)(2,1)}, bf16[3,512,2048]{2,1,0:T(8,128)(2,1)}) custom-call(s32[8]{0:T(128)} %and_select_fusion.lo_ref, f32[3,512,2048]{2,1,0:T(8,128)} %fusion.16.lin_ref, bf16[512,2048]{1,0:T(8,128)(2,1)} %convolution_convert_fusion.g_ref, f32[8,2048]{1,0:T(8,128)} %get-tuple-element.96.cos_ref, ...), custom_call_target="tpu_custom_call" | custom-call | flops 8053063680 | bytes 27262976 | tf_op jit(solution)/shard_map/attention/pallas_call | solution.py:145
  199.3 3.0 convolution_convert_fusion.4
  202.3 3.0 convolution_convert_fusion.8.dao
  205.4 3.9 multiply_convert_fusion.1
  209.3 3.0 fusion.23.dbq
  218.8 4.8 %add_convert_fusion.1.mu = bf16[1024,2048]{1,0:T(8,128)(2,1)S(1)} fusion(bf16[1024,512]{1,0:T(8,128)(2,1)S(1)} %get-tuple-element.83, bf16[1024,512]{1,0:T(8,128)(2,1)S(1)} %get-tuple-element.84, bf16[1024,512]{1,0:T(8,128)(2,1)S(1)} %get-tuple-element.85, bf16[1024,512]{1,0:T(8,128)(2,1)S(1)} %get-tuple-element.82, ...), kind=kOutput, calls=%fused_computation.21 | convolution fusion | flops 562036736 | bytes 9175040 | tf_op jit(solution)/shard_map/dot_general | solution.py:23
  225.6 14.1 %multiply_convert_fusion = (bf16[2048,2048]{1,0:T(8,128)(2,1)}, f32[2048,2048]{1,0:T(8,128)}) fusion(bf16[2048,1024]{1,0:T(8,128)(2,1)S(1)} %copy-done.4, bf16[1024,2048]{1,0:T(8,128)(2,1)S(1)} %add_convert_fusion.1.mu), kind=kOutput, calls=%fused_computation.7 | convolution fusion | flops 8610906112 | bytes 33554432 | tf_op jit(solution)/shard_map/dot_general | solution.py:23
  239.7 3.8 add_convert_fusion
  243.5 13.1 %fusion.51 = f32[2048,1024]{1,0:T(8,128)S(1)} fusion(bf16[2048,2048]{1,0:T(8,128)(2,1)} %get-tuple-element.101, bf16[2048,1024]{1,0:T(8,128)(2,1)S(1)} %add_convert_fusion), kind=kOutput, calls=%fused_computation.116 | convolution fusion | flops 8589934592 | bytes 20971520 | tf_op jit(solution)/shard_map/dot_general | solution.py:23
  259.6 4.1 convolution_convert_fusion.2
  263.7 19.5 %fusion.5.dp = bf16[2048,2048]{1,0:T(8,128)(2,1)} fusion(f32[2048,2048]{1,0:T(8,128)} %get-tuple-element.102, bf16[2048,1024]{1,0:T(8,128)(2,1)S(1)} %copy-done.7, bf16[2048,1024]{1,0:T(8,128)(2,1)} %copy-done.37), kind=kOutput, calls=%fused_computation.6 | convolution fusion | flops 8631877632 | bytes 33554432 | tf_op jit(solution)/shard_map/dot_general | solution.py:23
  285.8 10.6 %all-to-all-start = ((bf16[4,256,1024]{2,1,0:T(8,128)(2,1)}), bf16[4,256,1024]{2,1,0:T(8,128)(2,1)S(1)}, u32[]{:S(2)}, u32[]{:S(2)}) async-start(bf16[4,256,1024]{2,1,0:T(8,128)(2,1)} %fusion.15), calls=%async_computation | async-start | bytes 4194304 | tf_op jit(solution)/shard_map/all_to_all | solution.py:793
  296.4 4.2 fusion.22
  300.7 8.2 %fusion.19.dbu = bf16[128,2048]{1,0:T(8,128)(2,1)} fusion(bf16[2048,2048]{1,0:T(8,128)(2,1)} %fusion.5.dp, bf16[2048,1024]{1,0:T(8,128)(2,1)} %get-tuple-element.87, bf16[4,128,1024]{2,1,0:T(8,128)(2,1)} %get-tuple-element.31), kind=kOutput, calls=%fused_computation.38 | convolution fusion | flops 1611399168 | bytes 13369344 | tf_op jit(solution)/shard_map/dot_general | solution.py:23
  308.9 8.0 %convolution_convert_fusion.7 = bf16[128,1024]{1,0:T(8,128)(2,1)S(1)} fusion(bf16[2048,1024]{1,0:T(8,128)(2,1)} %get-tuple-element.87, bf16[2048,2048]{1,0:T(8,128)(2,1)} %fusion.5.dp, bf16[128,512]{1,0:T(8,128)(2,1)S(1)} %copy-done.27, bf16[128,512]{1,0:T(8,128)(2,1)S(1)} %copy-done.29, bf16[128,512]{1,0:T(8,128)(2,1)S(1)} %copy-done.31, ...), kind=kOutput, calls=%fused_computation.51 | convolution fusion | flops 1613365248 | bytes 13369344 | tf_op jit(solution)/shard_map/dot_general | solution.py:23
  316.9 6.0 %all-to-all-done = bf16[4,256,1024]{2,1,0:T(8,128)(2,1)S(1)} async-done(((bf16[4,256,1024]{2,1,0:T(8,128)(2,1)}), bf16[4,256,1024]{2,1,0:T(8,128)(2,1)S(1)}, u32[]{:S(2)}, u32[]{:S(2)}) %all-to-all-start) | async-done | bytes 2097184 | tf_op jit(solution)/shard_map/all_to_all | solution.py:793
  325.8 5.5 %convolution_convert_fusion.3.dad = bf16[128,2048]{1,0:T(8,128)(2,1)} fusion(bf16[2048,2048]{1,0:T(8,128)(2,1)} %get-tuple-element.101, bf16[256,2048]{1,0:T(8,128)(2,1)S(1)} %copy-done.15), kind=kOutput, calls=%fused_computation.37 | convolution fusion | flops 1074003968 | bytes 9437184 | tf_op jit(solution)/shard_map/dot_general | solution.py:23
  331.2 91.6 %back.1 = (bf16[2,512,1024]{2,1,0:T(8,128)(2,1)}, f32[3,128,256]{2,1,0:T(8,128)}, f32[128,1024]{1,0:T(8,128)}, f32[256,128]{1,0:T(8,128)}, f32[128,1024]{1,0:T(8...) custom-call(bf16[3,512,2048]{2,1,0:T(8,128)(2,1)} %get-tuple-element.40.dl, bf16[2048,2048]{1,0:T(8,128)(2,1)} %fusion.5.dp, ...), custom_call_target="tpu_custom_call" | custom-call | tf_op jit(solution)/shard_map/back/pallas_call | solution.py:739
  429.9 3.3 maximum_select_fusion
  (143 shorter events, 46.0 us)
Async XLA Ops:
  7.2 207.8 %all-gather.6.cloned.1.call-start = ((), (), s32[]{:S(2)}) async-start(), calls=%async_computation.2 | async-start | bytes 5898240 | tf_op jit(solution)/shard_map/all_gather | solution.py:811
  12.9 94.1 %copy-start.32 = (s32[2,1,2048]{2,1,0:T(1,128)S(1)}, s32[2,1,2048]{2,1,0:T(1,128)}, u32[]{:S(2)}) copy-start(s32[2,1,2048]{2,1,0:T(1,128)} %param.19) | copy-start | bytes 49156
  12.9 94.1 %copy-start.33 = (s32[2,1,2048]{2,1,0:T(1,128)S(1)}, s32[2,1,2048]{2,1,0:T(1,128)}, u32[]{:S(2)}) copy-start(s32[2,1,2048]{2,1,0:T(1,128)} %param.18) | copy-start | bytes 49156
  106.9 132.8 %all-gather.4.cloned.1.call-start = ((), (), s32[]{:S(2)}) async-start(), calls=%async_computation.1 | async-start | bytes 5898240 | tf_op jit(solution)/shard_map/all_gather | solution.py:812
  107.0 28.8 %collective-permute-start = (s32[2,2,2048]{2,1,0:T(2,128)S(1)}, s32[2,2,2048]{2,1,0:T(2,128)S(1)}, u32[]{:S(2)}, u32[]{:S(2)}) collective-permute-start(s32[2,2,2048]{2,1,0:T(2,128)S(1)} %pad_add_fusion), channel_id=1, source_target_pairs={{0,4},{4,0},{8,12},{12,8},{16,20},{20,16},{24,28},{28,24},{1,5},{5... | collective-permute-start | bytes 98312 | tf_op jit(solution)/shard_map/ppermute | solution.py:781
  120.8 5.6 %copy-start.11 = (bf16[3,1024,512]{2,1,0:T(8,128)(2,1)}, bf16[3,1024,512]{2,1,0:T(8,128)(2,1)S(1)}, u32[]{:S(2)}) copy-start(bf16[3,1024,512]{2,1,0:T(8,128)(2,1)S(1)} %add_convert_fusion.2.mq) | copy-start | bytes 9437188
  199.3 10.0 %slice-start = ((s8[6291456]{0:T(1024)(128)(4,1)}), s8[4194304]{0:T(1024)(128)(4,1)S(1)}, s32[]{:S(2)}) async-start(s8[6291456]{0:T(1024)(128)(4,1)} %bitcast.107), calls=%async_computation.3 | async-start | bytes 8388608
  218.8 6.8 %copy-start.4 = (bf16[2048,1024]{1,0:T(8,128)(2,1)S(1)}, bf16[2048,1024]{1,0:T(8,128)(2,1)}, u32[]{:S(2)}) copy-start(bf16[2048,1024]{1,0:T(8,128)(2,1)} %get-tuple-element.87) | copy-start | bytes 12582916
  225.6 14.1 %copy-start.24 = (bf16[2,128,1024]{2,1,0:T(8,128)(2,1)S(1)}, bf16[2,128,1024]{2,1,0:T(8,128)(2,1)}, u32[]{:S(2)}) copy-start(bf16[2,128,1024]{2,1,0:T(8,128)(2,1)} %get-tuple-element.35) | copy-start | bytes 1572868
  239.7 19.9 %slice-start.2 = ((s8[8388608]{0:T(1024)(128)(4,1)}), s8[4194304]{0:T(1024)(128)(4,1)S(1)}, s32[]{:S(2)}) async-start(s8[8388608]{0:T(1024)(128)(4,1)} %bitcast.109), calls=%async_computation.5 | async-start | bytes 8388608
  243.4 13.1 %copy-start.37 = (bf16[2048,1024]{1,0:T(8,128)(2,1)}, bf16[2048,1024]{1,0:T(8,128)(2,1)S(1)}, u32[]{:S(2)}) copy-start(bf16[2048,1024]{1,0:T(8,128)(2,1)S(1)} %add_convert_fusion) | copy-start | bytes 12582916
  243.4 13.1 %copy-start.5 = (bf16[512,2048]{1,0:T(8,128)(2,1)S(1)}, bf16[512,2048]{1,0:T(8,128)(2,1)}, u32[]{:S(2)}) copy-start(bf16[512,2048]{1,0:T(8,128)(2,1)} %get-tuple-element.37) | copy-start | bytes 6291460
  243.5 16.1 %slice-start.3 = ((s8[8388608]{0:T(1024)(128)(4,1)}), s8[4194304]{0:T(1024)(128)(4,1)S(1)}, s32[]{:S(2)}) async-start(s8[8388608]{0:T(1024)(128)(4,1)} %bitcast.109), calls=%async_computation.6 | async-start | bytes 8388608
  259.5 23.8 %collective-permute-start.1 = (bf16[4,256,1024]{2,1,0:T(8,128)(2,1)S(1)}, bf16[4,256,1024]{2,1,0:T(8,128)(2,1)S(1)}, u32[]{:S(2)}, u32[]{:S(2)}) collective-permute-start(bf16[4,256,1024]{2,1,0:T(8,128)(2,1)S(1)} %fusion.21), channel_id=1, source_target_pairs={{0,4},{4,0},{8,12},{12,8},{16,20},{20,16},{24,28},{28,24},{1,5},{5... | collective-permute-start | bytes 6291464 | tf_op jit(solution)/shard_map/ppermute | solution.py:781
  263.7 19.6 %copy-start.3 = (bf16[2048,1024]{1,0:T(8,128)(2,1)S(1)}, bf16[2048,1024]{1,0:T(8,128)(2,1)}, u32[]{:S(2)}) copy-start(bf16[2048,1024]{1,0:T(8,128)(2,1)} %get-tuple-element.29.xf) | copy-start | bytes 12582916
  285.8 10.6 %copy-start.18 = (bf16[128,2048]{1,0:T(8,128)(2,1)S(1)}, bf16[128,2048]{1,0:T(8,128)(2,1)}, u32[]{:S(2)}) copy-start(bf16[128,2048]{1,0:T(8,128)(2,1)} %convolution_convert_fusion.4) | copy-start | bytes 1572868
  285.8 37.1 %all-to-all-start = ((bf16[4,256,1024]{2,1,0:T(8,128)(2,1)}), bf16[4,256,1024]{2,1,0:T(8,128)(2,1)S(1)}, u32[]{:S(2)}, u32[]{:S(2)}) async-start(bf16[4,256,1024]{2,1,0:T(8,128)(2,1)} %fusion.15), calls=%async_computation | async-start | bytes 4194304 | tf_op jit(solution)/shard_map/all_to_all | solution.py:793
  300.7 8.2 %copy-start.27 = (bf16[128,512]{1,0:T(8,128)(2,1)S(1)}, bf16[128,512]{1,0:T(8,128)(2,1)}, u32[]{:S(2)}) copy-start(bf16[128,512]{1,0:T(8,128)(2,1)} %copy-done.26) | copy-start | bytes 393220
  300.7 8.2 %copy-start.29 = (bf16[128,512]{1,0:T(8,128)(2,1)S(1)}, bf16[128,512]{1,0:T(8,128)(2,1)}, u32[]{:S(2)}) copy-start(bf16[128,512]{1,0:T(8,128)(2,1)} %copy-done.28) | copy-start | bytes 393220
  300.7 8.2 %copy-start.31 = (bf16[128,512]{1,0:T(8,128)(2,1)S(1)}, bf16[128,512]{1,0:T(8,128)(2,1)}, u32[]{:S(2)}) copy-start(bf16[128,512]{1,0:T(8,128)(2,1)} %copy-done.30) | copy-start | bytes 393220
  324.2 105.7 %collective-permute-start.2 = (bf16[2,256,1024]{2,1,0:T(8,128)(2,1)}, bf16[2,256,1024]{2,1,0:T(8,128)(2,1)}, u32[]{:S(2)}, u32[]{:S(2)}) collective-permute-start(bf16[2,256,1024]{2,1,0:T(8,128)(2,1)} %get-tuple-element.89), channel_id=1, source_target_pairs={{0,4},{4,0},{8,12},{12,8},{16,20},{20,16},{24,28},{28,24},{1,5},{5... | collective-permute-start | bytes 3145736 | tf_op jit(solution)/shard_map/ppermute | solution.py:781
  426.5 6.7 %copy-start.12 = (bf16[2,512,1024]{2,1,0:T(8,128)(2,1)S(1)}, bf16[2,512,1024]{2,1,0:T(8,128)(2,1)}, u32[]{:S(2)}) copy-start(bf16[2,512,1024]{2,1,0:T(8,128)(2,1)} %get-tuple-element.41) | copy-start | bytes 6291460
  429.9 6.2 %copy-start.25 = (f32[256,128]{1,0:T(8,128)S(1)}, f32[256,128]{1,0:T(8,128)}, u32[]{:S(2)}) copy-start(f32[256,128]{1,0:T(8,128)} %get-tuple-element.120) | copy-start | bytes 393220
  429.9 6.9 %copy-start.1 = (bf16[1024,1024]{1,0:T(8,128)(2,1)S(1)}, bf16[1024,1024]{1,0:T(8,128)(2,1)}, u32[]{:S(2)}) copy-start(bf16[1024,1024]{1,0:T(8,128)(2,1)} %param.24) | copy-start | bytes 6291460
  (24 other events, 83.5 us)
Sparse Core Ops, SparseCore 0:
  107.0 56.9 all-gather.5
  165.9 57.0 all-gather.3

commit v6 on v5

--- a/solution.py
+++ b/solution.py
@@ -420,9 +420,10 @@
     return pl.ds(pl.multiple_of(i * n, n), n)
 
 
-def front_kernel(x, g, wq, wo, ain, bq, ao, bo,
-                 xf, gf, wqf, wof, ainf, bqf, aof, bof,
-                 row_sems, sems, local, xs, gs, wqs, wos, ains, bqs, aos, bos):
+def front_kernel(x, g, wq, wo, ain, bq, ao, bo, gain, bias,
+                 xf, gf, wqf, wof, ainf, bqf, aof, bof, n1, n2, mq, lin, low3, low1,
+                 row_sems, sems, local, xs, gs, wqs, wos, ains, bqs, aos, bos,
+                 block_sems, work_sems, xb, n1s, n2s, wv, av, bv, mt, stage):
     z, c, t = place()
     meet(z, c, t, (1,))
     at = dict(z=z, c=c, t=t)
@@ -440,31 +441,105 @@
                    lambda v, h: v.at[aligned(h, 64)], None, **at)
     b_out = Blocks(bo, lambda i: bof.at[:, aligned(i, 32)], sems.at[5], bos, local.at[7],
                    lambda v, h: v.at[pl.ds(h, 1)], None, **at)
+    blocks = (into, second, qkv, b_out, a_out, out)
     x_rows.start()
-    for v in (into, second, qkv, b_out, a_out, out):
+    for v in blocks:
         v.start()
+    x_rows.relay()
     g_rows.start()
-    x_rows.relay()
-    for v in (into, second, qkv, b_out, a_out, out):
+    for v in blocks:
         v.store()
-    for v in (into, second, qkv, b_out, a_out, out):
+    for v in blocks:
         v.relay()
-    for v in (into, second, qkv, b_out, a_out, out):
+    x_rows.finish()
+
+    def load(j):
+        return pltpu.make_async_copy(xf.at[aligned(j, 256)], xb.at[j % 2], block_sems.at[j % 2])
+
+    load(0).start()
+
+    def norms(j, carry):
+        load(j).wait()
+
+        @pl.when(j < 7)
+        def _():
+            load(j + 1).start()
+
+        def some(r, carry):
+            v = xb[j % 2, aligned(r, 32), :].astype(F32)
+            v = v - jnp.mean(v, axis=1, keepdims=True)
+            v = v * lax.rsqrt(jnp.mean(v * v, axis=1, keepdims=True) + EPSILON)
+            at = aligned(j * 8 + r, 32)
+            n1s[at, :] = (v * gain[0:1, :] + bias[0:1, :]).astype(BF)
+            n2s[at, :] = (v * gain[1:2, :] + bias[1:2, :]).astype(BF)
+            return carry
+
+        return lax.fori_loop(0, 8, some, carry)
+
+    lax.fori_loop(0, 8, norms, 0)
+    saves = (pltpu.make_async_copy(n1s, n1, work_sems.at[0]), pltpu.make_async_copy(n2s, n2, work_sems.at[1]))
+    for v in saves:
+        v.start()
+    for v in blocks:
         v.pass_on()
+    for v in (into, second, qkv):
+        v.finish()
+    loads = (pltpu.make_async_copy(wqf, wv, work_sems.at[2]), pltpu.make_async_copy(ainf, av, work_sems.at[3]),
+             pltpu.make_async_copy(bqf, bv, work_sems.at[4]))
+    for v in loads:
+        v.start()
+    for v in loads:
+        v.wait()
+
+    def fold(m, carry):
+        at = aligned(m, 256)
+        for i in range(3):
+            v = (wv[i, at, :].astype(F32) + SCALE * dot(av[i, :, at], bv[i], 0, 0)).astype(BF)
+            wv[i, at, :] = v
+            mt[i, :, at] = jnp.transpose(v)
+        return carry
+
+    lax.fori_loop(0, 4, fold, 0)
+    folded = pltpu.make_async_copy(wv, mq, work_sems.at[5])
+    folded.start()
+
+    def put(j):
+        return pltpu.make_async_copy(stage.at[j % 2], lin.at[:, :, aligned(j, 256)], block_sems.at[2 + j % 2])
+
+    def project(j, carry):
+        at = aligned(j, 256)
+
+        @pl.when(j > 1)
+        def _():
+            put(j - 2).wait()
+
+        for i in range(3):
+            stage[j % 2, i] = dot(mt[i], n1s[at, :], 1, 1)
+            low3[i, :, at] = dot(av[i], n1s[at, :], 1, 1).astype(BF)
+        low1[:, at] = dot(av[3], n2s[at, :], 1, 1).astype(BF)
+        put(j).start()
+        return carry
+
+    lax.fori_loop(0, 8, project, 0)
     g_rows.relay()
-    for v in (x_rows, into, second, qkv, b_out, a_out, out, g_rows):
+    for v in (b_out, a_out, out, g_rows):
         v.finish()
-
-
-def front(x, g, wq, wo, ain, bq, ao, bo):
+    put(6).wait()
+    put(7).wait()
+    folded.wait()
+    for v in saves:
+        v.wait()
+
+
+def front(x, g, wq, wo, ain, bq, ao, bo, gain, bias):
     shapes = [(2048, 1024), (2048, 1024), (3, 1024, 512), (512, 1024), (4, 128, 1024), (3, 128, 512), (512, 128),
-              (2, 128, 1024)]
-    anywhere = pl.BlockSpec(memory_space=pl.ANY)
+              (2, 128, 1024), (2048, 1024), (2048, 1024), (3, 1024, 512), (3, 512, 2048), (3, 128, 2048), (128, 2048)]
+    anywhere, vmem = pl.BlockSpec(memory_space=pl.ANY), pl.BlockSpec(memory_space=pltpu.VMEM)
     return pl.pallas_call(
         front_kernel,
-        in_specs=[anywhere] * 8,
-        out_specs=[anywhere] * 8,
-        out_shape=[jax.ShapeDtypeStruct(s, BF) for s in shapes],
+        in_specs=[anywhere] * 8 + [vmem] * 2,
+        out_specs=[anywhere] * 12 + [vmem] * 2,
+        out_shape=[jax.ShapeDtypeStruct(s, F32 if i == 11 else BF) for i, s in enumerate(shapes)],
         scratch_shapes=[
             pltpu.SemaphoreType.DMA((2, 16)),
             pltpu.SemaphoreType.DMA((6, 16)),
@@ -477,14 +552,24 @@
             pltpu.VMEM((3, 128, 128), BF),
             pltpu.VMEM((128, 128), BF),
             pltpu.VMEM((2, 32, 1024), BF),
+            pltpu.SemaphoreType.DMA((4,)),
+            pltpu.SemaphoreType.DMA((6,)),
+            pltpu.VMEM((2, 256, 1024), BF),
+            pltpu.VMEM((2048, 1024), BF),
+            pltpu.VMEM((2048, 1024), BF),
+            pltpu.VMEM((3, 1024, 512), BF),
+            pltpu.VMEM((4, 128, 1024), BF),
+            pltpu.VMEM((3, 128, 512), BF),
+            pltpu.VMEM((3, 512, 1024), BF),
+            pltpu.VMEM((2, 3, 512, 256), F32),
         ],
-        compiler_params=pltpu.CompilerParams(collective_id=0, has_side_effects=True),
+        compiler_params=pltpu.CompilerParams(collective_id=0, has_side_effects=True, vmem_limit_bytes=56 << 20),
         name="front",
-    )(x, g, wq, wo, ain, bq, ao, bo)
-
-
-def back_kernel(dl, dp, mq, mu, xf, gf, gain, dbq, dbu, dao, dad, dsh,
-                out, obq, obu, oao, oad, osh, ono,
+    )(x, g, wq, wo, ain, bq, ao, bo, gain, bias)
+
+
+def back_kernel(dl, dp, mq, mu, xf, gf, gain, y, dbq, dbu, dao, dad, dsh,
+                out, yout, obq, obu, oao, oad, osh, ono,
                 row_sems, share_sems, cross_sems, z_sems, last_sems, norm_sems, local, weight_sems,
                 sh_in, sh, rbq, rbu, rao, rad, rsh, pbq, pbu, pao, pad, psh, qbq, qbu, qao, qad, qsh,
                 no_plane, no_z, no_own, no_mid, wq, wu, dlb, dpb, xb, gb, dlt, one, two, std, inv, sends, gets, rows):
@@ -519,6 +604,13 @@
     def own_row():
         return pltpu.make_async_copy(rows.at[0], out.at[t // 2, aligned(c, 256)], row_sems.at[4 + slot])
 
+    def y_row(k):
+        return remote(y.at[t ^ k], yout.at[t // 2, aligned(c, 256)], row_sems.at[16 + k], row_sems.at[20 + slot],
+                      (2 * z + home, t ^ k))
+
+    def own_y():
+        return pltpu.make_async_copy(y.at[t], yout.at[t // 2, aligned(c, 256)], row_sems.at[20 + slot])
+
     def give(k):
         return remote(sends.at[k], gets.at[k], row_sems.at[8 + k], row_sems.at[12 + k], sibling)
 
@@ -565,6 +657,17 @@
         return remote(result[i], result[i], last_sems.at[0, i], last_sems.at[1, i], sibling)
 
     share().start()
+    for k in (1, 2, 3):
+        y_row(k).start()
+
+    @pl.when(local_row)
+    def _():
+        own_y().start()
+
+    @pl.when(jnp.logical_not(local_row))
+    def _():
+        y_row(0).start()
+
     for v in weights:
         v.wait()
     no_own[...] = jnp.zeros_like(no_own)
@@ -718,31 +821,34 @@
     for k in (1, 2, 3):
         norm_z(k).wait_send()
         row(k).wait_send()
+        y_row(k).wait_send()
     for k in range(4):
         give(k).wait_send()
 
     @pl.when(jnp.logical_not(local_row))
     def _():
         row(0).wait_send()
+        y_row(0).wait_send()
 
     for m in (0, 1):
         for h in (0, 1):
             pltpu.make_async_copy(rows.at[0], out.at[m, pl.ds(256 * h, 256)], row_sems.at[4 + 2 * m + h]).wait()
-
-
-def back(dl, dp, mq, mu, xf, gf, gain, dbq, dbu, dao, dad, dsh):
+            pltpu.make_async_copy(y.at[0], yout.at[m, pl.ds(256 * h, 256)], row_sems.at[20 + 2 * m + h]).wait()
+
+
+def back(dl, dp, mq, mu, xf, gf, gain, y, dbq, dbu, dao, dad, dsh):
     vmem = pl.BlockSpec(memory_space=pltpu.VMEM)
     anywhere = pl.BlockSpec(memory_space=pl.ANY)
     part = [(3, 128, 128), (128, 512), (128, 128), (128, 512), (6, 32, 512)]
-    outs = [((2, 512, 1024), BF), ((3, 128, 256), F32), ((128, 1024), F32), ((256, 128), F32), ((128, 1024), F32),
+    outs = [((2, 512, 1024), BF), ((2, 512, 1024), BF), ((3, 128, 256), F32), ((128, 1024), F32), ((256, 128), F32), ((128, 1024), F32),
             ((6, 32, 1024), F32), ((4, 1024), F32)]
     return pl.pallas_call(
         back_kernel,
-        in_specs=[anywhere] * 6 + [vmem] * 6,
-        out_specs=[anywhere] + [vmem] * 6,
+        in_specs=[anywhere] * 6 + [vmem] * 7,
+        out_specs=[anywhere] * 2 + [vmem] * 6,
         out_shape=[jax.ShapeDtypeStruct(s, d) for s, d in outs],
         scratch_shapes=[
-            pltpu.SemaphoreType.DMA((16,)),
+            pltpu.SemaphoreType.DMA((24,)),
             pltpu.SemaphoreType.DMA((2,)),
             pltpu.SemaphoreType.DMA((2, 3, 5)),
             pltpu.SemaphoreType.DMA((2, 3, 5)),
@@ -774,7 +880,7 @@
         ],
         compiler_params=pltpu.CompilerParams(collective_id=1, has_side_effects=True, vmem_limit_bytes=56 << 20),
         name="back",
-    )(dl, dp, mq, mu, xf, gf, gain, dbq, dbu, dao, dad, dsh)
+    )(dl, dp, mq, mu, xf, gf, gain, y, dbq, dbu, dao, dad, dsh)
 
 
 def swap(v, k=1):
@@ -787,13 +893,6 @@
 
 def half_rows(v, c):
     return pick(v.reshape(4, 2, 256, -1), 1, c, 1)[:, 0]
-
-
-def from_group(own, c):
-    got = lax.all_to_all(own, "tensor", 0, 0, tiled=True).reshape(2, 2, 256, -1)
-    mine = pick(got, 1, c, 1)[:, 0]
-    other = swap(pick(got, 1, 1 - c, 1)[:, 0])
-    return jnp.where(c == 0, jnp.stack([mine, other], 1), jnp.stack([other, mine], 1)).reshape(2, 512, -1)
 
 
 def by_groups(x, gy, segment, keep, gain, bias, w_qkv, w_out, w_up, w_down,
@@ -803,8 +902,8 @@
     pair = jnp.where(t % 2 == c, tables, swap(tables))
     seg, kept = jnp.where(t // 2 == 0, pair[0], pair[1])
 
-    x_full, g_full, qkv, out, a_full, b_qkv_all, a_out_all, b_full = front(
-        x[:, 0], gy[:, 0], w_qkv, w_out, jnp.swapaxes(a_in, 1, 2), b_qkv, a_out, b_out)
+    x_full, g_full, _, out, a_full, b_qkv_all, a_out_all, b_full, n1, n2, m_qkv, lin, low3, low1 = front(
+        x[:, 0], gy[:, 0], w_qkv, w_out, jnp.swapaxes(a_in, 1, 2), b_qkv, a_out, b_out, gain, bias)
     up, down = lax.optimization_barrier((
         jnp.concatenate([pick(w_up, 1, c, 512), pick(b_up, 1, c, 512)], axis=0),
         jnp.concatenate([pick(w_down, 0, c, 512), pick(a_down, 0, c, 512)], axis=1), x_full))[:2]
@@ -814,20 +913,11 @@
     b_up_all = jnp.concatenate([up[i, 1024:] for i in range(4)], axis=1)
     w_down_all, a_down_all = down[:, :1024], down[:, 1024:]
 
-    m_qkv = (qkv.astype(F32) + SCALE * jnp.einsum("nrk,nrc->nkc", a_full[:3], b_qkv_all,
-                                                  preferred_element_type=F32)).astype(BF)
     m_up = (w_up_all.astype(F32) + SCALE * dot(a_full[3], b_up_all, 0, 0)).astype(BF)
     m_out = (out.astype(F32) + SCALE * dot(a_out_all, b_full[0], 1, 0)).astype(BF)
     m_down = (w_down_all.astype(F32) + SCALE * dot(a_down_all, b_full[1], 1, 0)).astype(BF)
-    a_three = a_full[:3].reshape(3 * RANK, 1024)
     b_both = b_full.reshape(2 * RANK, 1024)
 
-    standard, _ = normalized(x_full.astype(F32))
-    n1 = (standard * gain[0] + bias[0]).astype(BF)
-    n2 = (standard * gain[1] + bias[1]).astype(BF)
-    lin = jnp.einsum("nkc,sk->ncs", m_qkv, n1, preferred_element_type=F32)
-    low3 = dot(a_three, n1, 1, 1).astype(BF).reshape(3, RANK, 2048)
-    low1 = dot(a_full[3], n2, 1, 1).astype(BF)
     g_ctx = dot(m_out, g_full, 1, 1).astype(BF)
     low_grad = (SCALE * dot(b_both, g_full, 1, 1)).astype(BF)
     cos, sin = rotary_tables(seg)
@@ -842,7 +932,6 @@
     part = dot(ctx, m_out, 0, 0) + dot(hidden, m_down, 1, 0)
     theirs = swap(half_rows(part, 1 - c).astype(BF))
     y = half_rows(x_full, c).astype(F32) + half_rows(part, c) + theirs.astype(F32)
-    y = from_group(y.astype(BF), c)
 
     lo = jnp.concatenate([dot(a_out_all, ctx, 0, 0), dot(a_down_all, hidden, 0, 1)], axis=0).astype(BF)
     d_a_out = dot(ctx, low_grad[:RANK], 1, 1).astype(BF)
@@ -853,8 +942,8 @@
     back1 = (SCALE * dot(b_up_all, d_pre, 1, 1)).astype(BF)
     shared = jnp.concatenate([dot(back3.reshape(3 * RANK, 2048), n1, 1, 0).astype(BF), dot(back1, n2, 1, 0).astype(BF),
                               (SCALE * dot(lo, g_full, 1, 0)).astype(BF)], axis=0).reshape(6, RANK, 1024)
-    grad, r_b_qkv, r_b_up, r_a_out, r_a_down, rest, norms = back(
-        d_lin, d_pre, m_qkv, m_up, x_full, g_full, gain, d_b_qkv, d_b_up, d_a_out, d_a_down, shared)
+    grad, y, r_b_qkv, r_b_up, r_a_out, r_a_down, rest, norms = back(
+        d_lin, d_pre, m_qkv, m_up, x_full, g_full, gain, y.astype(BF), d_b_qkv, d_b_up, d_a_out, d_a_down, shared)
     r_a_in = jnp.swapaxes(rest[:4], 1, 2)
     return (y[:, None], grad[:, None], norms[:2], norms[2:], r_a_in, r_b_qkv, r_b_up, r_a_out, jnp.transpose(r_a_down), rest[4:])
 

time: 450 us -> 452 us (level)
  Pallas kernels: 245 us -> 290 us
  matrix products: 122 us -> 102 us
  starting transfers between devices: 10.9 us -> 0.96 us
  other arithmetic: 20.5 us -> 11.8 us
  waiting for transfers between devices: 6.58 us -> 0.22 us
    pallas_call x2, Pallas kernels: 186 us -> 223 us  [the longest x1 116 us: front(): pl.pallas_call(front_kernel, in_specs=[anywhere] * 8 + [vmem] * 2, out_sp...]
    dot_general x18 -> x17, matrix products: 105 us -> 94.3 us  [dot(): lax.dot_general(a, b, (((ca,), (cb,)), ((), ())), preferred_element_type=...]
    all_to_all x1 -> x0, starting transfers between devices: 10.6 us -> none  [from_group(): got = lax.all_to_all(own, 'tensor', 0, 0, tiled=True).reshape(2, 2, 256, -1)]
    dot_general x2 -> x0, matrix products: 10.5 us -> none  [the longest x1 9.27 us: by_groups(): lin = jnp.einsum('nkc,sk->ncs', m_qkv, n1, preferred_element_type=F32)]
    pallas_call x1, Pallas kernels: 59.5 us -> 67.3 us  [attention(): pl.pallas_call(functools.partial(attention_kernel, heads), grid_spec=pltp...]
    all_to_all x1 -> x0, waiting for transfers between devices: 6 us -> none  [from_group(): got = lax.all_to_all(own, 'tensor', 0, 0, tiled=True).reshape(2, 2, 256, -1)]
    reduce_sum x2 -> x0, other arithmetic: 4.79 us -> none  [the longest x1 2.95 us: normalized(): average = jnp.mean(values, axis=-1, keepdims=True)]
    unnamed x89 -> x78, local copies, waits for them, and re-layouts: 8.38 us -> 12.5 us
  transfers between devices with their start and end apart: 6 -> 4, of which waited for: 1 -> 0; matrix products, arithmetic and copies ran while one was open for 29% -> 18% of each run, Pallas kernels for 34% -> 15%
where the time goes in v6:
time: 452 us; the launch traced here: 446 us
  Pallas kernels  290 us (64%)
  matrix products  102 us (23%)
  local copies, waits for them, and re-layouts  26.3 us (6%)
  between operations  14.8 us (3%)
  other arithmetic  11.8 us (3%)
    pallas_call x1, Pallas kernels, front(): pl.pallas_call(front_kernel, in_specs=[anywhere] * 8 + [vmem] * 2, out_sp...  116 us
    pallas_call x1, Pallas kernels, back(): pl.pallas_call(back_kernel, in_specs=[anywhere] * 6 + [vmem] * 7, out_spe...  106 us
    dot_general x17, matrix products, dot(): lax.dot_general(a, b, (((ca,), (cb,)), ((), ())), preferred_element_type=...  94.3 us
    pallas_call x1, Pallas kernels, attention(): pl.pallas_call(functools.partial(attention_kernel, heads), grid_spec=pltp...  67.3 us
    unnamed x78, local copies, waits for them, and re-layouts  12.5 us
  transfers between devices with their start and end apart: 4, of which 0 were waited for; matrix products, arithmetic and copies ran while one was open for 18% of the time, Pallas kernels for 15%

profile of v6, /device:TPU:0, one launch (start us, length us, event | category | flops | bytes accessed | tf_op | source)
XLA Modules:
  0.0 446.0 jit_solution(16626788253778655195)
XLA Ops:
  13.0 116.4 %front.1 = (bf16[2048,1024]{1,0:T(8,128)(2,1)}, bf16[2048,1024]{1,0:T(8,128)(2,1)}, bf16[3,1024,512]{2,1,0:T(8,128)(2,1)}, bf16[512,1024]{1,0:T(8,128)(2,1)}, bf...) custom-call(bf16[2,512,1024]{2,1,0:T(8,128)(2,1)} %bitcast.113, ...), custom_call_target="tpu_custom_call" | custom-call | tf_op jit(solution)/shard_map/front/pallas_call | solution.py:538
  132.1 3.5 fusion.9
  135.6 3.7 convolution_convert_fusion.g_ref
  143.4 67.3 %attention.1 = (bf16[512,2048]{1,0:T(8,128)(2,1)}, bf16[3,512,2048]{2,1,0:T(8,128)(2,1)}) custom-call(s32[8]{0:T(128)} %and_select_fusion.lo_ref, f32[3,512,2048]{2,1,0:T(8,128)} %get-tuple-element.35.lin_ref, bf16[512,2048]{1,0:T(8,128)(2,1)} %convolution_convert_fusion.g_ref, f32[8,2048]{1,0:T(8,128)} %get-tuple-element.104.cos_ref, ...), custom_call_target="tpu_custom_call" | custom-call | flops 8053063680 | bytes 27262976 | tf_op jit(solution)/shard_map/attention/pallas_call | solution.py:145
  210.8 3.0 convolution_convert_fusion.3
  213.8 3.0 convolution_convert_fusion.6.dao
  216.8 4.7 %multiply_convert_fusion.1 = bf16[3,128,2048]{2,1,0:T(8,128)(2,1)S(1)} fusion(bf16[3,128,512]{2,1,0:T(8,128)(2,1)S(1)} %copy-done.16, bf16[3,512,2048]{2,1,0:T(8,128)(2,1)} %get-tuple-element.40.dl), kind=kOutput, calls=%fused_computation.17 | convolution fusion | flops 806879232 | bytes 8257536 | tf_op jit(solution)/shard_map/nrc,ncs->nrs/dot_general | solution.py:941
  221.5 3.0 fusion.14.dbq
  224.5 2.7 convolution_convert_fusion.4
  228.4 2.6 slice_bitcast_fusion.3
  231.0 4.8 %add_convert_fusion.mu = bf16[1024,2048]{1,0:T(8,128)(2,1)S(1)} fusion(bf16[1024,512]{1,0:T(8,128)(2,1)S(1)} %get-tuple-element.95, bf16[1024,512]{1,0:T(8,128)(2,1)S(1)} %get-tuple-element.96, bf16[1024,512]{1,0:T(8,128)(2,1)S(1)} %get-tuple-element.97, bf16[1024,512]{1,0:T(8,128)(2,1)S(1)} %get-tuple-element.94, ...), kind=kOutput, calls=%fused_computation.9 | convolution fusion | flops 562036736 | bytes 9175040 | tf_op jit(solution)/shard_map/dot_general | solution.py:23
  237.8 14.0 %multiply_convert_fusion = (bf16[2048,2048]{1,0:T(8,128)(2,1)}, f32[2048,2048]{1,0:T(8,128)}) fusion(bf16[2048,1024]{1,0:T(8,128)(2,1)S(1)} %copy-done.26, bf16[1024,2048]{1,0:T(8,128)(2,1)S(1)} %add_convert_fusion.mu), kind=kOutput, calls=%fused_computation.7 | convolution fusion | flops 8610906112 | bytes 33554432 | tf_op jit(solution)/shard_map/dot_general | solution.py:23
  251.8 3.8 add_convert_fusion.1
  255.6 17.8 %fusion.5.dp = bf16[2048,2048]{1,0:T(8,128)(2,1)} fusion(f32[2048,2048]{1,0:T(8,128)} %get-tuple-element.106, bf16[2048,1024]{1,0:T(8,128)(2,1)} %get-tuple-element.39.gf, bf16[2048,1024]{1,0:T(8,128)(2,1)S(1)} %add_convert_fusion.1), kind=kOutput, calls=%fused_computation.6 | convolution fusion | flops 8631877632 | bytes 33554432 | tf_op jit(solution)/shard_map/dot_general | solution.py:23
  273.5 9.0 %fusion.36 = f32[2048,1024]{1,0:T(8,128)S(1)} fusion(bf16[2048,2048]{1,0:T(8,128)(2,1)S(1)} %bitcast.104, bf16[2048,1024]{1,0:T(8,128)(2,1)S(1)} %add_convert_fusion.1), kind=kOutput, calls=%fused_computation.93 | convolution fusion | flops 8589934592 | bytes 20971520 | tf_op jit(solution)/shard_map/dot_general | solution.py:23
  282.5 2.5 convolution_add_fusion
  285.9 6.5 %convolution_convert_fusion.1 = bf16[128,2048]{1,0:T(8,128)(2,1)S(1)} fusion(bf16[2048,2048]{1,0:T(8,128)(2,1)S(1)} %bitcast.104, bf16[2048,1152]{1,0:T(8,128)(2,1)} %all-gather.4.cloned.1.call-done), kind=kOutput, calls=%fused_computation.23 | convolution fusion | flops 1074003968 | bytes 9437184 | tf_op jit(solution)/shard_map/dot_general | solution.py:23
  294.4 8.3 %convolution_convert_fusion.5 = bf16[128,1024]{1,0:T(8,128)(2,1)S(1)} fusion(bf16[2048,1024]{1,0:T(8,128)(2,1)} %get-tuple-element.43, bf16[2048,2048]{1,0:T(8,128)(2,1)} %fusion.5.dp, bf16[128,512]{1,0:T(8,128)(2,1)} %copy-done.21, bf16[128,512]{1,0:T(8,128)(2,1)} %copy-done.22, bf16[128,512]{1,0:T(8,128)(2,1)} %copy-done.23, ...), kind=kOutput, calls=%fused_computation.36 | convolution fusion | flops 1613365248 | bytes 13369344 | tf_op jit(solution)/shard_map/dot_general | solution.py:23
  302.7 2.7 pad_maximum_fusion
  305.5 5.6 %convolution_convert_fusion.2.dad = bf16[128,2048]{1,0:T(8,128)(2,1)} fusion(bf16[2048,2048]{1,0:T(8,128)(2,1)} %get-tuple-element.105, bf16[256,2048]{1,0:T(8,128)(2,1)S(1)} %copy-done.12), kind=kOutput, calls=%fused_computation.24 | convolution fusion | flops 1074003968 | bytes 9437184 | tf_op jit(solution)/shard_map/dot_general | solution.py:23
  311.1 2.1 fusion.10.dbu
  314.7 4.2 fusion.8.y
  318.9 106.2 %back.1 = (bf16[2,512,1024]{2,1,0:T(8,128)(2,1)}, bf16[2,512,1024]{2,1,0:T(8,128)(2,1)}, f32[3,128,256]{2,1,0:T(8,128)}, f32[128,1024]{1,0:T(8,128)}, f32[256,12...) custom-call(bf16[3,512,2048]{2,1,0:T(8,128)(2,1)} %get-tuple-element.40.dl, ...), custom_call_target="tpu_custom_call" | custom-call | tf_op jit(solution)/shard_map/back/pallas_call | solution.py:845
  432.2 3.2 copy.51
  (117 shorter events, 30.6 us)
Async XLA Ops:
  7.2 220.0 %all-gather.6.cloned.1.call-start = ((), (), s32[]{:S(2)}) async-start(), calls=%async_computation.1 | async-start | bytes 5898240 | tf_op jit(solution)/shard_map/all_gather | solution.py:910
  13.0 116.5 %copy-start.24 = (s32[2,1,2048]{2,1,0:T(1,128)S(1)}, s32[2,1,2048]{2,1,0:T(1,128)}, u32[]{:S(2)}) copy-start(s32[2,1,2048]{2,1,0:T(1,128)} %param.19) | copy-start | bytes 49156
  13.0 116.5 %copy-start.25 = (s32[2,1,2048]{2,1,0:T(1,128)S(1)}, s32[2,1,2048]{2,1,0:T(1,128)}, u32[]{:S(2)}) copy-start(s32[2,1,2048]{2,1,0:T(1,128)} %param.18) | copy-start | bytes 49156
  129.4 122.4 %all-gather.4.cloned.1.call-start = ((), (), s32[]{:S(2)}) async-start(), calls=%async_computation | async-start | bytes 5898240 | tf_op jit(solution)/shard_map/all_gather | solution.py:911
  129.5 9.9 %collective-permute-start = (s32[2,2,2048]{2,1,0:T(2,128)S(1)}, s32[2,2,2048]{2,1,0:T(2,128)S(1)}, u32[]{:S(2)}, u32[]{:S(2)}) collective-permute-start(s32[2,2,2048]{2,1,0:T(2,128)S(1)} %pad_add_fusion), channel_id=1, source_target_pairs={{0,4},{4,0},{8,12},{12,8},{16,20},{20,16},{24,28},{28,24},{1,5},{5... | collective-permute-start | bytes 98312 | tf_op jit(solution)/shard_map/ppermute | solution.py:887
  135.6 78.2 %copy-start.11 = (bf16[256,2048]{1,0:T(8,128)(2,1)}, bf16[256,2048]{1,0:T(8,128)(2,1)S(1)}, u32[]{:S(2)}) copy-start(bf16[256,2048]{1,0:T(8,128)(2,1)S(1)} %fusion.9) | copy-start | bytes 3145732
  143.4 67.3 %copy-start.15 = (bf16[512,128]{1,0:T(8,128)(2,1)S(1)}, bf16[512,128]{1,0:T(8,128)(2,1)}, u32[]{:S(2)}) copy-start(bf16[512,128]{1,0:T(8,128)(2,1)} %get-tuple-element.37) | copy-start | bytes 393220
  210.7 6.0 %copy-start.16 = (bf16[3,128,512]{2,1,0:T(8,128)(2,1)S(1)}, bf16[3,128,512]{2,1,0:T(8,128)(2,1)}, u32[]{:S(2)}) copy-start(bf16[3,128,512]{2,1,0:T(8,128)(2,1)} %get-tuple-element.50) | copy-start | bytes 1179652
  210.8 10.7 %slice-start = ((s8[6291456]{0:T(1024)(128)(4,1)}), s8[4194304]{0:T(1024)(128)(4,1)S(1)}, s32[]{:S(2)}) async-start(s8[6291456]{0:T(1024)(128)(4,1)} %bitcast.99), calls=%async_computation.2 | async-start | bytes 8388608
  231.0 6.8 %copy-start.26 = (bf16[2048,1024]{1,0:T(8,128)(2,1)S(1)}, bf16[2048,1024]{1,0:T(8,128)(2,1)}, u32[]{:S(2)}) copy-start(bf16[2048,1024]{1,0:T(8,128)(2,1)} %get-tuple-element.43) | copy-start | bytes 12582916
  237.8 14.0 %copy-start.19 = (bf16[2,128,1024]{2,1,0:T(8,128)(2,1)S(1)}, bf16[2,128,1024]{2,1,0:T(8,128)(2,1)}, u32[]{:S(2)}) copy-start(bf16[2,128,1024]{2,1,0:T(8,128)(2,1)} %get-tuple-element.38) | copy-start | bytes 1572868
  251.8 21.6 %slice-start.4 = ((s8[8388608]{0:T(1024)(128)(4,1)}), s8[4194304]{0:T(1024)(128)(4,1)S(1)}, s32[]{:S(2)}) async-start(s8[8388608]{0:T(1024)(128)(4,1)} %bitcast.103), calls=%async_computation.6 | async-start | bytes 8388608
  255.6 17.9 %slice-start.5 = ((s8[8388608]{0:T(1024)(128)(4,1)}), s8[4194304]{0:T(1024)(128)(4,1)S(1)}, s32[]{:S(2)}) async-start(s8[8388608]{0:T(1024)(128)(4,1)} %bitcast.103), calls=%async_computation.7 | async-start | bytes 8388608
  273.5 9.0 %copy-start.3 = (bf16[512,2048]{1,0:T(8,128)(2,1)S(1)}, bf16[512,2048]{1,0:T(8,128)(2,1)}, u32[]{:S(2)}) copy-start(bf16[512,2048]{1,0:T(8,128)(2,1)} %get-tuple-element.47) | copy-start | bytes 6291460
  285.1 7.3 %copy-start.2 = (f32[2048,1024]{1,0:T(8,128)}, f32[2048,1024]{1,0:T(8,128)S(1)}, u32[]{:S(2)}) copy-start(f32[2048,1024]{1,0:T(8,128)S(1)} %convolution_add_fusion) | copy-start | bytes 25165828
  285.4 6.9 %copy-start.6 = (bf16[2048,1024]{1,0:T(8,128)(2,1)S(1)}, bf16[2048,1024]{1,0:T(8,128)(2,1)}, u32[]{:S(2)}) copy-start(bf16[2048,1024]{1,0:T(8,128)(2,1)} %get-tuple-element.39.gf) | copy-start | bytes 12582916
  285.4 6.9 %copy-start.14 = (bf16[128,2048]{1,0:T(8,128)(2,1)S(1)}, bf16[128,2048]{1,0:T(8,128)(2,1)}, u32[]{:S(2)}) copy-start(bf16[128,2048]{1,0:T(8,128)(2,1)} %convolution_convert_fusion.3) | copy-start | bytes 1572868
  285.4 27.8 %collective-permute-start.1 = (bf16[4,256,1024]{2,1,0:T(8,128)(2,1)S(1)}, bf16[4,256,1024]{2,1,0:T(8,128)(2,1)}, u32[]{:S(2)}, u32[]{:S(2)}) collective-permute-start(bf16[4,256,1024]{2,1,0:T(8,128)(2,1)S(1)} %fusion.12), channel_id=1, source_target_pairs={{0,4},{4,0},{8,12},{12,8},{16,20},{20,16},{24,28},{28,24},{1,5},{5... | collective-permute-start | bytes 6291464 | tf_op jit(solution)/shard_map/ppermute | solution.py:887
  294.4 11.0 %copy-start.12 = (bf16[256,2048]{1,0:T(8,128)(2,1)S(1)}, bf16[256,2048]{1,0:T(8,128)(2,1)}, u32[]{:S(2)}) copy-start(bf16[256,2048]{1,0:T(8,128)(2,1)} %copy-done.11) | copy-start | bytes 3145732
  302.7 8.3 %slice-start.2 = ((s8[8388608]{0:T(1024)(128)(4,1)}), s8[4194304]{0:T(1024)(128)(4,1)S(1)}, s32[]{:S(2)}) async-start(s8[8388608]{0:T(1024)(128)(4,1)} %bitcast.101), calls=%async_computation.4 | async-start | bytes 8388608
  305.5 5.6 %copy-start.10 = (bf16[128,2048]{1,0:T(8,128)(2,1)S(1)}, bf16[128,2048]{1,0:T(8,128)(2,1)}, u32[]{:S(2)}) copy-start(bf16[128,2048]{1,0:T(8,128)(2,1)} %get-tuple-element.49) | copy-start | bytes 1572868
  305.5 7.7 %slice-start.6 = ((s8[8388608]{0:T(1024)(128)(4,1)}), s8[4194304]{0:T(1024)(128)(4,1)S(1)}, s32[]{:S(2)}) async-start(s8[8388608]{0:T(1024)(128)(4,1)} %bitcast.106), calls=%async_computation.8 | async-start | bytes 8388608
  432.2 6.1 %copy-start.20 = (f32[256,128]{1,0:T(8,128)S(1)}, f32[256,128]{1,0:T(8,128)}, u32[]{:S(2)}) copy-start(f32[256,128]{1,0:T(8,128)} %get-tuple-element.124) | copy-start | bytes 393220
  432.2 6.8 %copy-start.1 = (bf16[1024,1024]{1,0:T(8,128)(2,1)S(1)}, bf16[1024,1024]{1,0:T(8,128)(2,1)}, u32[]{:S(2)}) copy-start(bf16[1024,1024]{1,0:T(8,128)(2,1)} %param.24) | copy-start | bytes 6291460
  (16 other events, 57.3 us)
Sparse Core Ops, SparseCore 0:
  129.5 57.2 all-gather.5
  188.7 56.9 all-gather.3

commit v7 on v5

--- a/solution.py
+++ b/solution.py
@@ -483,8 +483,8 @@
     )(x, g, wq, wo, ain, bq, ao, bo)
 
 
-def back_kernel(dl, dp, mq, mu, xf, gf, gain, dbq, dbu, dao, dad, dsh,
-                out, obq, obu, oao, oad, osh, ono,
+def back_kernel(dl, dp, mq, mu, xf, gf, gain, y, dbq, dbu, dao, dad, dsh,
+                out, yout, obq, obu, oao, oad, osh, ono,
                 row_sems, share_sems, cross_sems, z_sems, last_sems, norm_sems, local, weight_sems,
                 sh_in, sh, rbq, rbu, rao, rad, rsh, pbq, pbu, pao, pad, psh, qbq, qbu, qao, qad, qsh,
                 no_plane, no_z, no_own, no_mid, wq, wu, dlb, dpb, xb, gb, dlt, one, two, std, inv, sends, gets, rows):
@@ -518,6 +518,13 @@
 
     def own_row():
         return pltpu.make_async_copy(rows.at[0], out.at[t // 2, aligned(c, 256)], row_sems.at[4 + slot])
+
+    def y_row(k):
+        return remote(y.at[t ^ k], yout.at[t // 2, aligned(c, 256)], row_sems.at[16 + k], row_sems.at[20 + slot],
+                      (2 * z + home, t ^ k))
+
+    def own_y():
+        return pltpu.make_async_copy(y.at[t], yout.at[t // 2, aligned(c, 256)], row_sems.at[20 + slot])
 
     def give(k):
         return remote(sends.at[k], gets.at[k], row_sems.at[8 + k], row_sems.at[12 + k], sibling)
@@ -653,6 +660,16 @@
                     total = total + got[i][p].astype(F32)
                 sums[i][0] = total.astype(BF)
                 along(0, i).start()
+            for p in (1, 2, 3):
+                y_row(p).start()
+
+            @pl.when(local_row)
+            def _():
+                own_y().start()
+
+            @pl.when(jnp.logical_not(local_row))
+            def _():
+                y_row(0).start()
 
         for step, when in ((0, 4), (1, 6)):
             @pl.when(j == when)
@@ -718,31 +735,34 @@
     for k in (1, 2, 3):
         norm_z(k).wait_send()
         row(k).wait_send()
+        y_row(k).wait_send()
     for k in range(4):
         give(k).wait_send()
 
     @pl.when(jnp.logical_not(local_row))
     def _():
         row(0).wait_send()
+        y_row(0).wait_send()
 
     for m in (0, 1):
         for h in (0, 1):
             pltpu.make_async_copy(rows.at[0], out.at[m, pl.ds(256 * h, 256)], row_sems.at[4 + 2 * m + h]).wait()
-
-
-def back(dl, dp, mq, mu, xf, gf, gain, dbq, dbu, dao, dad, dsh):
+            pltpu.make_async_copy(y.at[0], yout.at[m, pl.ds(256 * h, 256)], row_sems.at[20 + 2 * m + h]).wait()
+
+
+def back(dl, dp, mq, mu, xf, gf, gain, y, dbq, dbu, dao, dad, dsh):
     vmem = pl.BlockSpec(memory_space=pltpu.VMEM)
     anywhere = pl.BlockSpec(memory_space=pl.ANY)
     part = [(3, 128, 128), (128, 512), (128, 128), (128, 512), (6, 32, 512)]
-    outs = [((2, 512, 1024), BF), ((3, 128, 256), F32), ((128, 1024), F32), ((256, 128), F32), ((128, 1024), F32),
+    outs = [((2, 512, 1024), BF), ((2, 512, 1024), BF), ((3, 128, 256), F32), ((128, 1024), F32), ((256, 128), F32), ((128, 1024), F32),
             ((6, 32, 1024), F32), ((4, 1024), F32)]
     return pl.pallas_call(
         back_kernel,
-        in_specs=[anywhere] * 6 + [vmem] * 6,
-        out_specs=[anywhere] + [vmem] * 6,
+        in_specs=[anywhere] * 6 + [vmem] * 7,
+        out_specs=[anywhere] * 2 + [vmem] * 6,
         out_shape=[jax.ShapeDtypeStruct(s, d) for s, d in outs],
         scratch_shapes=[
-            pltpu.SemaphoreType.DMA((16,)),
+            pltpu.SemaphoreType.DMA((24,)),
             pltpu.SemaphoreType.DMA((2,)),
             pltpu.SemaphoreType.DMA((2, 3, 5)),
             pltpu.SemaphoreType.DMA((2, 3, 5)),
@@ -774,7 +794,7 @@
         ],
         compiler_params=pltpu.CompilerParams(collective_id=1, has_side_effects=True, vmem_limit_bytes=56 << 20),
         name="back",
-    )(dl, dp, mq, mu, xf, gf, gain, dbq, dbu, dao, dad, dsh)
+    )(dl, dp, mq, mu, xf, gf, gain, y, dbq, dbu, dao, dad, dsh)
 
 
 def swap(v, k=1):
@@ -787,13 +807,6 @@
 
 def half_rows(v, c):
     return pick(v.reshape(4, 2, 256, -1), 1, c, 1)[:, 0]
-
-
-def from_group(own, c):
-    got = lax.all_to_all(own, "tensor", 0, 0, tiled=True).reshape(2, 2, 256, -1)
-    mine = pick(got, 1, c, 1)[:, 0]
-    other = swap(pick(got, 1, 1 - c, 1)[:, 0])
-    return jnp.where(c == 0, jnp.stack([mine, other], 1), jnp.stack([other, mine], 1)).reshape(2, 512, -1)
 
 
 def by_groups(x, gy, segment, keep, gain, bias, w_qkv, w_out, w_up, w_down,
@@ -842,7 +855,6 @@
     part = dot(ctx, m_out, 0, 0) + dot(hidden, m_down, 1, 0)
     theirs = swap(half_rows(part, 1 - c).astype(BF))
     y = half_rows(x_full, c).astype(F32) + half_rows(part, c) + theirs.astype(F32)
-    y = from_group(y.astype(BF), c)
 
     lo = jnp.concatenate([dot(a_out_all, ctx, 0, 0), dot(a_down_all, hidden, 0, 1)], axis=0).astype(BF)
     d_a_out = dot(ctx, low_grad[:RANK], 1, 1).astype(BF)
@@ -853,8 +865,8 @@
     back1 = (SCALE * dot(b_up_all, d_pre, 1, 1)).astype(BF)
     shared = jnp.concatenate([dot(back3.reshape(3 * RANK, 2048), n1, 1, 0).astype(BF), dot(back1, n2, 1, 0).astype(BF),
                               (SCALE * dot(lo, g_full, 1, 0)).astype(BF)], axis=0).reshape(6, RANK, 1024)
-    grad, r_b_qkv, r_b_up, r_a_out, r_a_down, rest, norms = back(
-        d_lin, d_pre, m_qkv, m_up, x_full, g_full, gain, d_b_qkv, d_b_up, d_a_out, d_a_down, shared)
+    grad, y, r_b_qkv, r_b_up, r_a_out, r_a_down, rest, norms = back(
+        d_lin, d_pre, m_qkv, m_up, x_full, g_full, gain, y.astype(BF), d_b_qkv, d_b_up, d_a_out, d_a_down, shared)
     r_a_in = jnp.swapaxes(rest[:4], 1, 2)
     return (y[:, None], grad[:, None], norms[:2], norms[2:], r_a_in, r_b_qkv, r_b_up, r_a_out, jnp.transpose(r_a_down), rest[4:])
 

time: 450 us -> 441 us (0.980)
  Pallas kernels: 245 us -> 259 us
  starting transfers between devices: 10.9 us -> 0.22 us
  matrix products: 122 us -> 115 us
  waiting for transfers between devices: 6.58 us -> 0.58 us
    pallas_call x1, Pallas kernels: 91.6 us -> 105 us  [back(): pl.pallas_call(back_kernel, in_specs=[anywhere] * 6 + [vmem] * 7, out_spe...]
    all_to_all x1 -> x0, starting transfers between devices: 10.6 us -> none  [from_group(): got = lax.all_to_all(own, 'tensor', 0, 0, tiled=True).reshape(2, 2, 256, -1)]
    dot_general x18, matrix products: 105 us -> 97.7 us  [dot(): lax.dot_general(a, b, (((ca,), (cb,)), ((), ())), preferred_element_type=...]
    all_to_all x1 -> x0, waiting for transfers between devices: 6 us -> none  [from_group(): got = lax.all_to_all(own, 'tensor', 0, 0, tiled=True).reshape(2, 2, 256, -1)]
    unnamed x89 -> x78, local copies, waits for them, and re-layouts: 8.38 us -> 11.6 us
  transfers between devices with their start and end apart: 6 -> 4, of which waited for: 1 -> 0; matrix products, arithmetic and copies ran while one was open for 29% -> 23% of each run, Pallas kernels for 34% -> 14%
where the time goes in v7:
time: 441 us; the launch traced here: 437 us
  Pallas kernels  259 us (59%)
  matrix products  115 us (26%)
  local copies, waits for them, and re-layouts  25.5 us (6%)
  other arithmetic  21.6 us (5%)
  between operations  14.9 us (3%)
    pallas_call x1, Pallas kernels, back(): pl.pallas_call(back_kernel, in_specs=[anywhere] * 6 + [vmem] * 7, out_spe...  105 us
    dot_general x18, matrix products, dot(): lax.dot_general(a, b, (((ca,), (cb,)), ((), ())), preferred_element_type=...  97.7 us
    pallas_call x1, Pallas kernels, front(): pl.pallas_call(front_kernel, in_specs=[anywhere] * 8, out_specs=[anywhere...  94 us
    pallas_call x1, Pallas kernels, attention(): pl.pallas_call(functools.partial(attention_kernel, heads), grid_spec=pltp...  59.7 us
    unnamed x78, local copies, waits for them, and re-layouts  11.6 us
    dot_general x1, matrix products, by_groups(): lin = jnp.einsum('nkc,sk->ncs', m_qkv, n1, preferred_element_type=F32)  9.23 us
  transfers between devices with their start and end apart: 4, of which 0 were waited for; matrix products, arithmetic and copies ran while one was open for 23% of the time, Pallas kernels for 14%

profile of v7, /device:TPU:0, one launch (start us, length us, event | category | flops | bytes accessed | tf_op | source)
XLA Modules:
  0.0 436.8 jit_solution(3816697331786949605)
XLA Ops:
  12.9 94.0 %front.1 = (bf16[2048,1024]{1,0:T(8,128)(2,1)}, bf16[2048,1024]{1,0:T(8,128)(2,1)}, bf16[3,1024,512]{2,1,0:T(8,128)(2,1)}, bf16[512,1024]{1,0:T(8,128)(2,1)}, bf...) custom-call(bf16[2,512,1024]{2,1,0:T(8,128)(2,1)} %bitcast.127, ...), custom_call_target="tpu_custom_call" | custom-call | tf_op jit(solution)/shard_map/front/pallas_call | solution.py:463
  107.7 3.0 convert_reduce_fusion
  115.8 3.7 convolution_convert_fusion.g_ref
  120.7 3.7 fusion.13
  126.4 9.2 %fusion.18.lin_ref = f32[3,512,2048]{2,1,0:T(8,128)} fusion(bf16[3,1024,512]{2,1,0:T(8,128)(2,1)S(1)} %add_convert_fusion.2.mq, bf16[2048,1024]{1,0:T(8,128)(2,1)S(1)} %get-tuple-element.89), kind=kOutput, calls=%fused_computation.28 | convolution fusion | flops 6442450944 | bytes 19922944 | tf_op jit(solution)/shard_map/nkc,sk->ncs/dot_general | solution.py:841
  139.7 59.7 %attention.1 = (bf16[512,2048]{1,0:T(8,128)(2,1)}, bf16[3,512,2048]{2,1,0:T(8,128)(2,1)}) custom-call(s32[8]{0:T(128)} %and_select_fusion.lo_ref, f32[3,512,2048]{2,1,0:T(8,128)} %fusion.18.lin_ref, bf16[512,2048]{1,0:T(8,128)(2,1)} %convolution_convert_fusion.g_ref, f32[8,2048]{1,0:T(8,128)} %get-tuple-element.96.cos_ref, ...), custom_call_target="tpu_custom_call" | custom-call | flops 8053063680 | bytes 27262976 | tf_op jit(solution)/shard_map/attention/pallas_call | solution.py:145
  199.4 3.0 convolution_convert_fusion.4
  202.4 3.0 convolution_convert_fusion.8.dao
  205.5 3.9 multiply_convert_fusion.1
  209.4 3.0 fusion.25.dbq
  212.4 2.7 convolution_convert_fusion.6
  216.3 2.6 slice_bitcast_fusion.3
  218.9 4.9 %add_convert_fusion.mu = bf16[1024,2048]{1,0:T(8,128)(2,1)S(1)} fusion(bf16[1024,512]{1,0:T(8,128)(2,1)S(1)} %get-tuple-element.85, bf16[1024,512]{1,0:T(8,128)(2,1)S(1)} %get-tuple-element.86, bf16[1024,512]{1,0:T(8,128)(2,1)S(1)} %get-tuple-element.87, bf16[1024,512]{1,0:T(8,128)(2,1)S(1)} %get-tuple-element.84, ...), kind=kOutput, calls=%fused_computation.20 | convolution fusion | flops 562036736 | bytes 9175040 | tf_op jit(solution)/shard_map/dot_general | solution.py:23
  225.7 14.0 %multiply_convert_fusion = (bf16[2048,2048]{1,0:T(8,128)(2,1)}, f32[2048,2048]{1,0:T(8,128)}) fusion(bf16[2048,1024]{1,0:T(8,128)(2,1)S(1)} %copy-done.4, bf16[1024,2048]{1,0:T(8,128)(2,1)S(1)} %add_convert_fusion.mu), kind=kOutput, calls=%fused_computation.7 | convolution fusion | flops 8610906112 | bytes 33554432 | tf_op jit(solution)/shard_map/dot_general | solution.py:23
  239.7 3.7 add_convert_fusion.1
  243.4 17.6 %fusion.5.dp = bf16[2048,2048]{1,0:T(8,128)(2,1)} fusion(f32[2048,2048]{1,0:T(8,128)} %get-tuple-element.102, bf16[2048,1024]{1,0:T(8,128)(2,1)} %get-tuple-element.37.gf, bf16[2048,1024]{1,0:T(8,128)(2,1)S(1)} %add_convert_fusion.1), kind=kOutput, calls=%fused_computation.6 | convolution fusion | flops 8631877632 | bytes 33554432 | tf_op jit(solution)/shard_map/dot_general | solution.py:23
  261.1 9.0 %fusion.53 = f32[2048,1024]{1,0:T(8,128)S(1)} fusion(bf16[2048,2048]{1,0:T(8,128)(2,1)S(1)} %bitcast.120, bf16[2048,1024]{1,0:T(8,128)(2,1)S(1)} %add_convert_fusion.1), kind=kOutput, calls=%fused_computation.115 | convolution fusion | flops 8589934592 | bytes 20971520 | tf_op jit(solution)/shard_map/dot_general | solution.py:23
  273.1 5.0 %convolution_convert_fusion.2 = bf16[128,2048]{1,0:T(8,128)(2,1)S(1)} fusion(bf16[2048,2048]{1,0:T(8,128)(2,1)S(1)} %bitcast.120, bf16[2048,1152]{1,0:T(8,128)(2,1)} %all-gather.4.cloned.1.call-done), kind=kOutput, calls=%fused_computation.38 | convolution fusion | flops 1074003968 | bytes 9437184 | tf_op jit(solution)/shard_map/dot_general | solution.py:23
  280.2 8.3 %convolution_convert_fusion.7 = bf16[128,1024]{1,0:T(8,128)(2,1)S(1)} fusion(bf16[2048,1024]{1,0:T(8,128)(2,1)} %get-tuple-element.88, bf16[2048,2048]{1,0:T(8,128)(2,1)} %fusion.5.dp, bf16[128,512]{1,0:T(8,128)(2,1)} %copy-done.24, bf16[128,512]{1,0:T(8,128)(2,1)} %copy-done.25, bf16[128,512]{1,0:T(8,128)(2,1)} %copy-done.26, ...), kind=kOutput, calls=%fused_computation.52 | convolution fusion | flops 1613365248 | bytes 13369344 | tf_op jit(solution)/shard_map/dot_general | solution.py:23
  291.1 5.4 %convolution_convert_fusion.3.dad = bf16[128,2048]{1,0:T(8,128)(2,1)} fusion(bf16[2048,2048]{1,0:T(8,128)(2,1)} %get-tuple-element.101, bf16[256,2048]{1,0:T(8,128)(2,1)S(1)} %copy-done.15), kind=kOutput, calls=%fused_computation.39 | convolution fusion | flops 1074003968 | bytes 9437184 | tf_op jit(solution)/shard_map/dot_general | solution.py:23
  296.5 8.2 %fusion.21.dbu = bf16[128,2048]{1,0:T(8,128)(2,1)} fusion(bf16[2048,2048]{1,0:T(8,128)(2,1)} %fusion.5.dp, bf16[2048,1024]{1,0:T(8,128)(2,1)} %get-tuple-element.88, bf16[4,128,1024]{2,1,0:T(8,128)(2,1)} %get-tuple-element.31), kind=kOutput, calls=%fused_computation.40 | convolution fusion | flops 1611399168 | bytes 13369344 | tf_op jit(solution)/shard_map/dot_general | solution.py:23
  304.7 5.9 %fusion.17.y = bf16[4,256,1024]{2,1,0:T(8,128)(2,1)} fusion(bf16[4,256,1024]{2,1,0:T(8,128)(2,1)} %collective-permute-done.1, f32[4,2,256,1024]{3,2,1,0:T(8,128)} %bitcast.122, s32[]{:T(128)S(6)} %select_n.85, bf16[4,2,256,1024]{3,2,1,0:T(8,128)(2,1)} %bitcast.116), kind=kLoop, calls=%fused_computation.27 | loop fusion | flops 5242880 | bytes 10485764 | tf_op jit(solution)/shard_map/convert_element_type | solution.py:869
  310.6 105.3 %back.1 = (bf16[2,512,1024]{2,1,0:T(8,128)(2,1)}, bf16[2,512,1024]{2,1,0:T(8,128)(2,1)}, f32[3,128,256]{2,1,0:T(8,128)}, f32[128,1024]{1,0:T(8,128)}, f32[256,12...) custom-call(bf16[3,512,2048]{2,1,0:T(8,128)(2,1)} %get-tuple-element.38.dl, ...), custom_call_target="tpu_custom_call" | custom-call | tf_op jit(solution)/shard_map/back/pallas_call | solution.py:759
  423.0 3.2 copy.59
  (126 shorter events, 39.8 us)
Async XLA Ops:
  7.2 207.9 %all-gather.6.cloned.1.call-start = ((), (), s32[]{:S(2)}) async-start(), calls=%async_computation.1 | async-start | bytes 5898240 | tf_op jit(solution)/shard_map/all_gather | solution.py:824
  12.9 94.1 %copy-start.27 = (s32[2,1,2048]{2,1,0:T(1,128)S(1)}, s32[2,1,2048]{2,1,0:T(1,128)}, u32[]{:S(2)}) copy-start(s32[2,1,2048]{2,1,0:T(1,128)} %param.19) | copy-start | bytes 49156
  12.9 94.1 %copy-start.28 = (s32[2,1,2048]{2,1,0:T(1,128)S(1)}, s32[2,1,2048]{2,1,0:T(1,128)}, u32[]{:S(2)}) copy-start(s32[2,1,2048]{2,1,0:T(1,128)} %param.18) | copy-start | bytes 49156
  106.9 132.7 %all-gather.4.cloned.1.call-start = ((), (), s32[]{:S(2)}) async-start(), calls=%async_computation | async-start | bytes 5898240 | tf_op jit(solution)/shard_map/all_gather | solution.py:825
  107.0 28.6 %collective-permute-start = (s32[2,2,2048]{2,1,0:T(2,128)S(1)}, s32[2,2,2048]{2,1,0:T(2,128)S(1)}, u32[]{:S(2)}, u32[]{:S(2)}) collective-permute-start(s32[2,2,2048]{2,1,0:T(2,128)S(1)} %pad_add_fusion), channel_id=1, source_target_pairs={{0,4},{4,0},{8,12},{12,8},{16,20},{20,16},{24,28},{28,24},{1,5},{5... | collective-permute-start | bytes 98312 | tf_op jit(solution)/shard_map/ppermute | solution.py:801
  107.7 5.0 %copy-start.13 = (bf16[4,128,1024]{2,1,0:T(8,128)(2,1)S(1)}, bf16[4,128,1024]{2,1,0:T(8,128)(2,1)}, u32[]{:S(2)}) copy-start(bf16[4,128,1024]{2,1,0:T(8,128)(2,1)} %get-tuple-element.31) | copy-start | bytes 3145732
  107.7 5.1 %copy-start.14 = (bf16[512,1024]{1,0:T(8,128)(2,1)S(1)}, bf16[512,1024]{1,0:T(8,128)(2,1)}, u32[]{:S(2)}) copy-start(bf16[512,1024]{1,0:T(8,128)(2,1)} %get-tuple-element.34) | copy-start | bytes 3145732
  107.7 5.1 %copy-start.18 = (bf16[512,128]{1,0:T(8,128)(2,1)S(1)}, bf16[512,128]{1,0:T(8,128)(2,1)}, u32[]{:S(2)}) copy-start(bf16[512,128]{1,0:T(8,128)(2,1)} %get-tuple-element.35) | copy-start | bytes 393220
  107.7 5.1 %copy-start.21 = (bf16[2,128,1024]{2,1,0:T(8,128)(2,1)S(1)}, bf16[2,128,1024]{2,1,0:T(8,128)(2,1)}, u32[]{:S(2)}) copy-start(bf16[2,128,1024]{2,1,0:T(8,128)(2,1)} %get-tuple-element.36) | copy-start | bytes 1572868
  120.7 5.6 %copy-start.11 = (bf16[3,1024,512]{2,1,0:T(8,128)(2,1)}, bf16[3,1024,512]{2,1,0:T(8,128)(2,1)S(1)}, u32[]{:S(2)}) copy-start(bf16[3,1024,512]{2,1,0:T(8,128)(2,1)S(1)} %add_convert_fusion.2.mq) | copy-start | bytes 9437188
  199.4 10.0 %slice-start = ((s8[6291456]{0:T(1024)(128)(4,1)}), s8[4194304]{0:T(1024)(128)(4,1)S(1)}, s32[]{:S(2)}) async-start(s8[6291456]{0:T(1024)(128)(4,1)} %bitcast.117), calls=%async_computation.2 | async-start | bytes 8388608
  218.9 6.8 %copy-start.4 = (bf16[2048,1024]{1,0:T(8,128)(2,1)S(1)}, bf16[2048,1024]{1,0:T(8,128)(2,1)}, u32[]{:S(2)}) copy-start(bf16[2048,1024]{1,0:T(8,128)(2,1)} %get-tuple-element.88) | copy-start | bytes 12582916
  225.7 14.0 %copy-start.22 = (bf16[2,128,1024]{2,1,0:T(8,128)(2,1)S(1)}, bf16[2,128,1024]{2,1,0:T(8,128)(2,1)}, u32[]{:S(2)}) copy-start(bf16[2,128,1024]{2,1,0:T(8,128)(2,1)} %get-tuple-element.36) | copy-start | bytes 1572868
  239.7 21.4 %slice-start.2 = ((s8[8388608]{0:T(1024)(128)(4,1)}), s8[4194304]{0:T(1024)(128)(4,1)S(1)}, s32[]{:S(2)}) async-start(s8[8388608]{0:T(1024)(128)(4,1)} %bitcast.119), calls=%async_computation.4 | async-start | bytes 8388608
  243.4 17.6 %slice-start.3 = ((s8[8388608]{0:T(1024)(128)(4,1)}), s8[4194304]{0:T(1024)(128)(4,1)S(1)}, s32[]{:S(2)}) async-start(s8[8388608]{0:T(1024)(128)(4,1)} %bitcast.119), calls=%async_computation.5 | async-start | bytes 8388608
  261.1 9.0 %copy-start.5 = (bf16[512,2048]{1,0:T(8,128)(2,1)S(1)}, bf16[512,2048]{1,0:T(8,128)(2,1)}, u32[]{:S(2)}) copy-start(bf16[512,2048]{1,0:T(8,128)(2,1)} %get-tuple-element.41) | copy-start | bytes 6291460
  272.7 5.5 %copy-start.3 = (f32[2048,1024]{1,0:T(8,128)}, f32[2048,1024]{1,0:T(8,128)S(1)}, u32[]{:S(2)}) copy-start(f32[2048,1024]{1,0:T(8,128)S(1)} %convolution_add_fusion) | copy-start | bytes 25165828
  273.0 5.1 %copy-start.7 = (bf16[2048,1024]{1,0:T(8,128)(2,1)S(1)}, bf16[2048,1024]{1,0:T(8,128)(2,1)}, u32[]{:S(2)}) copy-start(bf16[2048,1024]{1,0:T(8,128)(2,1)} %get-tuple-element.37.gf) | copy-start | bytes 12582916
  273.0 5.1 %copy-start.17 = (bf16[128,2048]{1,0:T(8,128)(2,1)S(1)}, bf16[128,2048]{1,0:T(8,128)(2,1)}, u32[]{:S(2)}) copy-start(bf16[128,2048]{1,0:T(8,128)(2,1)} %convolution_convert_fusion.4) | copy-start | bytes 1572868
  273.0 31.7 %collective-permute-start.1 = (bf16[4,256,1024]{2,1,0:T(8,128)(2,1)S(1)}, bf16[4,256,1024]{2,1,0:T(8,128)(2,1)}, u32[]{:S(2)}, u32[]{:S(2)}) collective-permute-start(bf16[4,256,1024]{2,1,0:T(8,128)(2,1)S(1)} %fusion.23), channel_id=1, source_target_pairs={{0,4},{4,0},{8,12},{12,8},{16,20},{20,16},{24,28},{28,24},{1,5},{5... | collective-permute-start | bytes 6291464 | tf_op jit(solution)/shard_map/ppermute | solution.py:801
  280.2 10.9 %copy-start.15 = (bf16[256,2048]{1,0:T(8,128)(2,1)S(1)}, bf16[256,2048]{1,0:T(8,128)(2,1)}, u32[]{:S(2)}) copy-start(bf16[256,2048]{1,0:T(8,128)(2,1)} %fusion.20) | copy-start | bytes 3145732
  423.0 5.3 %copy-start.16 = (f32[128,1024]{1,0:T(8,128)S(1)}, f32[128,1024]{1,0:T(8,128)}, u32[]{:S(2)}) copy-start(f32[128,1024]{1,0:T(8,128)} %get-tuple-element.119) | copy-start | bytes 1572868
  423.0 6.1 %copy-start.23 = (f32[256,128]{1,0:T(8,128)S(1)}, f32[256,128]{1,0:T(8,128)}, u32[]{:S(2)}) copy-start(f32[256,128]{1,0:T(8,128)} %get-tuple-element.120) | copy-start | bytes 393220
  423.0 6.8 %copy-start.1 = (bf16[1024,1024]{1,0:T(8,128)(2,1)S(1)}, bf16[1024,1024]{1,0:T(8,128)(2,1)}, u32[]{:S(2)}) copy-start(bf16[1024,1024]{1,0:T(8,128)(2,1)} %param.24) | copy-start | bytes 6291460
  (16 other events, 49.9 us)
Sparse Core Ops, SparseCore 0:
  107.0 57.0 all-gather.5
  166.0 56.9 all-gather.3

commit v8 on v7

--- a/solution.py
+++ b/solution.py
@@ -420,9 +420,9 @@
     return pl.ds(pl.multiple_of(i * n, n), n)
 
 
-def front_kernel(x, g, wq, wo, ain, bq, ao, bo,
-                 xf, gf, wqf, wof, ainf, bqf, aof, bof,
-                 row_sems, sems, local, xs, gs, wqs, wos, ains, bqs, aos, bos):
+def front_kernel(x, g, wq, wo, ain, bq, ao, bo, gain, bias,
+                 xf, gf, wqf, wof, ainf, bqf, aof, bof, n1, n2,
+                 row_sems, sems, local, xs, gs, wqs, wos, ains, bqs, aos, bos, norm_sems, xb, n1s, n2s):
     z, c, t = place()
     meet(z, c, t, (1,))
     at = dict(z=z, c=c, t=t)
@@ -440,30 +440,62 @@
                    lambda v, h: v.at[aligned(h, 64)], None, **at)
     b_out = Blocks(bo, lambda i: bof.at[:, aligned(i, 32)], sems.at[5], bos, local.at[7],
                    lambda v, h: v.at[pl.ds(h, 1)], None, **at)
+    blocks = (into, second, qkv, b_out, a_out, out)
     x_rows.start()
-    for v in (into, second, qkv, b_out, a_out, out):
+    for v in blocks:
         v.start()
     g_rows.start()
     x_rows.relay()
-    for v in (into, second, qkv, b_out, a_out, out):
+    for v in blocks:
         v.store()
-    for v in (into, second, qkv, b_out, a_out, out):
+    for v in blocks:
         v.relay()
-    for v in (into, second, qkv, b_out, a_out, out):
+    x_rows.finish()
+
+    def load(j):
+        return pltpu.make_async_copy(xf.at[aligned(j, 256)], xb.at[j % 2], norm_sems.at[j % 2])
+
+    load(0).start()
+
+    def norms(j, carry):
+        load(j).wait()
+
+        @pl.when(j < 7)
+        def _():
+            load(j + 1).start()
+
+        def some(r, carry):
+            v = xb[j % 2, aligned(r, 32), :].astype(F32)
+            v = v - jnp.mean(v, axis=1, keepdims=True)
+            v = v * lax.rsqrt(jnp.mean(v * v, axis=1, keepdims=True) + EPSILON)
+            at = aligned(j * 8 + r, 32)
+            n1s[at, :] = (v * gain[0:1, :] + bias[0:1, :]).astype(BF)
+            n2s[at, :] = (v * gain[1:2, :] + bias[1:2, :]).astype(BF)
+            return carry
+
+        return lax.fori_loop(0, 8, some, carry)
+
+    lax.fori_loop(0, 8, norms, 0)
+    saves = (pltpu.make_async_copy(n1s, n1, norm_sems.at[2]), pltpu.make_async_copy(n2s, n2, norm_sems.at[3]))
+    for v in saves:
+        v.start()
+    for v in blocks:
         v.pass_on()
     g_rows.relay()
-    for v in (x_rows, into, second, qkv, b_out, a_out, out, g_rows):
+    for v in blocks + (g_rows,):
         v.finish()
-
-
-def front(x, g, wq, wo, ain, bq, ao, bo):
+    for v in saves:
+        v.wait()
+
+
+def front(x, g, wq, wo, ain, bq, ao, bo, gain, bias):
     shapes = [(2048, 1024), (2048, 1024), (3, 1024, 512), (512, 1024), (4, 128, 1024), (3, 128, 512), (512, 128),
-              (2, 128, 1024)]
-    anywhere = pl.BlockSpec(memory_space=pl.ANY)
+              (2, 128, 1024), (2048, 1024), (2048, 1024)]
+    anywhere, vmem = pl.BlockSpec(memory_space=pl.ANY), pl.BlockSpec(memory_space=pltpu.VMEM)
     return pl.pallas_call(
         front_kernel,
-        in_specs=[anywhere] * 8,
-        out_specs=[anywhere] * 8,
+        in_specs=[anywhere] * 8 + [vmem] * 2,
+        out_specs=[anywhere] * 10,
         out_shape=[jax.ShapeDtypeStruct(s, BF) for s in shapes],
         scratch_shapes=[
             pltpu.SemaphoreType.DMA((2, 16)),
@@ -477,14 +509,18 @@
             pltpu.VMEM((3, 128, 128), BF),
             pltpu.VMEM((128, 128), BF),
             pltpu.VMEM((2, 32, 1024), BF),
+            pltpu.SemaphoreType.DMA((4,)),
+            pltpu.VMEM((2, 256, 1024), BF),
+            pltpu.VMEM((2048, 1024), BF),
+            pltpu.VMEM((2048, 1024), BF),
         ],
         compiler_params=pltpu.CompilerParams(collective_id=0, has_side_effects=True),
         name="front",
-    )(x, g, wq, wo, ain, bq, ao, bo)
+    )(x, g, wq, wo, ain, bq, ao, bo, gain, bias)
 
 
 def back_kernel(dl, dp, mq, mu, xf, gf, gain, y, dbq, dbu, dao, dad, dsh,
-                out, yout, obq, obu, oao, oad, osh, ono,
+                out, yout, obq, obu, oao, oad, oai, obo, ono,
                 row_sems, share_sems, cross_sems, z_sems, last_sems, norm_sems, local, weight_sems,
                 sh_in, sh, rbq, rbu, rao, rad, rsh, pbq, pbu, pao, pad, psh, qbq, qbu, qao, qad, qsh,
                 no_plane, no_z, no_own, no_mid, wq, wu, dlb, dpb, xb, gb, dlt, one, two, std, inv, sends, gets, rows):
@@ -564,9 +600,9 @@
         return remote(half(dst, i, j), half(dst, i, j), z_sems.at[0, step, i], z_sems.at[1, step, i], (d, t ^ 1))
 
     result = (obq.at[:, :, aligned(c, 128)], obu.at[:, aligned(c, 512)], oao.at[aligned(c, 128)],
-              oad.at[:, aligned(c, 512)], osh.at[:, :, aligned(c, 512)])
+              oad.at[:, aligned(c, 512)], oai.at[:, :, aligned(c, 512)], obo.at[:, :, aligned(c, 512)])
     theirs = (obq.at[:, :, aligned(c ^ 1, 128)], obu.at[:, aligned(c ^ 1, 512)], oao.at[aligned(c ^ 1, 128)],
-              oad.at[:, aligned(c ^ 1, 512)], osh.at[:, :, aligned(c ^ 1, 512)])
+              oad.at[:, aligned(c ^ 1, 512)], oai.at[:, :, aligned(c ^ 1, 512)], obo.at[:, :, aligned(c ^ 1, 512)])
 
     def last(i):
         return remote(result[i], result[i], last_sems.at[0, i], last_sems.at[1, i], sibling)
@@ -708,7 +744,12 @@
     no_plane[2 * t + c] = own
     for i in range(5):
         arrived(2, i).wait_recv()
-        result[i][...] = sums[i][2].astype(F32)
+        if i < 4:
+            result[i][...] = sums[i][2].astype(F32)
+        else:
+            result[4][...] = sums[4][2, :4].astype(F32)
+            result[5][...] = sums[4][2, 4:].astype(F32)
+            last(5).start()
         last(i).start()
     for n in range(7):
         norm_from(n).wait_recv()
@@ -719,9 +760,10 @@
     for k in (1, 2, 3):
         norm_z(k).start()
     no_z[z] = own
-    for i in range(5):
+    for i in range(6):
         remote(theirs[i], theirs[i], last_sems.at[0, i], last_sems.at[1, i], sibling).wait_recv()
         last(i).wait_send()
+    for i in range(5):
         for step in (0, 1, 2):
             along(step, i).wait_send()
         for k in (1, 2, 3):
@@ -755,18 +797,18 @@
     anywhere = pl.BlockSpec(memory_space=pl.ANY)
     part = [(3, 128, 128), (128, 512), (128, 128), (128, 512), (6, 32, 512)]
     outs = [((2, 512, 1024), BF), ((2, 512, 1024), BF), ((3, 128, 256), F32), ((128, 1024), F32), ((256, 128), F32), ((128, 1024), F32),
-            ((6, 32, 1024), F32), ((4, 1024), F32)]
+            ((4, 32, 1024), F32), ((2, 32, 1024), F32), ((4, 1024), F32)]
     return pl.pallas_call(
         back_kernel,
         in_specs=[anywhere] * 6 + [vmem] * 7,
-        out_specs=[anywhere] * 2 + [vmem] * 6,
+        out_specs=[anywhere] * 2 + [vmem] * 7,
         out_shape=[jax.ShapeDtypeStruct(s, d) for s, d in outs],
         scratch_shapes=[
             pltpu.SemaphoreType.DMA((24,)),
             pltpu.SemaphoreType.DMA((2,)),
             pltpu.SemaphoreType.DMA((2, 3, 5)),
             pltpu.SemaphoreType.DMA((2, 3, 5)),
-            pltpu.SemaphoreType.DMA((2, 5)),
+            pltpu.SemaphoreType.DMA((2, 6)),
             pltpu.SemaphoreType.DMA((2, 10)),
             pltpu.SemaphoreType.DMA((4, 2)),
             pltpu.SemaphoreType.DMA((2,)),
@@ -816,8 +858,8 @@
     pair = jnp.where(t % 2 == c, tables, swap(tables))
     seg, kept = jnp.where(t // 2 == 0, pair[0], pair[1])
 
-    x_full, g_full, qkv, out, a_full, b_qkv_all, a_out_all, b_full = front(
-        x[:, 0], gy[:, 0], w_qkv, w_out, jnp.swapaxes(a_in, 1, 2), b_qkv, a_out, b_out)
+    x_full, g_full, qkv, out, a_full, b_qkv_all, a_out_all, b_full, n1, n2 = front(
+        x[:, 0], gy[:, 0], w_qkv, w_out, jnp.swapaxes(a_in, 1, 2), b_qkv, a_out, b_out, gain, bias)
     up, down = lax.optimization_barrier((
         jnp.concatenate([pick(w_up, 1, c, 512), pick(b_up, 1, c, 512)], axis=0),
         jnp.concatenate([pick(w_down, 0, c, 512), pick(a_down, 0, c, 512)], axis=1), x_full))[:2]
@@ -835,9 +877,6 @@
     a_three = a_full[:3].reshape(3 * RANK, 1024)
     b_both = b_full.reshape(2 * RANK, 1024)
 
-    standard, _ = normalized(x_full.astype(F32))
-    n1 = (standard * gain[0] + bias[0]).astype(BF)
-    n2 = (standard * gain[1] + bias[1]).astype(BF)
     lin = jnp.einsum("nkc,sk->ncs", m_qkv, n1, preferred_element_type=F32)
     low3 = dot(a_three, n1, 1, 1).astype(BF).reshape(3, RANK, 2048)
     low1 = dot(a_full[3], n2, 1, 1).astype(BF)
@@ -865,10 +904,10 @@
     back1 = (SCALE * dot(b_up_all, d_pre, 1, 1)).astype(BF)
     shared = jnp.concatenate([dot(back3.reshape(3 * RANK, 2048), n1, 1, 0).astype(BF), dot(back1, n2, 1, 0).astype(BF),
                               (SCALE * dot(lo, g_full, 1, 0)).astype(BF)], axis=0).reshape(6, RANK, 1024)
-    grad, y, r_b_qkv, r_b_up, r_a_out, r_a_down, rest, norms = back(
+    grad, y, r_b_qkv, r_b_up, r_a_out, r_a_down, r_a_in, r_b_out, norms = back(
         d_lin, d_pre, m_qkv, m_up, x_full, g_full, gain, y.astype(BF), d_b_qkv, d_b_up, d_a_out, d_a_down, shared)
-    r_a_in = jnp.swapaxes(rest[:4], 1, 2)
-    return (y[:, None], grad[:, None], norms[:2], norms[2:], r_a_in, r_b_qkv, r_b_up, r_a_out, jnp.transpose(r_a_down), rest[4:])
+    r_a_in = jnp.swapaxes(r_a_in, 1, 2)
+    return (y[:, None], grad[:, None], norms[:2], norms[2:], r_a_in, r_b_qkv, r_b_up, r_a_out, jnp.transpose(r_a_down), r_b_out)
 
 
 def solution(mesh):

time: 441 us -> 442 us (level)
  other arithmetic: 21.6 us -> 13.4 us
  Pallas kernels: 259 us -> 264 us
    pallas_call x1, Pallas kernels: 59.7 us -> 67.1 us  [attention(): pl.pallas_call(functools.partial(attention_kernel, heads), grid_spec=pltp...]
    reduce_sum x2 -> x0, other arithmetic: 4.51 us -> none  [the longest x1 2.95 us: normalized(): average = jnp.mean(values, axis=-1, keepdims=True)]
  transfers between devices with their start and end apart: 4 -> 4, of which waited for: 0 -> 0; matrix products, arithmetic and copies ran while one was open for 23% -> 22% of each run, Pallas kernels for 14% -> 15%
where the time goes in v8:
time: 442 us; the launch traced here: 437 us
  Pallas kernels  264 us (60%)
  matrix products  119 us (27%)
  local copies, waits for them, and re-layouts  24.9 us (6%)
  between operations  15 us (3%)
  other arithmetic  13.4 us (3%)
    pallas_call x1, Pallas kernels, back(): pl.pallas_call(back_kernel, in_specs=[anywhere] * 6 + [vmem] * 7, out_spe...  102 us
    dot_general x18, matrix products, dot(): lax.dot_general(a, b, (((ca,), (cb,)), ((), ())), preferred_element_type=...  102 us
    pallas_call x1, Pallas kernels, front(): pl.pallas_call(front_kernel, in_specs=[anywhere] * 8 + [vmem] * 2, out_sp...  94.7 us
    pallas_call x1, Pallas kernels, attention(): pl.pallas_call(functools.partial(attention_kernel, heads), grid_spec=pltp...  67.1 us
    unnamed x78, local copies, waits for them, and re-layouts  13.5 us
    dot_general x1, matrix products, by_groups(): lin = jnp.einsum('nkc,sk->ncs', m_qkv, n1, preferred_element_type=F32)  9.73 us
  transfers between devices with their start and end apart: 4, of which 0 were waited for; matrix products, arithmetic and copies ran while one was open for 22% of the time, Pallas kernels for 15%

profile of v8, /device:TPU:0, one launch (start us, length us, event | category | flops | bytes accessed | tf_op | source)
XLA Modules:
  0.0 437.2 jit_solution(4951341237016425501)
XLA Ops:
  13.0 94.7 %front.1 = (bf16[2048,1024]{1,0:T(8,128)(2,1)}, bf16[2048,1024]{1,0:T(8,128)(2,1)}, bf16[3,1024,512]{2,1,0:T(8,128)(2,1)}, bf16[512,1024]{1,0:T(8,128)(2,1)}, bf...) custom-call(bf16[2,512,1024]{2,1,0:T(8,128)(2,1)} %bitcast.122, ...), custom_call_target="tpu_custom_call" | custom-call | tf_op jit(solution)/shard_map/front/pallas_call | solution.py:495
  111.3 4.5 %fusion.11 = bf16[256,2048]{1,0:T(8,128)(2,1)} fusion(bf16[256,1024]{1,0:T(8,128)(2,1)S(1)} %bitcast.131, bf16[2048,1024]{1,0:T(8,128)(2,1)} %get-tuple-element.40.gf), kind=kOutput, calls=%fused_computation.24 | convolution fusion | flops 1074790400 | bytes 5767168 | tf_op jit(solution)/shard_map/dot_general | solution.py:23
  115.8 3.7 convolution_convert_fusion.g_ref
  123.7 9.7 %fusion.9.lin_ref = f32[3,512,2048]{2,1,0:T(8,128)} fusion(bf16[3,1024,512]{2,1,0:T(8,128)(2,1)S(1)} %add_convert_fusion.2.mq, bf16[2048,1024]{1,0:T(8,128)(2,1)S(1)} %copy-done.28), kind=kOutput, calls=%fused_computation.17 | convolution fusion | flops 6442450944 | bytes 19922944 | tf_op jit(solution)/shard_map/nkc,sk->ncs/dot_general | solution.py:880
  137.5 67.1 %attention.1 = (bf16[512,2048]{1,0:T(8,128)(2,1)}, bf16[3,512,2048]{2,1,0:T(8,128)(2,1)}) custom-call(s32[8]{0:T(128)} %and_select_fusion.lo_ref, f32[3,512,2048]{2,1,0:T(8,128)} %fusion.9.lin_ref, bf16[512,2048]{1,0:T(8,128)(2,1)} %convolution_convert_fusion.g_ref, f32[8,2048]{1,0:T(8,128)} %get-tuple-element.100.cos_ref, ...), custom_call_target="tpu_custom_call" | custom-call | flops 8053063680 | bytes 27262976 | tf_op jit(solution)/shard_map/attention/pallas_call | solution.py:145
  204.6 3.0 convolution_convert_fusion.4
  207.6 3.0 convolution_convert_fusion.8.dao
  210.6 3.9 multiply_convert_fusion.1
  214.6 3.0 fusion.16.dbq
  217.6 2.7 convolution_convert_fusion.6
  221.4 2.6 slice_bitcast_fusion.3
  224.1 5.0 %add_convert_fusion.mu = bf16[1024,2048]{1,0:T(8,128)(2,1)S(1)} fusion(bf16[1024,512]{1,0:T(8,128)(2,1)S(1)} %get-tuple-element.91, bf16[1024,512]{1,0:T(8,128)(2,1)S(1)} %get-tuple-element.92, bf16[1024,512]{1,0:T(8,128)(2,1)S(1)} %get-tuple-element.93, bf16[1024,512]{1,0:T(8,128)(2,1)S(1)} %get-tuple-element.90, ...), kind=kOutput, calls=%fused_computation.9 | convolution fusion | flops 562036736 | bytes 9175040 | tf_op jit(solution)/shard_map/dot_general | solution.py:23
  231.0 14.0 %multiply_convert_fusion = (bf16[2048,2048]{1,0:T(8,128)(2,1)}, f32[2048,2048]{1,0:T(8,128)}) fusion(bf16[2048,1024]{1,0:T(8,128)(2,1)S(1)} %copy-done.6, bf16[1024,2048]{1,0:T(8,128)(2,1)S(1)} %add_convert_fusion.mu), kind=kOutput, calls=%fused_computation.7 | convolution fusion | flops 8610906112 | bytes 33554432 | tf_op jit(solution)/shard_map/dot_general | solution.py:23
  245.1 3.8 add_convert_fusion.1
  248.9 17.6 %fusion.5.dp = bf16[2048,2048]{1,0:T(8,128)(2,1)} fusion(f32[2048,2048]{1,0:T(8,128)} %get-tuple-element.102, bf16[2048,1024]{1,0:T(8,128)(2,1)} %get-tuple-element.40.gf, bf16[2048,1024]{1,0:T(8,128)(2,1)S(1)} %add_convert_fusion.1), kind=kOutput, calls=%fused_computation.6 | convolution fusion | flops 8631877632 | bytes 33554432 | tf_op jit(solution)/shard_map/dot_general | solution.py:23
  266.5 9.0 %fusion.42 = f32[2048,1024]{1,0:T(8,128)S(1)} fusion(bf16[2048,2048]{1,0:T(8,128)(2,1)S(1)} %bitcast.114, bf16[2048,1024]{1,0:T(8,128)(2,1)S(1)} %add_convert_fusion.1), kind=kOutput, calls=%fused_computation.99 | convolution fusion | flops 8589934592 | bytes 20971520 | tf_op jit(solution)/shard_map/dot_general | solution.py:23
  278.6 5.3 %convolution_convert_fusion.2 = bf16[128,2048]{1,0:T(8,128)(2,1)S(1)} fusion(bf16[2048,2048]{1,0:T(8,128)(2,1)S(1)} %bitcast.114, bf16[2048,1152]{1,0:T(8,128)(2,1)} %all-gather.4.cloned.1.call-done), kind=kOutput, calls=%fused_computation.27 | convolution fusion | flops 1074003968 | bytes 9437184 | tf_op jit(solution)/shard_map/dot_general | solution.py:23
  286.1 8.3 %convolution_convert_fusion.7 = bf16[128,1024]{1,0:T(8,128)(2,1)S(1)} fusion(bf16[2048,1024]{1,0:T(8,128)(2,1)} %get-tuple-element.44, bf16[2048,2048]{1,0:T(8,128)(2,1)} %fusion.5.dp, bf16[128,512]{1,0:T(8,128)(2,1)} %copy-done.23, bf16[128,512]{1,0:T(8,128)(2,1)} %copy-done.24, bf16[128,512]{1,0:T(8,128)(2,1)} %copy-done.25, ...), kind=kOutput, calls=%fused_computation.41 | convolution fusion | flops 1613365248 | bytes 13369344 | tf_op jit(solution)/shard_map/dot_general | solution.py:23
  294.4 2.6 pad_maximum_fusion
  296.9 5.4 %convolution_convert_fusion.3.dad = bf16[128,2048]{1,0:T(8,128)(2,1)} fusion(bf16[2048,2048]{1,0:T(8,128)(2,1)} %get-tuple-element.101, bf16[256,2048]{1,0:T(8,128)(2,1)S(1)} %copy-done.12), kind=kOutput, calls=%fused_computation.28 | convolution fusion | flops 1074003968 | bytes 9437184 | tf_op jit(solution)/shard_map/dot_general | solution.py:23
  302.3 8.2 %fusion.12.dbu = bf16[128,2048]{1,0:T(8,128)(2,1)} fusion(bf16[2048,2048]{1,0:T(8,128)(2,1)} %fusion.5.dp, bf16[2048,1024]{1,0:T(8,128)(2,1)} %get-tuple-element.44, bf16[4,128,1024]{2,1,0:T(8,128)(2,1)} %get-tuple-element.34), kind=kOutput, calls=%fused_computation.29 | convolution fusion | flops 1611399168 | bytes 13369344 | tf_op jit(solution)/shard_map/dot_general | solution.py:23
  310.5 5.9 %fusion.8.y = bf16[4,256,1024]{2,1,0:T(8,128)(2,1)} fusion(bf16[4,256,1024]{2,1,0:T(8,128)(2,1)} %collective-permute-done.1, f32[4,2,256,1024]{3,2,1,0:T(8,128)} %bitcast.116, s32[]{:T(128)S(6)} %select_n.85, bf16[4,2,256,1024]{3,2,1,0:T(8,128)(2,1)} %bitcast.117), kind=kLoop, calls=%fused_computation.16 | loop fusion | flops 5242880 | bytes 10485764 | tf_op jit(solution)/shard_map/convert_element_type | solution.py:908
  316.5 101.7 %back.1 = (bf16[2,512,1024]{2,1,0:T(8,128)(2,1)}, bf16[2,512,1024]{2,1,0:T(8,128)(2,1)}, f32[3,128,256]{2,1,0:T(8,128)}, f32[128,1024]{1,0:T(8,128)}, f32[256,12...) custom-call(bf16[3,512,2048]{2,1,0:T(8,128)(2,1)} %get-tuple-element, ...), custom_call_target="tpu_custom_call" | custom-call | tf_op jit(solution)/shard_map/back/pallas_call | solution.py:801
  421.7 3.2 copy.61
  (117 shorter events, 34.1 us)
Async XLA Ops:
  7.2 213.1 %all-gather.6.cloned.1.call-start = ((), (), s32[]{:S(2)}) async-start(), calls=%async_computation.1 | async-start | bytes 5898240 | tf_op jit(solution)/shard_map/all_gather | solution.py:866
  13.0 94.8 %copy-start.26 = (s32[2,1,2048]{2,1,0:T(1,128)S(1)}, s32[2,1,2048]{2,1,0:T(1,128)}, u32[]{:S(2)}) copy-start(s32[2,1,2048]{2,1,0:T(1,128)} %param.19) | copy-start | bytes 49156
  13.0 94.9 %copy-start.27 = (s32[2,1,2048]{2,1,0:T(1,128)S(1)}, s32[2,1,2048]{2,1,0:T(1,128)}, u32[]{:S(2)}) copy-start(s32[2,1,2048]{2,1,0:T(1,128)} %param.18) | copy-start | bytes 49156
  107.8 137.3 %all-gather.4.cloned.1.call-start = ((), (), s32[]{:S(2)}) async-start(), calls=%async_computation | async-start | bytes 5898240 | tf_op jit(solution)/shard_map/all_gather | solution.py:867
  107.9 25.5 %collective-permute-start = (s32[2,2,2048]{2,1,0:T(2,128)S(1)}, s32[2,2,2048]{2,1,0:T(2,128)S(1)}, u32[]{:S(2)}, u32[]{:S(2)}) collective-permute-start(s32[2,2,2048]{2,1,0:T(2,128)S(1)} %pad_add_fusion), channel_id=1, source_target_pairs={{0,4},{4,0},{8,12},{12,8},{16,20},{20,16},{24,28},{28,24},{1,5},{5... | collective-permute-start | bytes 98312 | tf_op jit(solution)/shard_map/ppermute | solution.py:843
  109.7 6.1 %copy-start.4 = (bf16[2048,1024]{1,0:T(8,128)(2,1)S(1)}, bf16[2048,1024]{1,0:T(8,128)(2,1)}, u32[]{:S(2)}) copy-start(bf16[2048,1024]{1,0:T(8,128)(2,1)} %get-tuple-element.40.gf) | copy-start | bytes 12582916
  137.4 67.1 %copy-start.16 = (bf16[512,128]{1,0:T(8,128)(2,1)S(1)}, bf16[512,128]{1,0:T(8,128)(2,1)}, u32[]{:S(2)}) copy-start(bf16[512,128]{1,0:T(8,128)(2,1)} %get-tuple-element.38) | copy-start | bytes 393220
  204.6 10.0 %slice-start = ((s8[6291456]{0:T(1024)(128)(4,1)}), s8[4194304]{0:T(1024)(128)(4,1)S(1)}, s32[]{:S(2)}) async-start(s8[6291456]{0:T(1024)(128)(4,1)} %bitcast.111), calls=%async_computation.2 | async-start | bytes 8388608
  210.6 3.9 slice-start.1
  224.0 7.0 %copy-start.6 = (bf16[2048,1024]{1,0:T(8,128)(2,1)S(1)}, bf16[2048,1024]{1,0:T(8,128)(2,1)}, u32[]{:S(2)}) copy-start(bf16[2048,1024]{1,0:T(8,128)(2,1)} %get-tuple-element.44) | copy-start | bytes 12582916
  231.0 14.1 %copy-start.21 = (bf16[2,128,1024]{2,1,0:T(8,128)(2,1)S(1)}, bf16[2,128,1024]{2,1,0:T(8,128)(2,1)}, u32[]{:S(2)}) copy-start(bf16[2,128,1024]{2,1,0:T(8,128)(2,1)} %get-tuple-element.39) | copy-start | bytes 1572868
  245.1 21.4 %slice-start.2 = ((s8[8388608]{0:T(1024)(128)(4,1)}), s8[4194304]{0:T(1024)(128)(4,1)S(1)}, s32[]{:S(2)}) async-start(s8[8388608]{0:T(1024)(128)(4,1)} %bitcast.113), calls=%async_computation.4 | async-start | bytes 8388608
  248.9 17.7 %slice-start.3 = ((s8[8388608]{0:T(1024)(128)(4,1)}), s8[4194304]{0:T(1024)(128)(4,1)S(1)}, s32[]{:S(2)}) async-start(s8[8388608]{0:T(1024)(128)(4,1)} %bitcast.113), calls=%async_computation.5 | async-start | bytes 8388608
  266.5 9.0 %copy-start.3 = (bf16[512,2048]{1,0:T(8,128)(2,1)S(1)}, bf16[512,2048]{1,0:T(8,128)(2,1)}, u32[]{:S(2)}) copy-start(bf16[512,2048]{1,0:T(8,128)(2,1)} %get-tuple-element.46) | copy-start | bytes 6291460
  278.1 5.8 %copy-start.2 = (f32[2048,1024]{1,0:T(8,128)}, f32[2048,1024]{1,0:T(8,128)S(1)}, u32[]{:S(2)}) copy-start(f32[2048,1024]{1,0:T(8,128)S(1)} %convolution_add_fusion) | copy-start | bytes 25165828
  278.5 5.5 %copy-start.5 = (bf16[2048,1024]{1,0:T(8,128)(2,1)S(1)}, bf16[2048,1024]{1,0:T(8,128)(2,1)}, u32[]{:S(2)}) copy-start(bf16[2048,1024]{1,0:T(8,128)(2,1)} %get-tuple-element.40.gf) | copy-start | bytes 12582916
  278.5 5.5 %copy-start.15 = (bf16[128,2048]{1,0:T(8,128)(2,1)S(1)}, bf16[128,2048]{1,0:T(8,128)(2,1)}, u32[]{:S(2)}) copy-start(bf16[128,2048]{1,0:T(8,128)(2,1)} %convolution_convert_fusion.4) | copy-start | bytes 1572868
  278.5 32.0 %collective-permute-start.1 = (bf16[4,256,1024]{2,1,0:T(8,128)(2,1)S(1)}, bf16[4,256,1024]{2,1,0:T(8,128)(2,1)}, u32[]{:S(2)}, u32[]{:S(2)}) collective-permute-start(bf16[4,256,1024]{2,1,0:T(8,128)(2,1)S(1)} %fusion.14), channel_id=1, source_target_pairs={{0,4},{4,0},{8,12},{12,8},{16,20},{20,16},{24,28},{28,24},{1,5},{5... | collective-permute-start | bytes 6291464 | tf_op jit(solution)/shard_map/ppermute | solution.py:843
  286.1 10.9 %copy-start.12 = (bf16[256,2048]{1,0:T(8,128)(2,1)S(1)}, bf16[256,2048]{1,0:T(8,128)(2,1)}, u32[]{:S(2)}) copy-start(bf16[256,2048]{1,0:T(8,128)(2,1)} %fusion.11) | copy-start | bytes 3145732
  421.6 4.6 %copy-start.14 = (f32[4,32,1024]{2,1,0:T(8,128)S(1)}, f32[4,32,1024]{2,1,0:T(8,128)}, u32[]{:S(2)}) copy-start(f32[4,32,1024]{2,1,0:T(8,128)} %get-tuple-element.50) | copy-start | bytes 1572868
  421.6 5.4 %copy-start.18 = (f32[3,128,256]{2,1,0:T(8,128)S(1)}, f32[3,128,256]{2,1,0:T(8,128)}, u32[]{:S(2)}) copy-start(f32[3,128,256]{2,1,0:T(8,128)} %get-tuple-element.118) | copy-start | bytes 1179652
  421.6 6.1 %copy-start.13 = (f32[128,1024]{1,0:T(8,128)S(1)}, f32[128,1024]{1,0:T(8,128)}, u32[]{:S(2)}) copy-start(f32[128,1024]{1,0:T(8,128)} %get-tuple-element.119) | copy-start | bytes 1572868
  421.6 8.3 %copy-start.1 = (bf16[1024,1024]{1,0:T(8,128)(2,1)S(1)}, bf16[1024,1024]{1,0:T(8,128)(2,1)}, u32[]{:S(2)}) copy-start(bf16[1024,1024]{1,0:T(8,128)(2,1)} %param.24) | copy-start | bytes 6291460
  424.9 4.3 copy-start.19
  (15 other events, 43.8 us)
Sparse Core Ops, SparseCore 0:
  107.9 56.9 all-gather.5
  166.8 56.9 all-gather.3
